TPU v7x, 32 devices: a whole 2x2x4 slice. The times are simulated.
32 devices in a mesh: dp: 2 (over y), seq: 4 (over z), chan: 4 (over x, core).
Axes of the slice: x: 2, y: 2, z: 4, core: 2. Of those that a mesh axis runs over, the one named last changes fastest.
Arguments:
- layer_input: bfloat16 [2, 512, 2560], P('dp', ('seq', 'chan')), may hold values from -6 to 6
- inner_weight: bfloat16 [2560, 2560], P(None, 'chan'), may hold values from -0.125 to 0.125
- mixer_weight: bfloat16 [2560, 256], replicated, may hold values from -0.01171875 to 0.01171875
- step_weight: bfloat16 [2560, 40], P(None, 'chan'), may hold values from -0.125 to 0.125
- conv_inner: float32 [4, 2560], P(None, 'chan'), may hold values from -3 to 3
- conv_mixer: float32 [4, 256], replicated, may hold values from -3 to 3
- step_bias: float32 [40], P('chan'), may hold values from -2 to 1
- decay_log: float32 [40], P('chan'), as said below
- skip_gain: float32 [40], P('chan'), may hold values from 0.5 to 1.5
- output_grad: bfloat16 [2, 512, 2560], P('dp', 'seq', 'chan'), may hold values from -6 to 6
Outputs:
- input_grad: bfloat16 [2, 512, 2560], P('dp', ('seq', 'chan'))
- inner_weight_grad: float32 [2560, 2560], P(('dp', 'seq'), 'chan')
- mixer_weight_grad: float32 [2560, 256], P(('dp', 'seq', 'chan'))
- step_weight_grad: float32 [2560, 40], P(('dp', 'seq'), 'chan')
Inputs may be any that keep to these rules, and one draw needn't show every extreme that they name: exp(decay_log) is at least 0.2 / 512.
All inputs are finite; a program needn't handle non-finite values.
Results may differ from a plain program's by a relative error of at most 0.014.
Values may be sent and summed in bfloat16 or wider, within the bound.
No kernel may reach another device: no remote copies, remote signals or barrier semaphores. Data moves between devices by JAX's collectives and lax.ppermute only.
A program may use at most 128 MiB of HBM per device.

v0:
```python
import math

import jax
import jax.numpy as jnp
from jax import lax
from jax.sharding import PartitionSpec as P

HDIM = 64


block_tokens = 256


def from_behind(value, axis, steps):
    count = lax.axis_size(axis)
    first, last = (max(0, -steps), min(count, count - steps))
    return lax.ppermute(value, axis, [(source, source + steps) for source in range(first, last)])


def prefix(value, axis, join, neutral):
    place = lax.axis_index(axis)
    gathered = jax.tree.map(
        lambda a, kind: lax.all_gather(a.astype(kind), axis), value, (jnp.bfloat16, jnp.bfloat16)
    )
    state = jax.tree.map(lambda a, e: jnp.zeros_like(a) + jnp.asarray(e, a.dtype), value, neutral)

    def one(hop, state):
        return join(
            state,
            jax.tree.map(
                lambda a, own: lax.dynamic_index_in_dim(a, hop, 0, False).astype(own.dtype),
                gathered,
                value,
            ),
        )

    return lax.fori_loop(0, place, one, state)


def prefix_2(value, axis, combine, identity):
    size, index = (lax.axis_size(axis), lax.axis_index(axis))
    everything = jax.tree.map(lambda part: lax.all_gather(part, axis), value)
    start = jax.tree.map(
        lambda part, zero: jnp.broadcast_to(jnp.asarray(zero, part.dtype), part.shape),
        value,
        identity,
    )

    def hop(k, before):
        at = size - 1 - k
        reached = at > index
        new = combine(before, jax.tree.map(lambda part: part[at], everything))
        return jax.tree.map(lambda a, b: jnp.where(reached, a, b), new, before)

    return lax.fori_loop(0, size, hop, start)


def conv_silu(inputs, history, kernel):
    length = inputs.shape[0]
    padded = jnp.concatenate([history, inputs], axis=0)
    summed = kernel[0][None, :] * padded[0:length]
    for offset in range(1, kernel.shape[0]):
        summed = summed + kernel[offset][None, :] * padded[offset : offset + length]
    return jax.nn.silu(summed)


def activations(
    inner_proj,
    mixer_proj,
    step_raw,
    inner_hist,
    mixer_hist,
    conv_inner,
    conv_mixer,
    step_bias,
    decay_log,
):
    length = inner_proj.shape[0]
    head_count = step_bias.shape[0]
    state_width = mixer_proj.shape[1] // 2
    inner_act = conv_silu(inner_proj, inner_hist, conv_inner).reshape(length, head_count, -1)
    mixer_act = conv_silu(mixer_proj, mixer_hist, conv_mixer)
    step_size = jax.nn.softplus(step_raw + step_bias[None, :])
    log_decay = -step_size * jnp.exp(decay_log)[None, :]
    return (inner_act, mixer_act[:, :state_width], mixer_act[:, state_width:], step_size, log_decay)


def spanned_scan(inner_act, input_mix, output_mix, step_size, log_decay, skip_gain, initial):
    length, head_count, head_dim = inner_act.shape
    block_len = min(block_tokens, length)
    blocks = length // block_len
    highest = lax.Precision.HIGHEST

    def to_blocks(values):
        return values.reshape((blocks, block_len) + values.shape[1:])

    def advance(carry_state, pieces):
        part_inner, part_input, part_output, part_step, part_decay = pieces
        cumulative = jnp.cumsum(part_decay, axis=0)
        scores = jnp.dot(part_output, part_input.T, precision=highest)
        causal = (jnp.arange(block_len)[:, None] >= jnp.arange(block_len)[None, :])[:, :, None]
        spread = cumulative[:, None, :] - cumulative[None, :, :]
        weights = jnp.where(causal, jnp.exp(jnp.where(causal, spread, 0.0)), 0.0)
        weights = weights * scores[:, :, None] * part_step[None, :, :]
        within = jnp.einsum("ijh,jhp->ihp", weights, part_inner, precision=highest)
        carried = jnp.exp(cumulative)[:, :, None] * jnp.einsum(
            "in,hpn->ihp", part_output, carry_state, precision=highest
        )
        result = within + carried + skip_gain[None, :, None] * part_inner
        tail_weight = jnp.exp(cumulative[-1][None, :] - cumulative) * part_step
        update_term = jnp.einsum(
            "jh,jhp,jn->hpn", tail_weight, part_inner, part_input, precision=highest
        )
        carry_state = jnp.exp(cumulative[-1])[:, None, None] * carry_state + update_term
        return (carry_state, result)

    final, results = lax.scan(
        advance,
        initial,
        (
            to_blocks(inner_act),
            to_blocks(input_mix),
            to_blocks(output_mix),
            to_blocks(step_size),
            to_blocks(log_decay),
        ),
    )
    return (results.reshape(length, head_count, head_dim), final)


def combine_carry(earlier, latter):
    return (earlier[0] + latter[0], jnp.exp(latter[0])[:, None, None] * earlier[1] + latter[1])


def contract_rows(left_rows, right_rows):
    return lax.dot_general(
        left_rows, right_rows, (((0,), (0,)), ((), ())), preferred_element_type=jnp.float32
    )


def project_back(gradient, weight):
    return lax.dot_general(
        gradient, weight, (((1,), (1,)), ((), ())), preferred_element_type=jnp.float32
    )


def split_pair(values):
    leading = values.astype(jnp.bfloat16)
    residue = (values - leading.astype(jnp.float32)).astype(jnp.bfloat16)
    return (leading, residue)


def body(
    layer_input,
    inner_weight,
    mixer_weight,
    step_weight,
    conv_inner,
    conv_mixer,
    step_bias,
    decay_log,
    skip_gain,
    output_grad,
):
    gathered = lax.all_gather(layer_input[0], "chan", axis=0, tiled=True)
    seg_len = gathered.shape[0]
    chan_count = lax.axis_size("chan")
    history_len = conv_inner.shape[0] - 1
    highest = lax.Precision.HIGHEST
    inner_proj = jnp.dot(gathered, inner_weight, preferred_element_type=jnp.float32).astype(
        jnp.bfloat16
    )
    mixer_proj = jnp.dot(gathered, mixer_weight, preferred_element_type=jnp.float32).astype(
        jnp.bfloat16
    )
    step_raw = jnp.dot(gathered, step_weight, preferred_element_type=jnp.float32)
    inner_hist, mixer_hist = from_behind(
        (inner_proj[seg_len - history_len :], mixer_proj[seg_len - history_len :]), "seq", 1
    )
    inner_wide = lax.optimization_barrier(inner_proj).astype(jnp.float32)
    mixer_wide = lax.optimization_barrier(mixer_proj).astype(jnp.float32)
    inner_prev = lax.optimization_barrier(inner_hist).astype(jnp.float32)
    mixer_prev = lax.optimization_barrier(mixer_hist).astype(jnp.float32)

    def local_acts(inner_in, mixer_in, step_in, inner_before, mixer_before):
        return activations(
            inner_in,
            mixer_in,
            step_in,
            inner_before,
            mixer_before,
            conv_inner,
            conv_mixer,
            step_bias,
            decay_log,
        )

    acts, pull_acts = jax.vjp(local_acts, inner_wide, mixer_wide, step_raw, inner_prev, mixer_prev)
    inner_act, input_mix, output_mix, step_size, log_decay = acts
    head_count = step_bias.shape[0]
    upstream = output_grad[0].astype(jnp.float32).reshape(seg_len, head_count, HDIM)
    cumulative = jnp.cumsum(log_decay, axis=0)
    segment_decay = cumulative[-1]
    local_state = jnp.einsum(
        "th,thp,tn->hpn",
        jnp.exp(segment_decay[None, :] - cumulative) * step_size,
        inner_act,
        input_mix,
        precision=highest,
    )
    local_grad = jnp.einsum(
        "th,thp,tn->hpn", jnp.exp(cumulative), upstream, output_mix, precision=highest
    )
    neutral = (jnp.zeros_like(segment_decay), jnp.zeros_like(local_state))
    start_state = prefix((segment_decay, local_state), "seq", combine_carry, neutral)[1]
    end_grad = prefix_2((segment_decay, local_grad), "seq", combine_carry, neutral)[1]

    def scan_local(inner_in, input_in, output_in, step_in, decay_in):
        return spanned_scan(
            inner_in, input_in, output_in, step_in, decay_in, skip_gain, start_state
        )

    unused, pull_scan = jax.vjp(scan_local, inner_act, input_mix, output_mix, step_size, log_decay)
    act_grads = pull_scan((upstream, end_grad))
    inner_local, mixer_local, step_local, inner_back, mixer_back = pull_acts(act_grads)
    inner_next, mixer_next = from_behind((inner_back, mixer_back), "seq", -1)
    keep_rows = seg_len - history_len
    inner_total = jnp.concatenate(
        [inner_local[:keep_rows], inner_local[keep_rows:] + inner_next], axis=0
    )
    grad_mixer = jnp.concatenate(
        [mixer_local[:keep_rows], mixer_local[keep_rows:] + mixer_next], axis=0
    )
    grad_inner = inner_total.astype(jnp.bfloat16)
    grad_step = step_local.astype(jnp.bfloat16)
    mixer_lead, mixer_rest = split_pair(grad_mixer)
    inner_rows, step_rows, lead_rows, rest_rows = (
        lax.all_to_all(grad_inner, "chan", split_axis=0, concat_axis=1, tiled=True),
        lax.all_to_all(grad_step, "chan", split_axis=0, concat_axis=1, tiled=True),
        lax.all_to_all(mixer_lead, "chan", split_axis=0, concat_axis=1, tiled=True),
        lax.all_to_all(mixer_rest, "chan", split_axis=0, concat_axis=1, tiled=True),
    )
    inner_full, step_full = (
        lax.all_gather(inner_weight, "chan", axis=1, tiled=True),
        lax.all_gather(step_weight, "chan", axis=1, tiled=True),
    )
    row_count = seg_len // chan_count
    mixer_rows = lead_rows.astype(jnp.float32) + rest_rows.astype(jnp.float32)
    mixer_rows = jnp.sum(mixer_rows.reshape(row_count, chan_count, -1), axis=1)
    rows_lead, rows_rest = split_pair(mixer_rows)
    summed = project_back(inner_rows, inner_full) + project_back(step_rows, step_full)
    summed = summed + project_back(rows_lead, mixer_weight) + project_back(rows_rest, mixer_weight)
    input_grad = summed.astype(jnp.bfloat16)
    token_count = seg_len * lax.axis_size("seq") * lax.axis_size("dp")
    norm_factor = 1.0 / math.sqrt(token_count)
    inner_term = contract_rows(gathered, grad_inner) * norm_factor
    step_term = contract_rows(gathered, grad_step) * norm_factor
    mixer_term = (
        contract_rows(gathered, mixer_lead) + contract_rows(gathered, mixer_rest)
    ) * norm_factor
    mixer_weight_grad = lax.psum_scatter(
        mixer_term, ("dp", "seq", "chan"), scatter_dimension=0, tiled=True
    )
    inner_weight_grad, step_weight_grad = (
        lax.psum_scatter(inner_term, ("dp", "seq"), scatter_dimension=0, tiled=True),
        lax.psum_scatter(step_term, ("dp", "seq"), scatter_dimension=0, tiled=True),
    )
    return (input_grad[None], inner_weight_grad, mixer_weight_grad, step_weight_grad)


def solution(mesh):
    in_specs = (
        P("dp", ("seq", "chan"), None),
        P(None, "chan"),
        P(),
        P(None, "chan"),
        P(None, "chan"),
        P(),
        P("chan"),
        P("chan"),
        P("chan"),
        P("dp", "seq", "chan"),
    )
    out_specs = (
        P("dp", ("seq", "chan"), None),
        P(("dp", "seq"), "chan"),
        P(("dp", "seq", "chan"), None),
        P(("dp", "seq"), "chan"),
    )
    return jax.shard_map(body, mesh=mesh, in_specs=in_specs, out_specs=out_specs, check_vma=False)
```

profile of v0, /device:TPU:0, one launch (start us, length us, event | category | flops | bytes accessed | tf_op | source)
XLA Modules:
  0.0 439.2 jit_solution(13962226168457161180)
XLA Ops:
  8.1 9.7 %all-gather = bf16[1,128,2560]{2,1,0:T(8,128)(2,1)S(1)} all-gather(bf16[1,32,2560]{2,1,0:T(8,128)(2,1)} %param.14), channel_id=2, replica_groups=mesh['dp'=2,'seq'=4,'chan'=4] {'chan'}, dimensions={1}, use_global_device_ids=true | all-gather | bytes 819200 | tf_op jit(solution)/shard_map/all_gather | solution.py:165
  18.2 3.5 collective-permute-start
  21.7 0.9 negate_multiply_fusion
  23.3 1.1 fusion.29
  24.6 2.6 convolution_convert_fusion.1
  27.2 3.9 collective-permute-start.1
  31.3 9.3 %all-gather.4 = bf16[4,1,10]{2,1,0:T(2,128)(2,1)S(1)} all-gather(bf16[1,1,10]{2,1,0:T(2,128)(2,1)S(1)} %bitcast.159), channel_id=1, replica_groups=mesh['dp'=2,'seq'=4,'chan'=4] {'seq'}, dimensions={0}, use_global_device_ids=true | all-gather | bytes 100 | tf_op jit(solution)/shard_map/all_gather | solution.py:23
  40.8 9.3 %all-gather.3 = f32[4,1,10]{2,1,0:T(1,128)S(1)} all-gather(f32[1,1,10]{2,1,0:T(1,128)S(1)} %bitcast.149), channel_id=1, replica_groups=mesh['dp'=2,'seq'=4,'chan'=4] {'seq'}, dimensions={0}, use_global_device_ids=true | all-gather | bytes 200 | tf_op jit(solution)/shard_map/all_gather | solution.py:42
  50.6 1.0 fusion.34
  51.6 1.1 copy.61
  52.7 5.9 %all-gather.11.cloned.1.call-done = f32[40,64,128]{2,1,0:T(8,128)} async-done(((f32[10,64,128]{2,1,0:T(8,128)}), f32[40,64,128]{2,1,0:T(8,128)}) %all-gather.11.cloned.1.call-update) | async-done | bytes 1310736 | tf_op jit(solution)/shard_map/all_gather | solution.py:42
  58.7 4.5 %while.23 = (s32[]{:T(128)}, f32[10,64,128]{2,1,0:T(8,128)S(1)}, s32[]{:T(128)}, f32[4,10]{1,0:T(4,128)S(1)}, f32[4,10,64,128]{3,2,1,0:T(8,128)}, /*index=5*/s32[]{:T(128)}, s32[]{:T(128)}, s32[]{:T(128)}, s32[]{:T(128)}) while((s32[]{:T(128)}, f32[10,64,128]{2,1,0:T(8,128)S(1)}, s32[]{:T(128)}, f32[4,10]{1,0:T(4,128)S(1)}, ...), condition=%wide.region_2.3_spmd.clone, body=%wide.region_1.2_spmd.clone.sunk | while | flops 327688 | bytes 983327 | solution.py:55
  58.7 1.1 fusion.111
  59.8 1.1 fusion.111
  61.0 1.1 fusion.111
  62.1 1.1 fusion.111
  63.2 1.2 multiply_reduce_fusion.2
  65.0 16.7 %all-gather.2 = bf16[40,64,128]{2,1,0:T(8,128)(2,1)} all-gather(bf16[10,64,128]{2,1,0:T(8,128)(2,1)S(1)} %convolution_convert_fusion), channel_id=4, replica_groups=mesh['dp'=2,'seq'=4,'chan'=4] {'seq'}, dimensions={0}, use_global_device_ids=true | all-gather | bytes 819200 | tf_op jit(solution)/shard_map/all_gather | solution.py:23
  82.6 1.5 fusion.21
  84.3 1.1 reduce_window_sum.31
  85.5 0.8 fusion.76
  87.1 1.6 copy.78
  89.4 0.7 convolution_bitcast_fusion.3
  90.1 0.7 convolution_bitcast_fusion.2
  91.5 1.3 collective-permute-start.3
  92.9 4.1 collective-permute-done.3
  97.6 2.0 fusion.2
  99.6 3.6 copy.76
  103.5 0.7 copy-done.2
  105.3 1.3 collective-permute-start.2
  106.8 4.2 collective-permute-done.2
  111.0 0.7 maximum_convert_fusion
  111.7 4.7 %multiply_bitcast_fusion = f32[2560,640]{0,1:T(8,128)} fusion(bf16[128,640]{1,0:T(8,128)(2,1)} %maximum_convert_fusion, bf16[1,128,2560]{2,1,0:T(8,128)(2,1)S(1)} %all-gather), kind=kOutput, calls=%fused_computation.5 | convolution fusion | flops 421068800 | bytes 7372800 | tf_op jit(solution)/shard_map/dot_general | solution.py:136
  116.4 8.2 %copy.74 = f32[2560,640]{1,0:T(8,128)} copy(f32[2560,640]{0,1:T(8,128)} %multiply_bitcast_fusion) | data formatting | bytes 13107200
  125.4 0.7 reshape.372
  126.1 3.2 all-to-all-start.1
  130.0 3.3 all-to-all-done.1
  133.2 7.4 %all_to_all.55 = bf16[4,32,256]{2,1,0:T(8,128)(2,1)S(1)} all-to-all(bf16[4,32,256]{2,1,0:T(8,128)(2,1)S(1)} %get-tuple-element.587), channel_id=1, replica_groups=mesh['dp'=2,'seq'=4,'chan'=4] {'chan'}, dimensions={0} | all-to-all | bytes 131072 | tf_op jit(solution)/shard_map/all_to_all | solution.py:240
  140.6 3.3 all-to-all-start.3
  143.9 9.3 %all-gather.5 = bf16[4,10,2560]{2,1,0:T(8,128)(2,1)S(1)} all-gather(bf16[1,10,2560]{2,1,0:T(8,128)(2,1)S(1)} %bitcast.147), channel_id=1, replica_groups=mesh['dp'=2,'seq'=4,'chan'=4] {'chan'}, dimensions={0}, use_global_device_ids=true | all-gather | bytes 256000 | tf_op jit(solution)/shard_map/all_gather | solution.py:245
  153.4 3.4 all-to-all-start
  156.8 7.0 %all-to-all-done = bf16[4,32,640]{2,1,0:T(8,128)(2,1)S(1)} async-done(((bf16[4,32,640]{2,1,0:T(8,128)(2,1)}), bf16[4,32,640]{2,1,0:T(8,128)(2,1)S(1)}, u32[]{:S(2)}, u32[]{:S(2)}) %all-to-all-start) | async-done | bytes 163872 | tf_op jit(solution)/shard_map/all_to_all | solution.py:238
  163.9 1.6 copy.79
  165.6 19.5 %all-gather.9.cloned.1.call-done = bf16[2560,2560]{1,0:T(8,128)(2,1)} async-done(((bf16[2560,640]{1,0:T(8,128)(2,1)}), bf16[2560,2560]{1,0:T(8,128)(2,1)}) %all-gather.9.cloned.1.call-update) | async-done | bytes 13107216 | tf_op jit(solution)/shard_map/all_gather | solution.py:244
  185.1 8.6 %fusion.88 = f32[32,2560]{1,0:T(8,128)S(1)} fusion(bf16[32,2560]{1,0:T(8,128)(2,1)S(1)} %bitcast.145, bf16[2560,2560]{1,0:T(8,128)(2,1)} %all-gather.9.cloned.1.call-done), kind=kOutput, calls=%fused_computation.165 | convolution fusion | flops 419430400 | bytes 13598720 | tf_op jit(solution)/shard_map/dot_general | solution.py:142
  194.5 1.2 fusion.5
  195.7 113.7 %reduce-scatter.12.cloned.1.call-done = f32[80,256]{1,0:T(8,128)} async-done(((f32[2560,256]{1,0:T(8,128)}), f32[80,256]{1,0:T(8,128)}) %reduce-scatter.12.cloned.1.call-update) | async-done | bytes 81936
  309.4 122.7 %reduce-scatter.10.cloned.1.call-done = f32[320,640]{1,0:T(8,128)} async-done(((f32[2560,640]{1,0:T(8,128)}), f32[320,640]{1,0:T(8,128)}) %reduce-scatter.10.cloned.1.call-update) | async-done | bytes 819216
  (164 shorter events, 10.2 us)
Async XLA Ops:
  8.0 9.8 %copy-start = (bf16[2560,256]{1,0:T(8,128)(2,1)S(1)}, bf16[2560,256]{1,0:T(8,128)(2,1)}, u32[]{:S(2)}) copy-start(bf16[2560,256]{1,0:T(8,128)(2,1)} %param.16) | copy-start | bytes 3932164
  8.0 13.7 %copy-start.38 = (f32[10]{0:T(128)S(1)}, f32[10]{0:T(128)}, u32[]{:S(2)}) copy-start(f32[10]{0:T(128)} %param.21) | copy-start | bytes 124
  8.0 13.7 %copy-start.5 = (bf16[2560,10]{0,1:T(8,128)(2,1)S(1)}, bf16[2560,10]{0,1:T(8,128)(2,1)}, u32[]{:S(2)}) copy-start(bf16[2560,10]{0,1:T(8,128)(2,1)} %param.17) | copy-start | bytes 153604
  8.0 13.7 %copy-start.39 = (f32[10]{0:T(128)S(1)}, f32[10]{0:T(128)}, u32[]{:S(2)}) copy-start(f32[10]{0:T(128)} %param.20) | copy-start | bytes 124
  8.0 14.6 %copy-start.36 = (f32[4,256]{1,0:T(4,128)S(1)}, f32[4,256]{1,0:T(4,128)}, u32[]{:S(2)}) copy-start(f32[4,256]{1,0:T(4,128)} %param.19) | copy-start | bytes 12292
  8.1 15.0 %copy-start.4 = (bf16[1,128,640]{2,1,0:T(8,128)(2,1)S(1)}, bf16[1,128,640]{2,1,0:T(8,128)(2,1)}, u32[]{:S(2)}) copy-start(bf16[1,128,640]{2,1,0:T(8,128)(2,1)} %param.23) | copy-start | bytes 491524
  8.1 50.6 %all-gather.11.cloned.1.call-start = ((), (), s32[]{:S(2)}) async-start(), calls=%async_computation.8 | async-start | bytes 1638400 | tf_op jit(solution)/shard_map/all_gather | solution.py:42
  18.2 5.1 %collective-permute-start = (bf16[3,256]{1,0:T(4,128)(2,1)S(1)}, bf16[3,256]{1,0:T(4,128)(2,1)S(1)}, u32[]{:S(2)}, u32[]{:S(2)}) collective-permute-start(bf16[3,256]{1,0:T(4,128)(2,1)S(1)} %slice.103), channel_id=1, source_target_pairs={{0,4},{4,8},{8,12},{1,5},{5,9},{9,13},{2,6},{6,10},{10,14},{3,7},{... | collective-permute-start | bytes 4616 | tf_op jit(solution)/shard_map/ppermute | solution.py:17
  22.6 4.5 %copy-start.26 = (f32[1,256]{1,0:T(1,128)}, f32[1,256]{1,0:T(1,128)S(1)}, u32[]{:S(2)}) copy-start(f32[1,256]{1,0:T(1,128)S(1)} %get-tuple-element.605) | copy-start | bytes 3076
  22.6 4.5 %copy-start.28 = (f32[1,256]{1,0:T(1,128)}, f32[1,256]{1,0:T(1,128)S(1)}, u32[]{:S(2)}) copy-start(f32[1,256]{1,0:T(1,128)S(1)} %get-tuple-element.606) | copy-start | bytes 3076
  22.6 4.5 %copy-start.30 = (f32[1,256]{1,0:T(1,128)}, f32[1,256]{1,0:T(1,128)S(1)}, u32[]{:S(2)}) copy-start(f32[1,256]{1,0:T(1,128)S(1)} %get-tuple-element.608) | copy-start | bytes 3076
  22.6 4.5 %copy-start.32 = (f32[1,256]{1,0:T(1,128)}, f32[1,256]{1,0:T(1,128)S(1)}, u32[]{:S(2)}) copy-start(f32[1,256]{1,0:T(1,128)S(1)} %get-tuple-element.607) | copy-start | bytes 3076
  24.5 25.7 %copy-start.25 = (f32[4,640]{1,0:T(4,128)S(1)}, f32[4,640]{1,0:T(4,128)}, u32[]{:S(2)}) copy-start(f32[4,640]{1,0:T(4,128)} %param.18) | copy-start | bytes 30724
  24.5 139.4 %reduce-scatter.14.cloned.1.call-start = ((), (), s32[]{:S(2)}) async-start(), calls=%async_computation.11 | async-start | bytes 1474560
  27.2 23.3 %collective-permute-start.1 = (bf16[3,640]{1,0:T(4,128)(2,1)S(1)}, bf16[3,640]{1,0:T(4,128)(2,1)S(1)}, u32[]{:S(2)}, u32[]{:S(2)}) collective-permute-start(bf16[3,640]{1,0:T(4,128)(2,1)S(1)} %slice.111), channel_id=1, source_target_pairs={{0,4},{4,8},{8,12},{1,5},{5,9},{9,13},{2,6},{6,10},{10,14},{3,7},{... | collective-permute-start | bytes 11528 | tf_op jit(solution)/shard_map/ppermute | solution.py:17
  40.8 43.3 %copy-start.24 = (f32[10]{0:T(128)}, f32[10]{0:T(128)S(1)}, u32[]{:S(2)}) copy-start(f32[10]{0:T(128)S(1)} %slice_reduce_fusion) | copy-start | bytes 124
  50.2 32.4 %copy-start.22 = (pred[128,128]{1,0:T(8,128)(4,1)}, pred[128,128]{1,0:T(8,128)(4,1)S(1)}, u32[]{:S(2)}) copy-start(pred[128,128]{1,0:T(8,128)(4,1)S(1)} %iota_compare_fusion) | copy-start | bytes 49156
  50.2 8.4 %copy-start.12 = (f32[640]{0:T(1024)}, f32[640]{0:T(1024)S(1)}, u32[]{:S(2)}) copy-start(f32[640]{0:T(1024)S(1)} %get-tuple-element.563) | copy-start | bytes 7684
  50.2 8.4 %copy-start.14 = (f32[640]{0:T(1024)}, f32[640]{0:T(1024)S(1)}, u32[]{:S(2)}) copy-start(f32[640]{0:T(1024)S(1)} %get-tuple-element.564) | copy-start | bytes 7684
  50.3 8.4 %copy-start.16 = (f32[640]{0:T(1024)}, f32[640]{0:T(1024)S(1)}, u32[]{:S(2)}) copy-start(f32[640]{0:T(1024)S(1)} %get-tuple-element.565) | copy-start | bytes 7684
  50.3 8.4 %copy-start.18 = (f32[640]{0:T(1024)}, f32[640]{0:T(1024)S(1)}, u32[]{:S(2)}) copy-start(f32[640]{0:T(1024)S(1)} %get-tuple-element.562) | copy-start | bytes 7684
  50.5 32.1 %copy-start.10 = (f32[128,128]{1,0:T(8,128)}, f32[128,128]{1,0:T(8,128)S(1)}, u32[]{:S(2)}) copy-start(f32[128,128]{1,0:T(8,128)S(1)} %fusion.64) | copy-start | bytes 196612
  58.6 5.7 %copy-start.9 = (f32[128,10]{0,1:T(8,128)S(1)}, f32[128,10]{0,1:T(8,128)}, u32[]{:S(2)}) copy-start(f32[128,10]{0,1:T(8,128)} %get-tuple-element.610) | copy-start | bytes 15364
  64.5 17.1 %copy-start.7 = (f32[128,10]{0,1:T(8,128)}, f32[128,10]{0,1:T(8,128)S(1)}, u32[]{:S(2)}) copy-start(f32[128,10]{0,1:T(8,128)S(1)} %get-tuple-element.603) | copy-start | bytes 15364
  64.6 18.0 %copy-start.34 = (f32[128,10]{0,1:T(8,128)}, f32[128,10]{0,1:T(8,128)S(1)}, u32[]{:S(2)}) copy-start(f32[128,10]{0,1:T(8,128)S(1)} %get-tuple-element.604) | copy-start | bytes 15364
  88.7 1.5 copy-start.8
  88.7 2.2 copy-start.3
  88.7 2.7 copy-start.33
  88.7 2.7 copy-start.27
  88.7 2.7 copy-start.29
  88.7 2.7 copy-start.31
  88.8 96.3 %all-gather.9.cloned.1.call-start = ((), (), s32[]{:S(2)}) async-start(), calls=%async_computation.7 | async-start | bytes 16384000 | tf_op jit(solution)/shard_map/all_gather | solution.py:244
  89.3 220.1 %reduce-scatter.12.cloned.1.call-start = ((), (), s32[]{:S(2)}) async-start(), calls=%async_computation.10 | async-start | bytes 2703360
  91.5 5.5 %collective-permute-start.3 = (f32[3,256]{1,0:T(4,128)S(1)}, f32[3,256]{1,0:T(4,128)S(1)}, u32[]{:S(2)}, u32[]{:S(2)}) collective-permute-start(f32[3,256]{1,0:T(4,128)S(1)} %pad_add_fusion.3), channel_id=1, source_target_pairs={{4,0},{8,4},{12,8},{5,1},{9,5},{13,9},{6,2},{10,6},{14,10},{7,3},{... | collective-permute-start | bytes 9224 | tf_op jit(solution)/shard_map/ppermute | solution.py:17
  103.2 1.0 copy-start.11
  103.2 1.0 copy-start.23
  103.2 1.0 copy-start.35
  103.2 1.8 copy-start.1
  103.2 1.8 copy-start.19
  103.2 2.0 copy-start.13
  103.2 2.0 copy-start.15
  103.2 2.0 copy-start.17
  103.3 328.8 %reduce-scatter.10.cloned.1.call-start = ((), (), s32[]{:S(2)}) async-start(), calls=%async_computation.9 | async-start | bytes 7372800
  105.3 5.7 %collective-permute-start.2 = (f32[3,640]{1,0:T(4,128)S(1)}, f32[3,640]{1,0:T(4,128)S(1)}, u32[]{:S(2)}, u32[]{:S(2)}) collective-permute-start(f32[3,640]{1,0:T(4,128)S(1)} %pad_add_fusion.2), channel_id=1, source_target_pairs={{4,0},{8,4},{12,8},{5,1},{9,5},{13,9},{6,2},{10,6},{14,10},{7,3},{... | collective-permute-start | bytes 23048 | tf_op jit(solution)/shard_map/ppermute | solution.py:17
  124.6 19.3 %copy-start.6 = (bf16[2560,10]{0,1:T(8,128)(2,1)S(1)}, bf16[2560,10]{0,1:T(8,128)(2,1)}, u32[]{:S(2)}) copy-start(bf16[2560,10]{0,1:T(8,128)(2,1)} %param.17) | copy-start | bytes 153604
  126.1 7.2 %all-to-all-start.1 = ((bf16[4,2,160]{2,1,0:T(2,128)(2,1)}), bf16[4,2,160]{2,1,0:T(2,128)(2,1)S(1)}, u32[]{:S(2)}, u32[]{:S(2)}) async-start(bf16[4,2,160]{2,1,0:T(2,128)(2,1)} %reshape.372), calls=%async_computation.1 | async-start | bytes 8192 | tf_op jit(solution)/shard_map/all_to_all | solution.py:239
  140.6 12.8 %all-to-all-start.3 = ((bf16[4,32,256]{2,1,0:T(8,128)(2,1)}), bf16[4,32,256]{2,1,0:T(8,128)(2,1)S(1)}, u32[]{:S(2)}, u32[]{:S(2)}) async-start(bf16[4,32,256]{2,1,0:T(8,128)(2,1)} %get-tuple-element.586), calls=%async_computation.3 | async-start | bytes 131072 | tf_op jit(solution)/shard_map/all_to_all | solution.py:241
  153.4 10.5 %all-to-all-start = ((bf16[4,32,640]{2,1,0:T(8,128)(2,1)}), bf16[4,32,640]{2,1,0:T(8,128)(2,1)S(1)}, u32[]{:S(2)}, u32[]{:S(2)}) async-start(bf16[4,32,640]{2,1,0:T(8,128)(2,1)} %bitcast.15), calls=%async_computation | async-start | bytes 327680 | tf_op jit(solution)/shard_map/all_to_all | solution.py:238
  (5 other events, 4.2 us)
Sparse Core Ops, SparseCore 0:
  24.6 33.9 all-gather.10
  88.8 68.8 reduce-scatter.13
  160.5 148.8 reduce-scatter.11
  313.4 118.5 reduce-scatter.9
Sparse Core Ops, SparseCore 1:
  90.8 94.2 all-gather.8
where the time goes:
time: 440 us; the launch traced here: 439 us
  waiting for transfers between devices  281 us (64%)
  blocking collectives  61.7 us (14%)
  matrix products  29.3 us (7%)
  local copies, waits for them, and re-layouts  20.6 us (5%)
  starting transfers between devices  20.2 us (5%)
  between operations  16 us (4%)
  other arithmetic  10 us (2%)
    unnamed x8, waiting for transfers between devices  237 us
    all_gather x2, blocking collectives, prefix(): lax.all_gather(a.astype(kind), axis)  25.9 us
    all_gather x1, waiting for transfers between devices, body(): lax.all_gather(inner_weight, 'chan', axis=1, tiled=True)  19.5 us
    unnamed x91, local copies, waits for them, and re-layouts  18.1 us
    dot_general x4, matrix products, project_back(): lax.dot_general(gradient, weight, (((1,), (1,)), ((), ())), preferred_ele...  10.6 us
    ppermute x4, starting transfers between devices, from_behind(): lax.ppermute(value, axis, [(source, source + steps) for source in range(f...  9.96 us
    all_gather x1, blocking collectives, body(): gathered = lax.all_gather(layer_input[0], 'chan', axis=0, tiled=True)  9.7 us
    all_gather x1, blocking collectives, body(): lax.all_gather(step_weight, 'chan', axis=1, tiled=True)  9.33 us
  transfers between devices with their start and end apart: 12, of which 8 were waited for; matrix products, arithmetic and copies ran while one was open for 10% of the time, Pallas kernels for 0%

commit v1 on v0

v1 whole, which is shorter than its diff:
```python
import functools
import math

import jax
import jax.numpy as jnp
from jax import lax
from jax.experimental import pallas as pl
from jax.experimental.pallas import tpu as pltpu
from jax.sharding import PartitionSpec as P


F32 = jnp.float32
BF16 = jnp.bfloat16
LANES = 128
PAD = 8
HIGHEST = lax.Precision.HIGHEST
DIRECT = 8


def dot(left, right, left_dim=1, right_dim=0, precision=None):
    return lax.dot_general(
        left,
        right,
        (((left_dim,), (right_dim,)), ((), ())),
        precision=precision,
        preferred_element_type=F32,
    )


def pieces(values):
    high = values.astype(BF16)
    rest = values - high.astype(F32)
    middle = rest.astype(BF16)
    low = (rest - middle.astype(F32)).astype(BF16)
    return high, middle, low


def head_map(width, head_dim):
    row = lax.broadcasted_iota(jnp.int32, (LANES, width), 0)
    column = lax.broadcasted_iota(jnp.int32, (LANES, width), 1)
    start = row * head_dim
    return jnp.where((column >= start) & (column < start + head_dim), 1.0, 0.0).astype(BF16)


def spread(values, heads):
    high, middle, low = pieces(values)
    return dot(high, heads) + dot(middle, heads) + dot(low, heads)


def collect(values, heads):
    high, middle, low = pieces(values)
    return dot(high, heads, 1, 1) + dot(middle, heads, 1, 1) + dot(low, heads, 1, 1)


def sigmoid(values):
    return 1.0 / (1.0 + jnp.exp(-values))


def softplus(values):
    small = jnp.exp(-jnp.abs(values))
    series = small * (1.0 - small * (0.5 - small * (1.0 / 3.0)))
    return jnp.maximum(values, 0.0) + jnp.where(small < 1e-3, series, jnp.log(1.0 + small))


def triangle(length):
    row = lax.broadcasted_iota(jnp.int32, (length, length), 0)
    column = lax.broadcasted_iota(jnp.int32, (length, length), 1)
    return row, column


def convolve(values, history, kernel, scratch):
    length = values.shape[0]
    taps = kernel.shape[0]
    scratch[:PAD] = history.astype(F32)
    scratch[PAD:] = values.astype(F32)
    total = kernel[taps - 1 : taps] * scratch[PAD : PAD + length]
    for tap in range(taps - 1):
        start = PAD - (taps - 1) + tap
        total = total + kernel[tap : tap + 1] * scratch[start : start + length]
    return total


def convolve_back(gradient, kernel, scratch):
    length = gradient.shape[0]
    taps = kernel.shape[0]
    zeros = jnp.zeros((PAD, gradient.shape[1]), F32)
    scratch[:PAD] = zeros
    scratch[PAD : PAD + length] = gradient
    scratch[PAD + length :] = zeros
    extent = length + PAD
    total = None
    for tap in range(taps):
        start = taps - 1 - tap
        term = kernel[tap : tap + 1] * scratch[start : start + extent]
        total = term if total is None else total + term
    return total


def blocks(
    rows,
    padded,
    dp_count,
    place_ref,
    own_ref,
    step_ref,
    bias_ref,
    log_ref,
    skip_ref,
    out_ref,
    head_ref,
    near_ref,
    far_ref,
    scratch,
):
    dp_place = place_ref[1]
    seq_count = out_ref.shape[0]
    head_count = bias_ref.shape[1]
    scratch[...] = jnp.zeros_like(scratch)
    scratch[:head_count] = step_ref[...].astype(F32)
    turned = scratch[...].T.astype(BF16)
    near_ref[...] = turned
    far_ref[...] = turned
    head_ref[...] = jnp.zeros_like(head_ref)
    head_ref[0:1, :head_count] = bias_ref[...]
    head_ref[1:2, :head_count] = log_ref[...]
    head_ref[2:3, :head_count] = skip_ref[...]
    fill = jnp.zeros((own_ref.shape[0], padded - rows), F32)
    for target in range(seq_count):
        for hop in range(dp_count):
            wanted = lax.rem(dp_place + hop, dp_count)
            chosen = None
            for other in range(dp_count):
                start = (other * seq_count + target) * rows
                part = own_ref[:, start : start + rows].astype(F32)
                chosen = part if chosen is None else jnp.where(wanted == other, part, chosen)
            span = slice(hop * padded, (hop + 1) * padded)
            if padded > rows:
                chosen = jnp.concatenate([chosen, fill], axis=1)
            out_ref[target, :, span] = chosen.astype(BF16)


def add_up(*refs):
    total = refs[0][...].astype(F32)
    for part in refs[1:-1]:
        total = total + part[...].astype(F32)
    refs[-1][...] = total.astype(refs[-1].dtype)


def project(count, place_ref, *refs):
    tokens = refs[:count]
    inner_ref, mixer_ref, step_ref, inner_out, mixer_out, raw_out, tail_out, scratch = refs[count:]
    place = place_ref[2]
    rows = tokens[0].shape[0]
    for hop in range(count):
        source = lax.rem(place - hop + count, count)
        scratch[pl.ds(pl.multiple_of(source * rows, rows), rows)] = tokens[hop][...]
    gathered = scratch[...]
    length = gathered.shape[0]
    width = inner_ref.shape[1]
    whole = width // (2 * LANES) * (2 * LANES)
    mixer = dot(gathered, mixer_ref[...]).astype(BF16)
    first = dot(gathered, inner_ref[:, :whole]).astype(BF16)
    joined = jnp.concatenate([inner_ref[:, whole:], step_ref[...]], axis=1)
    second = dot(gathered, joined)
    raw_out[...] = second[:, width - whole :]
    inner = jnp.concatenate([first, second[:, : width - whole].astype(BF16)], axis=1)
    inner_out[...] = inner
    mixer_out[...] = mixer
    tail_out[:, :width] = inner[length - 2 * PAD :]
    tail_out[:, width:] = mixer[length - 2 * PAD :]


def prepare(head_dim, relative, place_ref, *refs):
    (
        inner_ref,
        mixer_ref,
        history_ref,
        raw_ref,
        head_ref,
        upstream_ref,
        conv_inner_ref,
        conv_mixer_ref,
        inner_pre_ref,
        mixer_pre_ref,
        step_ref,
        decay_ref,
    ) = refs[:12]
    message_refs = refs[12:-2]
    inner_scratch, mixer_scratch = refs[-2:]
    length, width = inner_ref.shape
    state = mixer_ref.shape[1] // 2
    place = place_ref[0]
    history = history_ref[...].astype(F32)[PAD:]
    inner_pre = convolve(inner_ref[...], history[:, :width], conv_inner_ref[...], inner_scratch)
    mixer_pre = convolve(mixer_ref[...], history[:, width:], conv_mixer_ref[...], mixer_scratch)
    inner_pre_ref[...] = inner_pre
    mixer_pre_ref[...] = mixer_pre
    inner_act = inner_pre * sigmoid(inner_pre)
    mixer_act = mixer_pre * sigmoid(mixer_pre)
    step = softplus(raw_ref[...] + head_ref[0:1])
    log_decay = -step * jnp.exp(head_ref[1:2])
    row, column = triangle(length)
    lower = jnp.where(row >= column, 1.0, 0.0)
    decay = dot(lower, log_decay, precision=HIGHEST)
    step_ref[...] = step
    decay_ref[...] = decay
    heads = head_map(width, head_dim)
    last = decay[length - 1 : length]
    tail = spread(jnp.exp(last - decay) * step, heads)
    lead = spread(jnp.exp(decay), heads)
    upstream = upstream_ref[...].astype(F32)
    forward = dot(mixer_act[:, :state], tail * inner_act, 0, 0, HIGHEST).astype(BF16)
    backward = dot(mixer_act[:, state:], lead * upstream, 0, 0, HIGHEST).astype(BF16)
    high, middle, low = pieces(last)
    kinds = (high.astype(F32), middle.astype(F32), low.astype(F32))
    index = lax.broadcasted_iota(jnp.int32, (PAD, LANES), 0)
    stacked = jnp.zeros((PAD, LANES), F32)
    for number, kind in enumerate(kinds):
        stacked = jnp.where(index == number, kind, stacked)
    extra = dot(stacked.astype(BF16), heads).astype(BF16)
    if relative:
        count = len(message_refs) + 1
        for hop, message_ref in enumerate(message_refs, 1):
            message_ref[:state] = jnp.where(place + hop < count, forward, backward)
            message_ref[state:] = extra
    else:
        message_ref = message_refs[0]
        for target in range(message_ref.shape[0]):
            message_ref[target, :state] = jnp.where(target > place, forward, backward)
            message_ref[target, state:] = extra


def within(
    head_dim,
    inner_pre_ref,
    mixer_pre_ref,
    step_ref,
    decay_ref,
    head_ref,
    upstream_ref,
    inner_grad_ref,
    mixer_grad_ref,
    row_ref,
    column_ref,
):
    length, width = inner_pre_ref.shape
    state = mixer_pre_ref.shape[1] // 2
    mixer_pre = mixer_pre_ref[...]
    mixer_act = mixer_pre * sigmoid(mixer_pre)
    input_mix = mixer_act[:, :state]
    output_mix = mixer_act[:, state:]
    decay = decay_ref[...]
    step = step_ref[...]
    turned = decay.T
    row, column = triangle(length)
    causal = column >= row
    scores = dot(input_mix, output_mix, 1, 1, HIGHEST)
    heads = head_map(width, head_dim)
    skip = spread(head_ref[...], heads)[2:3]
    step_wide = spread(step, heads)
    group_heads = LANES // head_dim
    lane = lax.broadcasted_iota(jnp.int32, (length, LANES), 1)
    mixed = jnp.zeros((length, length), F32)
    rows = jnp.zeros((length, LANES), F32)
    columns = []
    for group in range(width // LANES):
        span = slice(group * LANES, (group + 1) * LANES)
        inner_pre = inner_pre_ref[:, span]
        inner_act = inner_pre * sigmoid(inner_pre)
        high = inner_act.astype(BF16)
        low = (inner_act - high.astype(F32)).astype(BF16)
        upstream = upstream_ref[:, span]
        total = None
        for member in range(group_heads):
            head = group * group_heads + member
            mine = (lane >= member * head_dim) & (lane < (member + 1) * head_dim)
            mine_upstream = jnp.where(mine, upstream.astype(F32), 0.0).astype(BF16)
            spread_of = turned[head : head + 1] - decay[:, head : head + 1]
            fall = jnp.exp(jnp.where(causal, spread_of, -1e30))
            match = dot(high, mine_upstream, 1, 1) + dot(low, mine_upstream, 1, 1)
            weight = fall * scores
            cross = weight * match
            step_column = step[:, head : head + 1]
            mixed = mixed + step_column * (fall * match)
            rows = jnp.where(lane == head, jnp.sum(cross, axis=1, keepdims=True), rows)
            columns.append(jnp.sum(step_column * cross, axis=0, keepdims=True))
            weight_high = weight.astype(BF16)
            weight_low = (weight - weight_high.astype(F32)).astype(BF16)
            term = dot(weight_high, mine_upstream) + dot(weight_low, mine_upstream)
            total = term if total is None else total + term
        inner_grad_ref[:, span] = step_wide[:, span] * total + skip[:, span] * upstream.astype(F32)
    mixer_grad_ref[:, :state] = dot(mixed, output_mix, precision=HIGHEST)
    mixer_grad_ref[:, state:] = dot(mixed, input_mix, 0, 0, HIGHEST)
    row_ref[...] = rows
    index = lax.broadcasted_iota(jnp.int32, (LANES, length), 0)
    stacked = jnp.zeros((LANES, length), F32)
    for number, kind in enumerate(columns):
        stacked = jnp.where(index == number, kind, stacked)
    column_ref[...] = stacked


def finish(
    head_dim,
    relative,
    count,
    chan_count,
    place_ref,
    *refs,
):
    messages = refs[: count - 1] if relative else refs[:1]
    inner_scratch, mixer_scratch = refs[-2:]
    mixer_sent_refs = refs[-2 - chan_count : -2]
    refs = refs[len(messages) : -2 - chan_count]
    (
        inner_pre_ref,
        mixer_pre_ref,
        step_ref,
        decay_ref,
        raw_ref,
        head_ref,
        upstream_ref,
        conv_inner_ref,
        conv_mixer_ref,
        inner_grad_ref,
        mixer_grad_ref,
        row_ref,
        column_ref,
        pair_ref,
        mixer_out_ref,
        step_out_ref,
    ) = refs
    length, width = inner_pre_ref.shape
    state = mixer_pre_ref.shape[1] // 2
    place = place_ref[0]

    def message(hop):
        if relative:
            return messages[hop - 1][...].astype(F32)
        return messages[0][lax.rem(place - hop + count, count)].astype(F32)

    def shard_decay(parts):
        return parts[state : state + 1] + parts[state + 1 : state + 2] + parts[state + 2 : state + 3]

    start = jnp.zeros((state, width), F32)
    running = jnp.zeros((1, width), F32)
    end = jnp.zeros((state, width), F32)
    if relative:
        received = [None] + [message(hop) for hop in range(1, count)]
        back_running = jnp.zeros((1, width), F32)
        for hop in range(1, count):
            factor = jnp.where(hop <= place, jnp.exp(running), 0.0)
            start = start + factor * received[hop][:state]
            running = running + shard_decay(received[hop])
            other = count - hop
            factor = jnp.where(other > place, jnp.exp(back_running), 0.0)
            end = end + factor * received[other][:state]
            back_running = back_running + shard_decay(received[other])
    else:

        def before(hop, carried):
            start, running = carried
            parts = message(hop)
            return start + jnp.exp(running) * parts[:state], running + shard_decay(parts)

        def after(step, carried):
            end, running = carried
            parts = message(count - step)
            return end + jnp.exp(running) * parts[:state], running + shard_decay(parts)

        start, unused = lax.fori_loop(1, place + 1, before, (start, running))
        end, unused = lax.fori_loop(1, count - place, after, (end, running))

    inner_pre = inner_pre_ref[...]
    mixer_pre = mixer_pre_ref[...]
    inner_sig = sigmoid(inner_pre)
    mixer_sig = sigmoid(mixer_pre)
    inner_act = inner_pre * inner_sig
    mixer_act = mixer_pre * mixer_sig
    input_mix = mixer_act[:, :state]
    output_mix = mixer_act[:, state:]
    decay = decay_ref[...]
    step = step_ref[...]
    upstream = upstream_ref[...].astype(F32)
    heads = head_map(width, head_dim)
    last = decay[length - 1 : length]
    lead = jnp.exp(decay)
    rest = jnp.exp(last - decay)
    lead_wide = spread(lead, heads)
    tail_wide = spread(rest * step, heads)
    from_end = dot(input_mix, end, precision=HIGHEST)
    from_start = dot(output_mix, start, precision=HIGHEST)
    inner_grad = inner_grad_ref[...] + tail_wide * from_end
    input_grad = mixer_grad_ref[:, :state] + dot(tail_wide * inner_act, end, 1, 1, HIGHEST)
    output_grad = mixer_grad_ref[:, state:] + dot(lead_wide * upstream, start, 1, 1, HIGHEST)
    end_part = rest * collect(inner_act * from_end, heads)
    start_part = lead * collect(upstream * from_start, heads)
    product = jnp.sum(end * start, axis=0, keepdims=True)
    product = collect(jnp.broadcast_to(product, (PAD, width)), heads)[0:1]
    step_grad = row_ref[...] + end_part
    sums = start_part - step * step_grad
    total = jnp.sum(step * end_part, axis=0, keepdims=True) + jnp.exp(last) * product
    row, column = triangle(length)
    upper = jnp.where(column >= row, 1.0, 0.0)
    decay_grad = (
        dot(upper, sums, precision=HIGHEST) + dot(upper, column_ref[...], 1, 1, HIGHEST) + total
    )
    step_grad = step_grad - jnp.exp(head_ref[1:2]) * decay_grad
    raw_grad = step_grad * sigmoid(raw_ref[...] + head_ref[0:1])
    step_out_ref[...] = raw_grad.astype(BF16)
    turned = raw_grad.T
    groups = width // length
    packed = jnp.zeros((PAD, width), F32)
    index = lax.broadcasted_iota(jnp.int32, (PAD, width), 0)
    head_count = width // head_dim
    for number in range(-(-head_count // groups)):
        line = [turned[number * groups + group : number * groups + group + 1] for group in range(groups)]
        packed = jnp.where(index == number, jnp.concatenate(line, axis=1), packed)
    inner_slope = inner_sig * (1.0 + inner_pre * (1.0 - inner_sig))
    mixer_slope = mixer_sig * (1.0 + mixer_pre * (1.0 - mixer_sig))
    inner_total = convolve_back(inner_grad * inner_slope, conv_inner_ref[...], inner_scratch)
    mixer_total = jnp.concatenate([input_grad, output_grad], axis=1) * mixer_slope
    mixer_total = convolve_back(mixer_total, conv_mixer_ref[...], mixer_scratch)
    taps = conv_inner_ref.shape[0] - 1
    early = PAD - taps
    inner_scratch[:PAD] = jnp.where(index >= early, inner_total[:PAD], packed)
    mixed = 2 * state
    inner_scratch[early - taps : early, :mixed] = mixer_total[early:PAD]
    pair_ref[:length] = inner_total[PAD:].astype(BF16)
    pair_ref[length:] = inner_scratch[:PAD].astype(BF16)
    mixer_out_ref[...] = mixer_total[PAD:].astype(BF16)
    rows = length // chan_count
    back = mixer_total[:PAD].astype(BF16)
    mixer_scratch[:length] = mixer_total[PAD:]
    for hop, sent_ref in enumerate(mixer_sent_refs):
        target = lax.rem(place_ref[2] + hop, chan_count)
        start = pl.multiple_of(target * rows, rows)
        sent_ref[:rows] = mixer_scratch[pl.ds(start, rows)].astype(BF16)
        sent_ref[rows:] = back


def add_late(ending, extra, taps, valid):
    index = lax.broadcasted_iota(jnp.int32, ending.shape, 0)
    late = jnp.where((index >= PAD - taps) & valid, extra, 0.0)
    return ending + late


def project_back(
    taps,
    seq_count,
    place_ref,
    pair_ref,
    next_ref,
    mixer_ref,
    step_ref,
    inner_weight_ref,
    mixer_weight_ref,
    step_weight_ref,
    out_ref,
    inner_scratch,
    mixer_scratch,
):
    count, rows, _ = out_ref.shape
    length, mixed = mixer_ref.shape
    width = pair_ref.shape[1]
    valid = place_ref[0] < seq_count - 1
    extra = next_ref[length:].astype(F32)
    head = length - PAD
    inner_scratch[:head] = pair_ref[:head]
    ending = add_late(pair_ref[head:length].astype(F32), extra, taps, valid)
    inner_scratch[head:] = ending.astype(BF16)
    shifted = jnp.concatenate([extra[PAD - taps :, :mixed], extra[: PAD - taps, :mixed]], axis=0)
    mixer_scratch[:head] = mixer_ref[:head]
    ending = add_late(mixer_ref[head:].astype(F32), shifted, taps, valid)
    mixer_scratch[head:] = ending.astype(BF16)
    whole = width // (2 * LANES) * (2 * LANES)
    share = dot(inner_scratch[:, :whole], inner_weight_ref[:, :whole], 1, 1)
    left = jnp.concatenate([inner_scratch[:, whole:], step_ref[...]], axis=1)
    right = jnp.concatenate([inner_weight_ref[:, whole:], step_weight_ref[...]], axis=1)
    share = share + dot(left, right, 1, 1)
    share = share + dot(mixer_scratch[...], mixer_weight_ref[...], 1, 1)
    share = share.astype(BF16)
    for target in range(count):
        span = slice(target * rows, (target + 1) * rows)
        out_ref[target] = share[span]


def turn(relative, place_ref, *refs):
    column_refs, out_ref, columns = refs[:-2], refs[-2], refs[-1]
    seq_place = place_ref[0]
    chan_place = place_ref[2]
    chan_count = len(column_refs)
    seq_count, rows, _ = column_refs[0].shape
    length = chan_count * rows
    for hop in range(seq_count):
        source = lax.rem(seq_place - hop + seq_count, seq_count) if relative else hop
        for chan_hop in range(chan_count):
            chan_source = lax.rem(chan_place - chan_hop + chan_count, chan_count)
            start = pl.multiple_of(hop * length + chan_source * rows, rows)
            columns[pl.ds(start, rows)] = column_refs[chan_hop][source]
    out_ref[...] = columns[...].T


def arrange(relative, taps, place_ref, pair_refs, grads, steps):
    seq_place = place_ref[0]
    seq_count = len(pair_refs) if relative else pair_refs[0].shape[0]
    length = grads.shape[0] // seq_count

    def message(hop):
        return pair_refs[hop][...] if relative else pair_refs[0][hop]

    for hop in range(seq_count):
        if relative:
            shard = lax.rem(seq_place - hop + seq_count, seq_count)
            after = (hop - 1) % seq_count
        else:
            shard = hop
            after = (hop + 1) % seq_count
        pair = message(hop)
        start = hop * length
        head = length - PAD
        grads[start : start + head] = pair[:head]
        extra = message(after)[length:].astype(F32)
        ending = add_late(pair[head:length].astype(F32), extra, taps, shard < seq_count - 1)
        grads[start + head : start + length] = ending.astype(BF16)
        packed = pair[length:].astype(F32)
        groups = packed.shape[1] // length
        lines = [packed[:, group * length : (group + 1) * length] for group in range(groups)]
        steps[:, start : start + length] = jnp.concatenate(lines, axis=0).astype(BF16)


def leave(relative, taps, rows, scale, place_ref, *refs):
    turned_ref = refs[0]
    out_ref, grads, steps = refs[-3:]
    arrange(relative, taps, place_ref, refs[1:-3], grads, steps)
    padded = turned_ref.shape[0] // 2
    chosen = turned_ref[padded : padded + rows]
    out_ref[:rows] = (dot(chosen, grads[...]) * scale).astype(BF16)
    lines = steps.shape[0]
    term = dot(steps[...], turned_ref[padded:], 1, 1) * scale
    out_ref[rows:, :padded] = term.astype(BF16)
    out_ref[rows:, padded:] = jnp.zeros((lines, out_ref.shape[1] - padded), BF16)


def keep(rows, scale, turned_ref, grads_ref, steps_ref, out_ref, step_ref):
    padded = turned_ref.shape[0] // 2
    out_ref[...] = dot(turned_ref[:rows], grads_ref[...]) * scale
    step_ref[...] = dot(steps_ref[...], turned_ref[:padded], 1, 1) * scale


def mix(relative, taps, rows, scale, place_ref, *refs):
    column_ref, out_ref, columns, grads = refs[0], refs[-3], refs[-2], refs[-1]
    grad_refs = refs[1:-3]
    seq_place = place_ref[0]
    dp_place = place_ref[1]
    chan_place = place_ref[2]
    seq_count, tokens, wide = column_ref.shape
    chan_count = out_ref.shape[0] // 2

    def message(hop):
        return grad_refs[hop][...] if relative else grad_refs[0][hop]

    for hop in range(seq_count):
        if relative:
            source = lax.rem(seq_place - hop + seq_count, seq_count)
            after = (hop - 1) % seq_count
        else:
            source = hop
            after = (hop + 1) % seq_count
        start = hop * tokens
        head = tokens - PAD
        columns[start : start + tokens] = column_ref[source]
        block = message(hop)
        grads[start : start + head] = block[:head]
        valid = (source < seq_count - 1) & (chan_place == chan_count - 1)
        extra = message(after)[tokens:].astype(F32)
        ending = add_late(block[head:tokens].astype(F32), extra, taps, valid)
        grads[start + head : start + tokens] = ending.astype(BF16)
    padded = wide // 2
    term = (dot(columns[...], grads[...], 0, 0) * scale).astype(BF16)
    for hop in range(2):
        target = lax.rem(dp_place + hop, 2)
        for chan in range(chan_count):
            start = hop * padded + chan * rows
            out_ref[target * chan_count + chan] = term[start : start + rows]


def shape(*dims, dtype=F32):
    return pltpu.VMEM(dims, dtype)


def ring(axis, hop):
    count = lax.axis_size(axis)
    return [(source, (source + hop) % count) for source in range(count)]


def call(body, place, arrays, out_shape, scratch=(), cost=3, plain=()):
    vmem = pltpu.MemorySpace.VMEM
    hbm = pltpu.MemorySpace.HBM
    arrays = [
        pltpu.with_memory_space_constraint(array, hbm if number in plain else vmem)
        for number, array in enumerate(arrays)
    ]
    in_specs = [pl.BlockSpec(memory_space=pltpu.VMEM)] * len(arrays)
    if place is not None:
        in_specs = [pl.BlockSpec(memory_space=pltpu.SMEM)] + in_specs
        arrays = [place] + arrays
    return pl.pallas_call(
        body,
        out_shape=out_shape,
        in_specs=in_specs,
        out_specs=[pl.BlockSpec(memory_space=pltpu.VMEM)] * len(out_shape),
        scratch_shapes=list(scratch),
        cost_estimate=pl.CostEstimate(flops=cost * 10**8, bytes_accessed=0, transcendentals=0),
        compiler_params=pltpu.CompilerParams(vmem_limit_bytes=24 * 2**20),
    )(*arrays)


def around(block, axis):
    count = lax.axis_size(axis)
    return [block] + [
        lax.ppermute(block, axis, ring(axis, hop)) for hop in reversed(range(1, count))
    ][::-1]


def body(
    layer_input,
    inner_weight,
    mixer_weight,
    step_weight,
    conv_inner,
    conv_mixer,
    step_bias,
    decay_log,
    skip_gain,
    output_grad,
):
    own = layer_input[0]
    dp_count = lax.axis_size("dp")
    seq_count = lax.axis_size("seq")
    chan_count = lax.axis_size("chan")
    place = lax.axis_index("seq")
    relative = seq_count <= DIRECT
    rows, model = own.shape
    length = rows * chan_count
    width = inner_weight.shape[1]
    head_count = step_bias.shape[0]
    head_dim = width // head_count
    mixed = mixer_weight.shape[1]
    state = mixed // 2
    upstream = output_grad[0]
    grad_rows = model // (dp_count * seq_count)
    padded = -(-grad_rows // LANES) * LANES
    taps = conv_inner.shape[0] - 1
    places = [place, lax.axis_index("dp"), lax.axis_index("chan")]
    places = jnp.stack(places).astype(jnp.int32)
    norm_factor = 1.0 / math.sqrt(length * seq_count * dp_count)

    gathered = around(own, "chan")
    sorted_columns, head_rows, step_near, step_far = call(
        functools.partial(blocks, grad_rows, padded, dp_count),
        places,
        [own, step_weight.T, step_bias[None], decay_log[None], skip_gain[None]],
        [
            shape(seq_count, rows, dp_count * padded, dtype=BF16),
            shape(PAD, LANES),
            shape(model, LANES, dtype=BF16),
            jax.ShapeDtypeStruct((model, LANES), BF16),
        ],
        [pltpu.VMEM((LANES, model), F32)],
        cost=2,
    )
    columns = lax.all_to_all(sorted_columns, "seq", split_axis=0, concat_axis=0)
    inner_proj, mixer_proj, step_raw, tail = call(
        functools.partial(project, chan_count),
        places,
        gathered + [inner_weight, mixer_weight, step_near],
        [
            shape(length, width, dtype=BF16),
            shape(length, mixed, dtype=BF16),
            shape(length, LANES),
            shape(2 * PAD, width + mixed, dtype=BF16),
        ],
        [pltpu.VMEM((length, model), BF16)],
        cost=4,
    )
    forward_pairs = [(source, source + 1) for source in range(seq_count - 1)]
    history = lax.ppermute(tail, "seq", forward_pairs)

    if relative:
        message_shapes = [shape(state + PAD, width, dtype=BF16)] * (seq_count - 1)
    else:
        message_shapes = [shape(seq_count, state + PAD, width, dtype=BF16)]
    inner_pre, mixer_pre, step, decay, *messages = call(
        functools.partial(prepare, head_dim, relative),
        places,
        [inner_proj, mixer_proj, history, step_raw, head_rows, upstream, conv_inner, conv_mixer],
        [
            shape(length, width),
            shape(length, mixed),
            shape(length, LANES),
            shape(length, LANES),
        ]
        + message_shapes,
        [pltpu.VMEM((PAD + length, width), F32), pltpu.VMEM((PAD + length, mixed), F32)],
    )
    if relative:
        received = [
            lax.ppermute(message, "seq", ring("seq", hop))
            for hop, message in enumerate(messages, 1)
        ]
    else:
        received = [lax.all_to_all(messages[0], "seq", split_axis=0, concat_axis=0)]
    inner_part, mixer_part, row_part, column_part = call(
        functools.partial(within, head_dim),
        None,
        [inner_pre, mixer_pre, step, decay, head_rows, upstream],
        [shape(length, width), shape(length, mixed), shape(length, LANES), shape(LANES, length)],
    )
    all_columns = around(columns, "chan")
    (turned,) = call(
        functools.partial(turn, relative),
        places,
        all_columns,
        [shape(dp_count * padded, seq_count * length, dtype=BF16)],
        [pltpu.VMEM((seq_count * length, dp_count * padded), BF16)],
    )

    pair, mixer_local, step_grad, *mixer_sent = call(
        functools.partial(finish, head_dim, relative, seq_count, chan_count),
        places,
        received
        + [
            inner_pre,
            mixer_pre,
            step,
            decay,
            step_raw,
            head_rows,
            upstream,
            conv_inner,
            conv_mixer,
            inner_part,
            mixer_part,
            row_part,
            column_part,
        ],
        [
            shape(length + PAD, width, dtype=BF16),
            shape(length, mixed, dtype=BF16),
            shape(length, LANES, dtype=BF16),
        ]
        + [shape(rows + PAD, mixed, dtype=BF16)] * chan_count,
        [pltpu.VMEM((length + 2 * PAD, width), F32), pltpu.VMEM((length + 2 * PAD, mixed), F32)],
        cost=5,
    )

    def over_seq(block):
        if relative:
            return around(block, "seq")
        return [lax.all_gather(block, "seq")]

    pairs = over_seq(pair)
    if relative:
        following = pairs[-1]
    else:
        following = lax.rem(place + 1, seq_count)
        following = lax.dynamic_index_in_dim(pairs[0], following, 0, False)

    mixer_rows = mixer_sent[:1] + [
        lax.ppermute(block, "chan", ring("chan", hop))
        for hop, block in enumerate(mixer_sent[1:], 1)
    ]
    (mixer_rows,) = call(add_up, None, mixer_rows, [shape(rows + PAD, mixed, dtype=BF16)], cost=1)
    mixers = over_seq(mixer_rows)

    (sent,) = call(
        functools.partial(project_back, taps, seq_count),
        places,
        [pair, following, mixer_local, step_grad, inner_weight, mixer_weight, step_far],
        [shape(chan_count, rows, model, dtype=BF16)],
        [pltpu.VMEM((length, width), BF16), pltpu.VMEM((length, mixed), BF16)],
        cost=4,
        plain=(4, 5, 6),
    )
    taken = lax.all_to_all(sent, "chan", split_axis=0, concat_axis=0)

    groups = width // length
    step_lines = PAD * groups
    leaving, grads, steps = call(
        functools.partial(leave, relative, taps, grad_rows, norm_factor),
        places,
        [turned] + pairs,
        [
            shape(grad_rows + step_lines, width, dtype=BF16),
            shape(seq_count * length, width, dtype=BF16),
            shape(step_lines, seq_count * length, dtype=BF16),
        ],
    )
    arrived = lax.ppermute(leaving, "dp", ring("dp", 1))
    kept, kept_step = call(
        functools.partial(keep, grad_rows, norm_factor),
        None,
        [turned, grads, steps],
        [shape(grad_rows, width), shape(step_lines, padded)],
    )
    (mixer_blocks,) = call(
        functools.partial(mix, relative, taps, grad_rows // chan_count, norm_factor),
        places,
        [columns] + mixers,
        [shape(dp_count * chan_count, grad_rows // chan_count, mixed, dtype=BF16)],
        [
            pltpu.VMEM((seq_count * rows, dp_count * padded), BF16),
            pltpu.VMEM((seq_count * rows, mixed), BF16),
        ],
        cost=2,
    )
    taken, mixer_blocks = lax.optimization_barrier((taken, mixer_blocks))
    mixer_blocks = lax.all_to_all(
        mixer_blocks, ("dp", "chan"), split_axis=0, concat_axis=0
    )
    mixer_weight_grad = jnp.sum(mixer_blocks.astype(F32), axis=0)
    input_grad = jnp.sum(taken.astype(F32), axis=0).astype(BF16)
    inner_weight_grad = kept + arrived[:grad_rows].astype(F32)
    kept_step = kept_step[:, :grad_rows] + arrived[grad_rows:, :grad_rows].astype(F32)
    lines = [kept_step[(head % groups) * PAD + head // groups] for head in range(head_count)]
    step_weight_grad = jnp.stack(lines, axis=1)
    return (input_grad[None], inner_weight_grad, mixer_weight_grad, step_weight_grad)


def solution(mesh):
    in_specs = (
        P("dp", ("seq", "chan"), None),
        P(None, "chan"),
        P(),
        P(None, "chan"),
        P(None, "chan"),
        P(),
        P("chan"),
        P("chan"),
        P("chan"),
        P("dp", "seq", "chan"),
    )
    out_specs = (
        P("dp", ("seq", "chan"), None),
        P(("dp", "seq"), "chan"),
        P(("dp", "seq", "chan"), None),
        P(("dp", "seq"), "chan"),
    )
    return jax.shard_map(body, mesh=mesh, in_specs=in_specs, out_specs=out_specs, check_vma=False)
```

time: 440 us -> 111 us (0.25)
  waiting for transfers between devices: 281 us -> 34.6 us
  blocking collectives: 61.7 us -> 0 us
  matrix products: 29.3 us -> 0 us
  starting transfers between devices: 20.2 us -> 42.1 us
  Pallas kernels: 0 us -> 18.9 us
  between operations: 16 us -> 0.78 us
  local copies, waits for them, and re-layouts: 20.6 us -> 10 us
  other arithmetic: 10 us -> 4.25 us
    unnamed x8 -> x0, waiting for transfers between devices: 237 us -> none
    all_gather x5 -> x0, blocking collectives: 54.3 us -> none  [the longest x2 25.9 us: prefix(): lax.all_gather(a.astype(kind), axis)]
    dot_general x22 -> x0, matrix products: 29.3 us -> none  [the longest x4 10.6 us: project_back(): lax.dot_general(gradient, weight, (((1,), (1,)), ((), ())), preferred_ele...]
    all_gather x2 -> x0, waiting for transfers between devices: 25.4 us -> none  [the longest x1 19.5 us: body(): lax.all_gather(inner_weight, 'chan', axis=1, tiled=True)]
    ppermute x4 -> x20, waiting for transfers between devices: 8.31 us -> 31 us  [the longest x12 16.5 us: around(): lax.ppermute(block, axis, ring(axis, hop))]
    ppermute x4 -> x20, starting transfers between devices: 9.96 us -> 30.2 us  [the longest x12 15 us: around(): lax.ppermute(block, axis, ring(axis, hop))]
    pallas_call x0 -> x11, Pallas kernels: none -> 18.9 us  [call(): pl.pallas_call(body, out_shape=out_shape, in_specs=in_specs, out_specs=[p...]
    unnamed x91 -> x24, local copies, waits for them, and re-layouts: 18.1 us -> 8.77 us
  transfers between devices with their start and end apart: 12 -> 23, of which waited for: 8 -> 11; matrix products, arithmetic and copies ran while one was open for 10% -> 4% of each run, Pallas kernels for 0% -> 16%
where the time goes in v1:
time: 111 us
  starting transfers between devices  42.1 us (38%)
  waiting for transfers between devices  34.6 us (31%)
  Pallas kernels  18.9 us (17%)
  local copies, waits for them, and re-layouts  10 us (9%)
  other arithmetic  4.25 us (4%)
    pallas_call x11, Pallas kernels, call(): pl.pallas_call(body, out_shape=out_shape, in_specs=in_specs, out_specs=[p...  18.9 us
    ppermute x12, waiting for transfers between devices, around(): lax.ppermute(block, axis, ring(axis, hop))  16.5 us
    ppermute x12, starting transfers between devices, around(): lax.ppermute(block, axis, ring(axis, hop))  15 us
    unnamed x24, local copies, waits for them, and re-layouts  8.77 us
    ppermute x3, waiting for transfers between devices, body(): lax.ppermute(block, 'chan', ring('chan', hop))  7.39 us
    ppermute x3, starting transfers between devices, body(): lax.ppermute(message, 'seq', ring('seq', hop))  6.2 us
    ppermute x3, waiting for transfers between devices, body(): lax.ppermute(message, 'seq', ring('seq', hop))  5.58 us
    all_to_all x1, starting transfers between devices, body(): columns = lax.all_to_all(sorted_columns, 'seq', split_axis=0, concat_axis=0)  5 us
  transfers between devices with their start and end apart: 23, of which 11 were waited for; matrix products, arithmetic and copies ran while one was open for 4% of the time, Pallas kernels for 16%

profile of v1, /device:TPU:0, one launch (start us, length us, event | category | flops | bytes accessed | tf_op | source)
XLA Modules:
  0.0 110.6 jit_solution(9331048122013574794)
XLA Ops:
  1.2 2.6 %collective-permute-start.1 = (bf16[32,2560]{1,0:T(8,128)(2,1)}, bf16[32,2560]{1,0:T(8,128)(2,1)S(1)}, u32[]{:S(2)}, u32[]{:S(2)}) collective-permute-start(bf16[32,2560]{1,0:T(8,128)(2,1)} %bitcast.31), channel_id=1, source_target_pairs={{0,2},{1,3},{2,0},{3,1},{4,6},{5,7},{6,4},{7,5},{8,10},{9,11},{10,... | collective-permute-start | bytes 491528 | tf_op jit(solution)/shard_map/ppermute | solution.py:621
  3.7 1.4 %collective-permute-start.2 = (bf16[32,2560]{1,0:T(8,128)(2,1)}, bf16[32,2560]{1,0:T(8,128)(2,1)S(1)}, u32[]{:S(2)}, u32[]{:S(2)}) collective-permute-start(bf16[32,2560]{1,0:T(8,128)(2,1)} %bitcast.32), channel_id=1, source_target_pairs={{0,3},{1,0},{2,1},{3,2},{4,7},{5,4},{6,5},{7,6},{8,11},{9,8},{10,9... | collective-permute-start | bytes 491528 | tf_op jit(solution)/shard_map/ppermute | solution.py:621
  5.2 0.9 copy-done.3
  6.1 0.9 copy-done.8
  7.0 0.7 copy-done.9
  7.7 0.7 copy-done.10
  9.0 1.5 %shard_map.129 = (bf16[4,32,768]{2,1,0:T(8,128)(2,1)}, f32[8,128]{1,0:T(8,128)S(1)}, bf16[2560,128]{1,0:T(8,128)(2,1)S(1)}, bf16[2560,128]{1,0:T(8,128)(2,1)S(1)}) custom-call(s32[3]{0:T(128)S(1)} %pad_add_fusion.place_ref, bf16[32,2560]{1,0:T(8,128)(2,1)S(1)} %bitcast.33, bf16[10,2560]{1,0:T(8,128)(2,1)S(1)} %bitcast.38, f32[1,10]{1,0:T(1,128)S(1)} %bitcast.39, ...), custom_call_target="tpu_custom_call" | custom-call | flops 200000000 | tf_op jit(solution)/shard_map/pallas_call | solution.py:607
  10.5 0.8 copy-done.2
  11.3 5.0 %all-to-all-start.1 = ((bf16[4,32,768]{2,1,0:T(8,128)(2,1)}), bf16[4,32,768]{2,1,0:T(8,128)(2,1)S(1)}, u32[]{:S(2)}, u32[]{:S(2)}) async-start(bf16[4,32,768]{2,1,0:T(8,128)(2,1)} %get-tuple-element.58), calls=%async_computation.1 | async-start | bytes 393216 | tf_op jit(solution)/shard_map/all_to_all | solution.py:672
  16.3 1.9 %copy-done = bf16[2560,640]{1,0:T(8,128)(2,1)S(1)} copy-done((bf16[2560,640]{1,0:T(8,128)(2,1)S(1)}, bf16[2560,640]{1,0:T(8,128)(2,1)}, u32[]{:S(2)}) %copy-start) | copy-done | bytes 3276824
  18.3 1.3 %copy-done.1 = bf16[2560,256]{1,0:T(8,128)(2,1)S(1)} copy-done((bf16[2560,256]{1,0:T(8,128)(2,1)S(1)}, bf16[2560,256]{1,0:T(8,128)(2,1)}, u32[]{:S(2)}) %copy-start.1) | copy-done | bytes 1310744
  19.6 0.9 copy-done.4
  20.5 1.4 %shard_map.130 = (bf16[128,640]{1,0:T(8,128)(2,1)S(1)}, bf16[128,256]{1,0:T(8,128)(2,1)S(1)}, f32[128,128]{1,0:T(8,128)S(1)}, bf16[16,896]{1,0:T(8,128)(2,1)S(1)}) custom-call(s32[3]{0:T(128)S(1)} %pad_add_fusion.place_ref, bf16[32,2560]{1,0:T(8,128)(2,1)S(1)} %bitcast.34, bf16[32,2560]{1,0:T(8,128)(2,1)S(1)} %collective-permute-done.refs_1_, ...), custom_call_target="tpu_custom_call" | custom-call | flops 400000000 | tf_op jit(solution)/shard_map/pallas_call | solution.py:607
  22.0 3.9 %collective-permute-start.3 = (bf16[16,896]{1,0:T(8,128)(2,1)S(1)}, bf16[16,896]{1,0:T(8,128)(2,1)S(1)}, u32[]{:S(2)}, u32[]{:S(2)}) collective-permute-start(bf16[16,896]{1,0:T(8,128)(2,1)S(1)} %get-tuple-element.40), channel_id=1, source_target_pairs={{0,4},{4,8},{8,12},{1,5},{5,9},{9,13},{2,6},{6,10},{10,14},{3,7},{... | collective-permute-start | bytes 86024 | tf_op jit(solution)/shard_map/ppermute | solution.py:687
  25.9 1.5 %collective-permute-done.3.refs_2_ = bf16[16,896]{1,0:T(8,128)(2,1)S(1)} collective-permute-done((bf16[16,896]{1,0:T(8,128)(2,1)S(1)}, bf16[16,896]{1,0:T(8,128)(2,1)S(1)}, u32[]{:S(2)}, u32[]{:S(2)}) %collective-permute-start.3) | collective-permute-done | bytes 28704 | tf_op jit(solution)/shard_map/ppermute | solution.py:687
  27.4 2.1 %shard_map.131 = (f32[128,640]{1,0:T(8,128)S(1)}, f32[128,256]{1,0:T(8,128)S(1)}, f32[128,128]{1,0:T(8,128)S(1)}, f32[128,128]{1,0:T(8,128)S(1)}, bf16[136,640]{...) custom-call(s32[3]{0:T(128)S(1)} %pad_add_fusion.place_ref, ...), custom_call_target="tpu_custom_call" | custom-call | flops 300000000 | tf_op jit(solution)/shard_map/pallas_call | solution.py:607
  29.5 2.4 %collective-permute-start.4 = (bf16[136,640]{1,0:T(8,128)(2,1)S(1)}, bf16[136,640]{1,0:T(8,128)(2,1)S(1)}, u32[]{:S(2)}, u32[]{:S(2)}) collective-permute-start(bf16[136,640]{1,0:T(8,128)(2,1)S(1)} %get-tuple-element.43), channel_id=1, source_target_pairs={{0,4},{4,8},{8,12},{12,0},{1,5},{5,9},{9,13},{13,1},{2,6},{6,10},{... | collective-permute-start | bytes 522248 | tf_op jit(solution)/shard_map/ppermute | solution.py:708
  31.9 2.4 %collective-permute-start.5 = (bf16[136,640]{1,0:T(8,128)(2,1)S(1)}, bf16[136,640]{1,0:T(8,128)(2,1)S(1)}, u32[]{:S(2)}, u32[]{:S(2)}) collective-permute-start(bf16[136,640]{1,0:T(8,128)(2,1)S(1)} %get-tuple-element.44), channel_id=1, source_target_pairs={{0,8},{4,12},{8,0},{12,4},{1,9},{5,13},{9,1},{13,5},{2,10},{6,14},... | collective-permute-start | bytes 522248 | tf_op jit(solution)/shard_map/ppermute | solution.py:708
  34.2 1.5 %collective-permute-start.6 = (bf16[136,640]{1,0:T(8,128)(2,1)S(1)}, bf16[136,640]{1,0:T(8,128)(2,1)S(1)}, u32[]{:S(2)}, u32[]{:S(2)}) collective-permute-start(bf16[136,640]{1,0:T(8,128)(2,1)S(1)} %get-tuple-element.45), channel_id=1, source_target_pairs={{0,12},{4,0},{8,4},{12,8},{1,13},{5,1},{9,5},{13,9},{2,14},{6,2},{... | collective-permute-start | bytes 522248 | tf_op jit(solution)/shard_map/ppermute | solution.py:708
  36.2 2.8 %collective-permute-done.4.refs_0_ = bf16[136,640]{1,0:T(8,128)(2,1)S(1)} collective-permute-done((bf16[136,640]{1,0:T(8,128)(2,1)S(1)}, bf16[136,640]{1,0:T(8,128)(2,1)S(1)}, u32[]{:S(2)}, u32[]{:S(2)}) %collective-permute-start.4) | collective-permute-done | bytes 174112 | tf_op jit(solution)/shard_map/ppermute | solution.py:708
  39.0 1.4 %shard_map.132 = (f32[128,640]{1,0:T(8,128)S(1)}, f32[128,256]{1,0:T(8,128)S(1)}, f32[128,128]{1,0:T(8,128)S(1)}, f32[128,128]{1,0:T(8,128)S(1)}) custom-call(f32[128,640]{1,0:T(8,128)S(1)} %get-tuple-element.46.inner_pre_ref.refs_3_, f32[128,256]{1,0:T(8,128)S(1)} %get-tuple-element.47.mixer_pre_ref.refs_4_, ...), custom_call_target="tpu_custom_call" | custom-call | flops 300000000 | tf_op jit(solution)/shard_map/pallas_call | solution.py:607
  40.4 2.8 %collective-permute-done.5.refs_1_ = bf16[136,640]{1,0:T(8,128)(2,1)S(1)} collective-permute-done((bf16[136,640]{1,0:T(8,128)(2,1)S(1)}, bf16[136,640]{1,0:T(8,128)(2,1)S(1)}, u32[]{:S(2)}, u32[]{:S(2)}) %collective-permute-start.5) | collective-permute-done | bytes 174112 | tf_op jit(solution)/shard_map/ppermute | solution.py:708
  43.2 3.3 %shard_map.133 = (bf16[136,640]{1,0:T(8,128)(2,1)S(1)}, bf16[128,256]{1,0:T(8,128)(2,1)S(1)}, bf16[128,128]{1,0:T(8,128)(2,1)S(1)}, bf16[40,256]{1,0:T(8,128)(2,...) custom-call(s32[3]{0:T(128)S(1)} %pad_add_fusion.place_ref, ...), custom_call_target="tpu_custom_call" | custom-call | flops 500000000 | tf_op jit(solution)/shard_map/pallas_call | solution.py:607
  46.6 5.4 %collective-permute-start.7 = (bf16[136,640]{1,0:T(8,128)(2,1)S(1)}, bf16[136,640]{1,0:T(8,128)(2,1)S(1)}, u32[]{:S(2)}, u32[]{:S(2)}) collective-permute-start(bf16[136,640]{1,0:T(8,128)(2,1)S(1)} %get-tuple-element.54.pair_ref.refs_1_), channel_id=1, source_target_pairs={{0,12},{4,0},{8,4},{12,8},{1,13},{5,1},{9,5},{13,9},{2,14},{6,2},{... | collective-permute-start | bytes 522248 | tf_op jit(solution)/shard_map/ppermute | solution.py:621
  52.0 0.7 collective-permute-start.18
  52.7 0.9 shard_map.137.refs_0_.turned_ref
  53.6 3.3 %collective-permute-done.7.next_ref.refs_4_ = bf16[136,640]{1,0:T(8,128)(2,1)S(1)} collective-permute-done((bf16[136,640]{1,0:T(8,128)(2,1)S(1)}, bf16[136,640]{1,0:T(8,128)(2,1)S(1)}, u32[]{:S(2)}, u32[]{:S(2)}) %collective-permute-start.7) | collective-permute-done | bytes 174112 | tf_op jit(solution)/shard_map/ppermute | solution.py:621
  56.9 4.4 %collective-permute-done.17.refs_2_ = bf16[136,640]{1,0:T(8,128)(2,1)S(1)} collective-permute-done((bf16[136,640]{1,0:T(8,128)(2,1)S(1)}, bf16[136,640]{1,0:T(8,128)(2,1)S(1)}, u32[]{:S(2)}, u32[]{:S(2)}) %collective-permute-start.17) | collective-permute-done | bytes 174112 | tf_op jit(solution)/shard_map/ppermute | solution.py:621
  61.2 6.6 %collective-permute-done.18.refs_3_ = bf16[136,640]{1,0:T(8,128)(2,1)S(1)} collective-permute-done((bf16[136,640]{1,0:T(8,128)(2,1)S(1)}, bf16[136,640]{1,0:T(8,128)(2,1)S(1)}, u32[]{:S(2)}, u32[]{:S(2)}) %collective-permute-start.18) | collective-permute-done | bytes 174112 | tf_op jit(solution)/shard_map/ppermute | solution.py:621
  67.8 1.1 shard_map.138
  68.9 1.6 %collective-permute-start.19 = (bf16[360,640]{1,0:T(8,128)(2,1)S(1)}, bf16[360,640]{1,0:T(8,128)(2,1)}, u32[]{:S(2)}, u32[]{:S(2)}) collective-permute-start(bf16[360,640]{1,0:T(8,128)(2,1)S(1)} %get-tuple-element.67), channel_id=1, source_target_pairs={{0,16},{16,0},{1,17},{17,1},{2,18},{18,2},{3,19},{19,3},{4,20},{20... | collective-permute-start | bytes 1382408 | tf_op jit(solution)/shard_map/ppermute | solution.py:799
  70.4 5.1 %shard_map.134 = bf16[4,32,2560]{2,1,0:T(8,128)(2,1)} custom-call(s32[3]{0:T(128)S(1)} %pad_add_fusion.place_ref, bf16[136,640]{1,0:T(8,128)(2,1)S(1)} %get-tuple-element.54.pair_ref.refs_1_, bf16[136,640]{1,0:T(8,128)(2,1)S(1)} %collective-permute-done.7.next_ref.refs_4_, bf16[128,256]{1,0:T(8,128)(2,1)S(1)} %get-tuple-element.55.mixer_ref, ...), custom_call_target="tpu_custom_call" | custom-call | flops 400000000 | tf_op jit(solution)/shard_map/pallas_call | solution.py:607
  75.6 3.5 %all-to-all-start = ((bf16[4,32,2560]{2,1,0:T(8,128)(2,1)}), bf16[4,32,2560]{2,1,0:T(8,128)(2,1)S(1)}, u32[]{:S(2)}, u32[]{:S(2)}) async-start(bf16[4,32,2560]{2,1,0:T(8,128)(2,1)} %shard_map.134), calls=%async_computation | async-start | bytes 1310720 | tf_op jit(solution)/shard_map/all_to_all | solution.py:785
  79.5 1.6 %collective-permute-start.9 = (bf16[40,256]{1,0:T(8,128)(2,1)S(1)}, bf16[40,256]{1,0:T(8,128)(2,1)S(1)}, u32[]{:S(2)}, u32[]{:S(2)}) collective-permute-start(bf16[40,256]{1,0:T(8,128)(2,1)S(1)} %get-tuple-element.61), channel_id=1, source_target_pairs={{0,2},{1,3},{2,0},{3,1},{4,6},{5,7},{6,4},{7,5},{8,10},{9,11},{10,... | collective-permute-start | bytes 61448 | tf_op jit(solution)/shard_map/ppermute | solution.py:770
  81.2 1.3 %collective-permute-start.10 = (bf16[40,256]{1,0:T(8,128)(2,1)S(1)}, bf16[40,256]{1,0:T(8,128)(2,1)S(1)}, u32[]{:S(2)}, u32[]{:S(2)}) collective-permute-start(bf16[40,256]{1,0:T(8,128)(2,1)S(1)} %get-tuple-element.62), channel_id=1, source_target_pairs={{0,3},{1,0},{2,1},{3,2},{4,7},{5,4},{6,5},{7,6},{8,11},{9,8},{10,9... | collective-permute-start | bytes 61448 | tf_op jit(solution)/shard_map/ppermute | solution.py:770
  82.5 6.6 %collective-permute-done.8.refs_1_ = bf16[40,256]{1,0:T(8,128)(2,1)S(1)} collective-permute-done((bf16[40,256]{1,0:T(8,128)(2,1)S(1)}, bf16[40,256]{1,0:T(8,128)(2,1)S(1)}, u32[]{:S(2)}, u32[]{:S(2)}) %collective-permute-start.8) | collective-permute-done | bytes 20512 | tf_op jit(solution)/shard_map/ppermute | solution.py:770
  89.1 0.8 collective-permute-done.9.refs_2_
  90.0 1.7 %collective-permute-start.12 = (bf16[40,256]{1,0:T(8,128)(2,1)S(1)}, bf16[40,256]{1,0:T(8,128)(2,1)S(1)}, u32[]{:S(2)}, u32[]{:S(2)}) collective-permute-start(bf16[40,256]{1,0:T(8,128)(2,1)S(1)} %shard_map.135.refs_1_), channel_id=1, source_target_pairs={{0,8},{4,12},{8,0},{12,4},{1,9},{5,13},{9,1},{13,5},{2,10},{6,14},... | collective-permute-start | bytes 61448 | tf_op jit(solution)/shard_map/ppermute | solution.py:621
  91.7 2.1 %collective-permute-start.13 = (bf16[40,256]{1,0:T(8,128)(2,1)S(1)}, bf16[40,256]{1,0:T(8,128)(2,1)S(1)}, u32[]{:S(2)}, u32[]{:S(2)}) collective-permute-start(bf16[40,256]{1,0:T(8,128)(2,1)S(1)} %shard_map.135.refs_1_), channel_id=1, source_target_pairs={{0,12},{4,0},{8,4},{12,8},{1,13},{5,1},{9,5},{13,9},{2,14},{6,2},{... | collective-permute-start | bytes 61448 | tf_op jit(solution)/shard_map/ppermute | solution.py:621
  93.8 1.8 %collective-permute-done.11.refs_2_ = bf16[40,256]{1,0:T(8,128)(2,1)S(1)} collective-permute-done((bf16[40,256]{1,0:T(8,128)(2,1)S(1)}, bf16[40,256]{1,0:T(8,128)(2,1)S(1)}, u32[]{:S(2)}, u32[]{:S(2)}) %collective-permute-start.11) | collective-permute-done | bytes 20512 | tf_op jit(solution)/shard_map/ppermute | solution.py:621
  96.1 1.5 %shard_map.136 = bf16[8,80,256]{2,1,0:T(8,128)(2,1)} custom-call(s32[3]{0:T(128)S(1)} %pad_add_fusion.place_ref, bf16[4,32,768]{2,1,0:T(8,128)(2,1)S(1)} %all-to-all-done.1.refs_0_, bf16[40,256]{1,0:T(8,128)(2,1)S(1)} %shard_map.135.refs_1_, bf16[40,256]{1,0:T(8,128)(2,1)S(1)} %collective-permute-done.11.refs_2_, ...), custom_call_target="tpu_custom_call" | custom-call | flops 200000000 | tf_op jit(solution)/shard_map/pallas_call | solution.py:607
  98.2 0.8 convert_add_fusion.1
  99.0 3.4 %all-to-all-start.2 = ((bf16[8,80,256]{2,1,0:T(8,128)(2,1)}), bf16[8,80,256]{2,1,0:T(8,128)(2,1)S(1)}, u32[]{:S(2)}, u32[]{:S(2)}) async-start(bf16[8,80,256]{2,1,0:T(8,128)(2,1)} %shard_map.136), calls=%async_computation.2 | async-start | bytes 655360 | tf_op jit(solution)/shard_map/all_to_all | solution.py:818
  102.4 1.2 %stack.19 = f32[320,10]{0,1:T(8,128)} concatenate(f32[320,1]{0,1:T(1,128)S(1)} %get-tuple-element.79, f32[320,1]{0,1:T(1,128)S(1)} %get-tuple-element.78, f32[320,1]{0,1:T(1,128)S(1)} %get-tuple-element.77, f32[320,1]{0,1:T(1,128)S(1)} %get-tuple-element.76, f32[320,1]{0,1:T(1,128)S(1)} %get-tuple-element.75, f32[320,1]{0,1:T(1,128)S(1)} %get-tuple-element.74, ...), dimensions={1} | concatenate | bytes 25600 | tf_op jit(solution)/shard_map/stack | solution.py:826
  103.7 2.0 %convert_add_fusion = f32[320,640]{1,0:T(8,128)} fusion(f32[320,640]{1,0:T(8,128)S(1)} %get-tuple-element.66, bf16[360,640]{1,0:T(8,128)(2,1)} %collective-permute-done.19), kind=kLoop, calls=%fused_computation | loop fusion | flops 409600 | bytes 2048000 | tf_op jit(solution)/shard_map/add | solution.py:823
  105.6 0.8 reduce_sum.21
  106.4 3.5 %all-to-all-done.2 = bf16[8,80,256]{2,1,0:T(8,128)(2,1)S(1)} async-done(((bf16[8,80,256]{2,1,0:T(8,128)(2,1)}), bf16[8,80,256]{2,1,0:T(8,128)(2,1)S(1)}, u32[]{:S(2)}, u32[]{:S(2)}) %all-to-all-start.2) | async-done | bytes 327712 | tf_op jit(solution)/shard_map/all_to_all | solution.py:818
  109.9 0.7 convert_reduce_fusion
  (40 shorter events, 3.5 us)
Async XLA Ops:
  0.6 15.7 %collective-permute-start = (bf16[32,2560]{1,0:T(8,128)(2,1)}, bf16[32,2560]{1,0:T(8,128)(2,1)S(1)}, u32[]{:S(2)}, u32[]{:S(2)}) collective-permute-start(bf16[32,2560]{1,0:T(8,128)(2,1)} %bitcast.30), channel_id=1, source_target_pairs={{0,1},{1,2},{2,3},{3,0},{4,5},{5,6},{6,7},{7,4},{8,9},{9,10},{10,1... | collective-permute-start | bytes 491528 | tf_op jit(solution)/shard_map/ppermute | solution.py:621
  1.2 15.1 %collective-permute-start.1 = (bf16[32,2560]{1,0:T(8,128)(2,1)}, bf16[32,2560]{1,0:T(8,128)(2,1)S(1)}, u32[]{:S(2)}, u32[]{:S(2)}) collective-permute-start(bf16[32,2560]{1,0:T(8,128)(2,1)} %bitcast.31), channel_id=1, source_target_pairs={{0,2},{1,3},{2,0},{3,1},{4,6},{5,7},{6,4},{7,5},{8,10},{9,11},{10,... | collective-permute-start | bytes 491528 | tf_op jit(solution)/shard_map/ppermute | solution.py:621
  3.7 12.6 %collective-permute-start.2 = (bf16[32,2560]{1,0:T(8,128)(2,1)}, bf16[32,2560]{1,0:T(8,128)(2,1)S(1)}, u32[]{:S(2)}, u32[]{:S(2)}) collective-permute-start(bf16[32,2560]{1,0:T(8,128)(2,1)} %bitcast.32), channel_id=1, source_target_pairs={{0,3},{1,0},{2,1},{3,2},{4,7},{5,4},{6,5},{7,6},{8,11},{9,8},{10,9... | collective-permute-start | bytes 491528 | tf_op jit(solution)/shard_map/ppermute | solution.py:621
  5.2 0.9 copy-start.3
  6.1 0.9 copy-start.8
  7.0 0.7 copy-start.9
  7.7 0.7 copy-start.10
  8.3 0.7 copy-start.11
  10.5 0.8 copy-start.2
  11.3 16.1 %copy-start.5 = (bf16[1,128,640]{2,1,0:T(8,128)(2,1)S(1)}, bf16[1,128,640]{2,1,0:T(8,128)(2,1)}, u32[]{:S(2)}) copy-start(bf16[1,128,640]{2,1,0:T(8,128)(2,1)} %param.19) | copy-start | bytes 491524
  11.3 16.1 %copy-start.6 = (f32[4,640]{1,0:T(4,128)S(1)}, f32[4,640]{1,0:T(4,128)}, u32[]{:S(2)}) copy-start(f32[4,640]{1,0:T(4,128)} %refs_10_.1) | copy-start | bytes 30724
  11.3 16.1 %copy-start.7 = (f32[4,256]{1,0:T(4,128)S(1)}, f32[4,256]{1,0:T(4,128)}, u32[]{:S(2)}) copy-start(f32[4,256]{1,0:T(4,128)} %refs_11_.1) | copy-start | bytes 12292
  11.3 24.4 %all-to-all-start.1 = ((bf16[4,32,768]{2,1,0:T(8,128)(2,1)}), bf16[4,32,768]{2,1,0:T(8,128)(2,1)S(1)}, u32[]{:S(2)}, u32[]{:S(2)}) async-start(bf16[4,32,768]{2,1,0:T(8,128)(2,1)} %get-tuple-element.58), calls=%async_computation.1 | async-start | bytes 393216 | tf_op jit(solution)/shard_map/all_to_all | solution.py:672
  16.3 1.9 %copy-start = (bf16[2560,640]{1,0:T(8,128)(2,1)S(1)}, bf16[2560,640]{1,0:T(8,128)(2,1)}, u32[]{:S(2)}) copy-start(bf16[2560,640]{1,0:T(8,128)(2,1)} %inner_weight_ref.1) | copy-start | bytes 9830404
  18.3 1.3 %copy-start.1 = (bf16[2560,256]{1,0:T(8,128)(2,1)S(1)}, bf16[2560,256]{1,0:T(8,128)(2,1)}, u32[]{:S(2)}) copy-start(bf16[2560,256]{1,0:T(8,128)(2,1)} %mixer_weight_ref.1) | copy-start | bytes 3932164
  19.6 0.9 copy-start.4
  22.0 5.5 %collective-permute-start.3 = (bf16[16,896]{1,0:T(8,128)(2,1)S(1)}, bf16[16,896]{1,0:T(8,128)(2,1)S(1)}, u32[]{:S(2)}, u32[]{:S(2)}) collective-permute-start(bf16[16,896]{1,0:T(8,128)(2,1)S(1)} %get-tuple-element.40), channel_id=1, source_target_pairs={{0,4},{4,8},{8,12},{1,5},{5,9},{9,13},{2,6},{6,10},{10,14},{3,7},{... | collective-permute-start | bytes 86024 | tf_op jit(solution)/shard_map/ppermute | solution.py:687
  29.5 9.5 %collective-permute-start.4 = (bf16[136,640]{1,0:T(8,128)(2,1)S(1)}, bf16[136,640]{1,0:T(8,128)(2,1)S(1)}, u32[]{:S(2)}, u32[]{:S(2)}) collective-permute-start(bf16[136,640]{1,0:T(8,128)(2,1)S(1)} %get-tuple-element.43), channel_id=1, source_target_pairs={{0,4},{4,8},{8,12},{12,0},{1,5},{5,9},{9,13},{13,1},{2,6},{6,10},{... | collective-permute-start | bytes 522248 | tf_op jit(solution)/shard_map/ppermute | solution.py:708
  31.9 11.4 %collective-permute-start.5 = (bf16[136,640]{1,0:T(8,128)(2,1)S(1)}, bf16[136,640]{1,0:T(8,128)(2,1)S(1)}, u32[]{:S(2)}, u32[]{:S(2)}) collective-permute-start(bf16[136,640]{1,0:T(8,128)(2,1)S(1)} %get-tuple-element.44), channel_id=1, source_target_pairs={{0,8},{4,12},{8,0},{12,4},{1,9},{5,13},{9,1},{13,5},{2,10},{6,14},... | collective-permute-start | bytes 522248 | tf_op jit(solution)/shard_map/ppermute | solution.py:708
  34.2 9.0 %collective-permute-start.6 = (bf16[136,640]{1,0:T(8,128)(2,1)S(1)}, bf16[136,640]{1,0:T(8,128)(2,1)S(1)}, u32[]{:S(2)}, u32[]{:S(2)}) collective-permute-start(bf16[136,640]{1,0:T(8,128)(2,1)S(1)} %get-tuple-element.45), channel_id=1, source_target_pairs={{0,12},{4,0},{8,4},{12,8},{1,13},{5,1},{9,5},{13,9},{2,14},{6,2},{... | collective-permute-start | bytes 522248 | tf_op jit(solution)/shard_map/ppermute | solution.py:708
  35.7 16.3 %collective-permute-start.14 = (bf16[4,32,768]{2,1,0:T(8,128)(2,1)S(1)}, bf16[4,32,768]{2,1,0:T(8,128)(2,1)S(1)}, u32[]{:S(2)}, u32[]{:S(2)}) collective-permute-start(bf16[4,32,768]{2,1,0:T(8,128)(2,1)S(1)} %all-to-all-done.1.refs_0_), channel_id=1, source_target_pairs={{0,1},{1,2},{2,3},{3,0},{4,5},{5,6},{6,7},{7,4},{8,9},{9,10},{10,1... | collective-permute-start | bytes 589832 | tf_op jit(solution)/shard_map/ppermute | solution.py:621
  35.7 17.0 %collective-permute-start.15 = (bf16[4,32,768]{2,1,0:T(8,128)(2,1)S(1)}, bf16[4,32,768]{2,1,0:T(8,128)(2,1)S(1)}, u32[]{:S(2)}, u32[]{:S(2)}) collective-permute-start(bf16[4,32,768]{2,1,0:T(8,128)(2,1)S(1)} %all-to-all-done.1.refs_0_), channel_id=1, source_target_pairs={{0,2},{1,3},{2,0},{3,1},{4,6},{5,7},{6,4},{7,5},{8,10},{9,11},{10,... | collective-permute-start | bytes 589832 | tf_op jit(solution)/shard_map/ppermute | solution.py:621
  39.0 13.7 %collective-permute-start.16 = (bf16[4,32,768]{2,1,0:T(8,128)(2,1)S(1)}, bf16[4,32,768]{2,1,0:T(8,128)(2,1)S(1)}, u32[]{:S(2)}, u32[]{:S(2)}) collective-permute-start(bf16[4,32,768]{2,1,0:T(8,128)(2,1)S(1)} %all-to-all-done.1.refs_0_), channel_id=1, source_target_pairs={{0,3},{1,0},{2,1},{3,2},{4,7},{5,4},{6,5},{7,6},{8,11},{9,8},{10,9... | collective-permute-start | bytes 589832 | tf_op jit(solution)/shard_map/ppermute | solution.py:621
  46.6 10.3 %collective-permute-start.7 = (bf16[136,640]{1,0:T(8,128)(2,1)S(1)}, bf16[136,640]{1,0:T(8,128)(2,1)S(1)}, u32[]{:S(2)}, u32[]{:S(2)}) collective-permute-start(bf16[136,640]{1,0:T(8,128)(2,1)S(1)} %get-tuple-element.54.pair_ref.refs_1_), channel_id=1, source_target_pairs={{0,12},{4,0},{8,4},{12,8},{1,13},{5,1},{9,5},{13,9},{2,14},{6,2},{... | collective-permute-start | bytes 522248 | tf_op jit(solution)/shard_map/ppermute | solution.py:621
  52.0 9.2 %collective-permute-start.17 = (bf16[136,640]{1,0:T(8,128)(2,1)S(1)}, bf16[136,640]{1,0:T(8,128)(2,1)S(1)}, u32[]{:S(2)}, u32[]{:S(2)}) collective-permute-start(bf16[136,640]{1,0:T(8,128)(2,1)S(1)} %get-tuple-element.54.pair_ref.refs_1_), channel_id=1, source_target_pairs={{0,4},{4,8},{8,12},{12,0},{1,5},{5,9},{9,13},{13,1},{2,6},{6,10},{... | collective-permute-start | bytes 522248 | tf_op jit(solution)/shard_map/ppermute | solution.py:621
  52.0 15.8 %collective-permute-start.18 = (bf16[136,640]{1,0:T(8,128)(2,1)S(1)}, bf16[136,640]{1,0:T(8,128)(2,1)S(1)}, u32[]{:S(2)}, u32[]{:S(2)}) collective-permute-start(bf16[136,640]{1,0:T(8,128)(2,1)S(1)} %get-tuple-element.54.pair_ref.refs_1_), channel_id=1, source_target_pairs={{0,8},{4,12},{8,0},{12,4},{1,9},{5,13},{9,1},{13,5},{2,10},{6,14},... | collective-permute-start | bytes 522248 | tf_op jit(solution)/shard_map/ppermute | solution.py:621
  68.9 29.3 %collective-permute-start.19 = (bf16[360,640]{1,0:T(8,128)(2,1)S(1)}, bf16[360,640]{1,0:T(8,128)(2,1)}, u32[]{:S(2)}, u32[]{:S(2)}) collective-permute-start(bf16[360,640]{1,0:T(8,128)(2,1)S(1)} %get-tuple-element.67), channel_id=1, source_target_pairs={{0,16},{16,0},{1,17},{17,1},{2,18},{18,2},{3,19},{19,3},{4,20},{20... | collective-permute-start | bytes 1382408 | tf_op jit(solution)/shard_map/ppermute | solution.py:799
  75.6 23.4 %all-to-all-start = ((bf16[4,32,2560]{2,1,0:T(8,128)(2,1)}), bf16[4,32,2560]{2,1,0:T(8,128)(2,1)S(1)}, u32[]{:S(2)}, u32[]{:S(2)}) async-start(bf16[4,32,2560]{2,1,0:T(8,128)(2,1)} %shard_map.134), calls=%async_computation | async-start | bytes 1310720 | tf_op jit(solution)/shard_map/all_to_all | solution.py:785
  79.1 10.0 %collective-permute-start.8 = (bf16[40,256]{1,0:T(8,128)(2,1)S(1)}, bf16[40,256]{1,0:T(8,128)(2,1)S(1)}, u32[]{:S(2)}, u32[]{:S(2)}) collective-permute-start(bf16[40,256]{1,0:T(8,128)(2,1)S(1)} %get-tuple-element.60), channel_id=1, source_target_pairs={{0,1},{1,2},{2,3},{3,0},{4,5},{5,6},{6,7},{7,4},{8,9},{9,10},{10,1... | collective-permute-start | bytes 61448 | tf_op jit(solution)/shard_map/ppermute | solution.py:770
  79.5 10.4 %collective-permute-start.9 = (bf16[40,256]{1,0:T(8,128)(2,1)S(1)}, bf16[40,256]{1,0:T(8,128)(2,1)S(1)}, u32[]{:S(2)}, u32[]{:S(2)}) collective-permute-start(bf16[40,256]{1,0:T(8,128)(2,1)S(1)} %get-tuple-element.61), channel_id=1, source_target_pairs={{0,2},{1,3},{2,0},{3,1},{4,6},{5,7},{6,4},{7,5},{8,10},{9,11},{10,... | collective-permute-start | bytes 61448 | tf_op jit(solution)/shard_map/ppermute | solution.py:770
  81.2 8.7 %collective-permute-start.10 = (bf16[40,256]{1,0:T(8,128)(2,1)S(1)}, bf16[40,256]{1,0:T(8,128)(2,1)S(1)}, u32[]{:S(2)}, u32[]{:S(2)}) collective-permute-start(bf16[40,256]{1,0:T(8,128)(2,1)S(1)} %get-tuple-element.62), channel_id=1, source_target_pairs={{0,3},{1,0},{2,1},{3,2},{4,7},{5,4},{6,5},{7,6},{8,11},{9,8},{10,9... | collective-permute-start | bytes 61448 | tf_op jit(solution)/shard_map/ppermute | solution.py:770
  89.9 5.6 %collective-permute-start.11 = (bf16[40,256]{1,0:T(8,128)(2,1)S(1)}, bf16[40,256]{1,0:T(8,128)(2,1)S(1)}, u32[]{:S(2)}, u32[]{:S(2)}) collective-permute-start(bf16[40,256]{1,0:T(8,128)(2,1)S(1)} %shard_map.135.refs_1_), channel_id=1, source_target_pairs={{0,4},{4,8},{8,12},{12,0},{1,5},{5,9},{9,13},{13,1},{2,6},{6,10},{... | collective-permute-start | bytes 61448 | tf_op jit(solution)/shard_map/ppermute | solution.py:621
  90.0 5.6 %collective-permute-start.12 = (bf16[40,256]{1,0:T(8,128)(2,1)S(1)}, bf16[40,256]{1,0:T(8,128)(2,1)S(1)}, u32[]{:S(2)}, u32[]{:S(2)}) collective-permute-start(bf16[40,256]{1,0:T(8,128)(2,1)S(1)} %shard_map.135.refs_1_), channel_id=1, source_target_pairs={{0,8},{4,12},{8,0},{12,4},{1,9},{5,13},{9,1},{13,5},{2,10},{6,14},... | collective-permute-start | bytes 61448 | tf_op jit(solution)/shard_map/ppermute | solution.py:621
  91.7 4.4 %collective-permute-start.13 = (bf16[40,256]{1,0:T(8,128)(2,1)S(1)}, bf16[40,256]{1,0:T(8,128)(2,1)S(1)}, u32[]{:S(2)}, u32[]{:S(2)}) collective-permute-start(bf16[40,256]{1,0:T(8,128)(2,1)S(1)} %shard_map.135.refs_1_), channel_id=1, source_target_pairs={{0,12},{4,0},{8,4},{12,8},{1,13},{5,1},{9,5},{13,9},{2,14},{6,2},{... | collective-permute-start | bytes 61448 | tf_op jit(solution)/shard_map/ppermute | solution.py:621
  99.0 11.0 %all-to-all-start.2 = ((bf16[8,80,256]{2,1,0:T(8,128)(2,1)}), bf16[8,80,256]{2,1,0:T(8,128)(2,1)S(1)}, u32[]{:S(2)}, u32[]{:S(2)}) async-start(bf16[8,80,256]{2,1,0:T(8,128)(2,1)} %shard_map.136), calls=%async_computation.2 | async-start | bytes 655360 | tf_op jit(solution)/shard_map/all_to_all | solution.py:818

commit v2 on v1

--- a/solution.py
+++ b/solution.py
@@ -13,16 +13,14 @@
 BF16 = jnp.bfloat16
 LANES = 128
 PAD = 8
-HIGHEST = lax.Precision.HIGHEST
 DIRECT = 8
 
 
-def dot(left, right, left_dim=1, right_dim=0, precision=None):
+def dot(left, right, left_dim=1, right_dim=0):
     return lax.dot_general(
         left,
         right,
         (((left_dim,), (right_dim,)), ((), ())),
-        precision=precision,
         preferred_element_type=F32,
     )
 
@@ -35,6 +33,22 @@
     return high, middle, low
 
 
+def fine(left, right, left_dim=1, right_dim=0):
+    left_high = left.astype(BF16)
+    left_low = (left - left_high.astype(F32)).astype(BF16)
+    right_high = right.astype(BF16)
+    right_low = (right - right_high.astype(F32)).astype(BF16)
+    lefts = jnp.concatenate([left_high, left_low, left_high], axis=left_dim)
+    rights = jnp.concatenate([right_high, right_high, right_low], axis=right_dim)
+    return dot(lefts, rights, left_dim, right_dim)
+
+
+def masked_sum(mask, values, values_dim=0):
+    chosen = jnp.where(mask, 1.0, 0.0).astype(BF16)
+    masks = jnp.concatenate([chosen] * 3, axis=1)
+    return dot(masks, jnp.concatenate(pieces(values), axis=values_dim), 1, values_dim)
+
+
 def head_map(width, head_dim):
     row = lax.broadcasted_iota(jnp.int32, (LANES, width), 0)
     column = lax.broadcasted_iota(jnp.int32, (LANES, width), 1)
@@ -43,13 +57,12 @@
 
 
 def spread(values, heads):
-    high, middle, low = pieces(values)
-    return dot(high, heads) + dot(middle, heads) + dot(low, heads)
+    return dot(jnp.concatenate(pieces(values), axis=1), jnp.concatenate([heads] * 3, axis=0))
 
 
 def collect(values, heads):
-    high, middle, low = pieces(values)
-    return dot(high, heads, 1, 1) + dot(middle, heads, 1, 1) + dot(low, heads, 1, 1)
+    high, middle, _ = pieces(values)
+    return dot(high, heads, 1, 1) + dot(middle, heads, 1, 1)
 
 
 def sigmoid(values):
@@ -96,34 +109,31 @@
     return total
 
 
-def blocks(
-    rows,
-    padded,
-    dp_count,
-    place_ref,
-    own_ref,
-    step_ref,
-    bias_ref,
-    log_ref,
-    skip_ref,
-    out_ref,
-    head_ref,
-    near_ref,
-    far_ref,
-    scratch,
-):
-    dp_place = place_ref[1]
-    seq_count = out_ref.shape[0]
+def blocks(rows, padded, dp_count, relative, place_ref, *refs):
+    own_ref, step_ref, bias_ref, log_ref, skip_ref, inner_ref, mixer_ref = refs[:7]
+    own_out_ref, step_out_ref, head_ref, inner_out_ref, mixer_out_ref = refs[7:12]
+    out_refs, scratch, wide, sems = refs[12:-3], refs[-3], refs[-2], refs[-1]
+    parts = sems.shape[1]
+    depth = inner_ref.shape[0] // parts
+    copies = []
+    for part in range(parts):
+        span = pl.ds(part * depth, depth)
+        pair = ((inner_ref, inner_out_ref), (mixer_ref, mixer_out_ref))
+        for number, (source, target) in enumerate(pair):
+            copy = pltpu.make_async_copy(source.at[span], target.at[span], sems.at[number, part])
+            copy.start()
+            copies.append(copy)
+    own_out_ref[...] = own_ref[...]
     head_count = bias_ref.shape[1]
-    scratch[...] = jnp.zeros_like(scratch)
-    scratch[:head_count] = step_ref[...].astype(F32)
-    turned = scratch[...].T.astype(BF16)
-    near_ref[...] = turned
-    far_ref[...] = turned
+    wide[...] = jnp.zeros_like(wide)
+    wide[:head_count] = step_ref[...].astype(F32)
+    step_out_ref[...] = wide[...].T.astype(BF16)
     head_ref[...] = jnp.zeros_like(head_ref)
     head_ref[0:1, :head_count] = bias_ref[...]
     head_ref[1:2, :head_count] = log_ref[...]
     head_ref[2:3, :head_count] = skip_ref[...]
+    dp_place = place_ref[1]
+    seq_count = scratch.shape[0]
     fill = jnp.zeros((own_ref.shape[0], padded - rows), F32)
     for target in range(seq_count):
         for hop in range(dp_count):
@@ -136,7 +146,36 @@
             span = slice(hop * padded, (hop + 1) * padded)
             if padded > rows:
                 chosen = jnp.concatenate([chosen, fill], axis=1)
-            out_ref[target, :, span] = chosen.astype(BF16)
+            scratch[target, :, span] = chosen.astype(BF16)
+    if relative:
+        for hop, out_ref in enumerate(out_refs):
+            out_ref[...] = scratch[lax.rem(place_ref[0] + hop, seq_count)]
+    else:
+        out_refs[0][...] = scratch[...]
+    for copy in copies:
+        copy.wait()
+
+
+def copied(sources, targets, sems):
+    copies = [
+        pltpu.make_async_copy(source, target, sems.at[number])
+        for number, (source, target) in enumerate(zip(sources, targets))
+    ]
+    for copy in copies:
+        copy.start()
+    return copies
+
+
+def add_parts(parts_ref, out_ref):
+    total = parts_ref[0].astype(F32)
+    for part in range(1, parts_ref.shape[0]):
+        total = total + parts_ref[part].astype(F32)
+    out_ref[...] = total.astype(out_ref.dtype)
+
+
+def pack(*refs):
+    for number, ref in enumerate(refs[:-1]):
+        refs[-1][number] = ref[...]
 
 
 def add_up(*refs):
@@ -152,18 +191,18 @@
     place = place_ref[2]
     rows = tokens[0].shape[0]
     for hop in range(count):
-        source = lax.rem(place - hop + count, count)
+        source = lax.bitwise_xor(place, hop)
         scratch[pl.ds(pl.multiple_of(source * rows, rows), rows)] = tokens[hop][...]
     gathered = scratch[...]
     length = gathered.shape[0]
     width = inner_ref.shape[1]
     whole = width // (2 * LANES) * (2 * LANES)
     mixer = dot(gathered, mixer_ref[...]).astype(BF16)
-    first = dot(gathered, inner_ref[:, :whole]).astype(BF16)
+    first = dot(gathered, inner_ref[:, :whole])
     joined = jnp.concatenate([inner_ref[:, whole:], step_ref[...]], axis=1)
     second = dot(gathered, joined)
     raw_out[...] = second[:, width - whole :]
-    inner = jnp.concatenate([first, second[:, : width - whole].astype(BF16)], axis=1)
+    inner = jnp.concatenate([first, second[:, : width - whole]], axis=1).astype(BF16)
     inner_out[...] = inner
     mixer_out[...] = mixer
     tail_out[:, :width] = inner[length - 2 * PAD :]
@@ -200,8 +239,7 @@
     step = softplus(raw_ref[...] + head_ref[0:1])
     log_decay = -step * jnp.exp(head_ref[1:2])
     row, column = triangle(length)
-    lower = jnp.where(row >= column, 1.0, 0.0)
-    decay = dot(lower, log_decay, precision=HIGHEST)
+    decay = masked_sum(row >= column, log_decay)
     step_ref[...] = step
     decay_ref[...] = decay
     heads = head_map(width, head_dim)
@@ -209,8 +247,8 @@
     tail = spread(jnp.exp(last - decay) * step, heads)
     lead = spread(jnp.exp(decay), heads)
     upstream = upstream_ref[...].astype(F32)
-    forward = dot(mixer_act[:, :state], tail * inner_act, 0, 0, HIGHEST).astype(BF16)
-    backward = dot(mixer_act[:, state:], lead * upstream, 0, 0, HIGHEST).astype(BF16)
+    forward = fine(mixer_act[:, :state].T, tail * inner_act).astype(BF16)
+    backward = fine(mixer_act[:, state:].T, lead * upstream).astype(BF16)
     high, middle, low = pieces(last)
     kinds = (high.astype(F32), middle.astype(F32), low.astype(F32))
     index = lax.broadcasted_iota(jnp.int32, (PAD, LANES), 0)
@@ -238,11 +276,19 @@
     decay_ref,
     head_ref,
     upstream_ref,
+    inner_weight_ref,
+    mixer_weight_ref,
     inner_grad_ref,
     mixer_grad_ref,
     row_ref,
     column_ref,
+    inner_near_ref,
+    mixer_near_ref,
+    sems,
 ):
+    copies = copied(
+        (inner_weight_ref, mixer_weight_ref), (inner_near_ref, mixer_near_ref), sems
+    )
     length, width = inner_pre_ref.shape
     state = mixer_pre_ref.shape[1] // 2
     mixer_pre = mixer_pre_ref[...]
@@ -254,7 +300,7 @@
     turned = decay.T
     row, column = triangle(length)
     causal = column >= row
-    scores = dot(input_mix, output_mix, 1, 1, HIGHEST)
+    scores = fine(input_mix, output_mix, 1, 1)
     heads = head_map(width, head_dim)
     skip = spread(head_ref[...], heads)[2:3]
     step_wide = spread(step, heads)
@@ -289,14 +335,16 @@
             term = dot(weight_high, mine_upstream) + dot(weight_low, mine_upstream)
             total = term if total is None else total + term
         inner_grad_ref[:, span] = step_wide[:, span] * total + skip[:, span] * upstream.astype(F32)
-    mixer_grad_ref[:, :state] = dot(mixed, output_mix, precision=HIGHEST)
-    mixer_grad_ref[:, state:] = dot(mixed, input_mix, 0, 0, HIGHEST)
+    mixer_grad_ref[:, :state] = fine(mixed, output_mix)
+    mixer_grad_ref[:, state:] = fine(mixed.T, input_mix)
     row_ref[...] = rows
     index = lax.broadcasted_iota(jnp.int32, (LANES, length), 0)
     stacked = jnp.zeros((LANES, length), F32)
     for number, kind in enumerate(columns):
         stacked = jnp.where(index == number, kind, stacked)
     column_ref[...] = stacked
+    for copy in copies:
+        copy.wait()
 
 
 def finish(
@@ -328,6 +376,7 @@
         pair_ref,
         mixer_out_ref,
         step_out_ref,
+        early_ref,
     ) = refs
     length, width = inner_pre_ref.shape
     state = mixer_pre_ref.shape[1] // 2
@@ -387,11 +436,11 @@
     rest = jnp.exp(last - decay)
     lead_wide = spread(lead, heads)
     tail_wide = spread(rest * step, heads)
-    from_end = dot(input_mix, end, precision=HIGHEST)
-    from_start = dot(output_mix, start, precision=HIGHEST)
+    from_end = fine(input_mix, end)
+    from_start = fine(output_mix, start)
     inner_grad = inner_grad_ref[...] + tail_wide * from_end
-    input_grad = mixer_grad_ref[:, :state] + dot(tail_wide * inner_act, end, 1, 1, HIGHEST)
-    output_grad = mixer_grad_ref[:, state:] + dot(lead_wide * upstream, start, 1, 1, HIGHEST)
+    input_grad = mixer_grad_ref[:, :state] + fine(tail_wide * inner_act, end, 1, 1)
+    output_grad = mixer_grad_ref[:, state:] + fine(lead_wide * upstream, start, 1, 1)
     end_part = rest * collect(inner_act * from_end, heads)
     start_part = lead * collect(upstream * from_start, heads)
     product = jnp.sum(end * start, axis=0, keepdims=True)
@@ -400,10 +449,8 @@
     sums = start_part - step * step_grad
     total = jnp.sum(step * end_part, axis=0, keepdims=True) + jnp.exp(last) * product
     row, column = triangle(length)
-    upper = jnp.where(column >= row, 1.0, 0.0)
-    decay_grad = (
-        dot(upper, sums, precision=HIGHEST) + dot(upper, column_ref[...], 1, 1, HIGHEST) + total
-    )
+    after_row = column >= row
+    decay_grad = masked_sum(after_row, sums) + masked_sum(after_row, column_ref[...], 1) + total
     step_grad = step_grad - jnp.exp(head_ref[1:2]) * decay_grad
     raw_grad = step_grad * sigmoid(raw_ref[...] + head_ref[0:1])
     step_out_ref[...] = raw_grad.astype(BF16)
@@ -423,8 +470,8 @@
     taps = conv_inner_ref.shape[0] - 1
     early = PAD - taps
     inner_scratch[:PAD] = jnp.where(index >= early, inner_total[:PAD], packed)
-    mixed = 2 * state
-    inner_scratch[early - taps : early, :mixed] = mixer_total[early:PAD]
+    early_ref[:, :width] = inner_total[:PAD]
+    early_ref[:, width:] = mixer_total[:PAD]
     pair_ref[:length] = inner_total[PAD:].astype(BF16)
     pair_ref[length:] = inner_scratch[:PAD].astype(BF16)
     mixer_out_ref[...] = mixer_total[PAD:].astype(BF16)
@@ -445,11 +492,8 @@
 
 
 def project_back(
-    taps,
-    seq_count,
-    place_ref,
     pair_ref,
-    next_ref,
+    late_ref,
     mixer_ref,
     step_ref,
     inner_weight_ref,
@@ -460,23 +504,22 @@
     mixer_scratch,
 ):
     count, rows, _ = out_ref.shape
-    length, mixed = mixer_ref.shape
+    length, _ = mixer_ref.shape
     width = pair_ref.shape[1]
-    valid = place_ref[0] < seq_count - 1
-    extra = next_ref[length:].astype(F32)
     head = length - PAD
-    inner_scratch[:head] = pair_ref[:head]
-    ending = add_late(pair_ref[head:length].astype(F32), extra, taps, valid)
-    inner_scratch[head:] = ending.astype(BF16)
-    shifted = jnp.concatenate([extra[PAD - taps :, :mixed], extra[: PAD - taps, :mixed]], axis=0)
+    whole = width // (2 * LANES) * (2 * LANES)
+
+    late = late_ref[...]
+    inner_scratch[:head, :width] = pair_ref[:head]
+    ending = pair_ref[head:length].astype(F32) + late[:, :width]
+    inner_scratch[head:, :width] = ending.astype(BF16)
+    inner_scratch[:, width:] = step_ref[...]
     mixer_scratch[:head] = mixer_ref[:head]
-    ending = add_late(mixer_ref[head:].astype(F32), shifted, taps, valid)
+    ending = mixer_ref[head:].astype(F32) + late[:, width:]
     mixer_scratch[head:] = ending.astype(BF16)
-    whole = width // (2 * LANES) * (2 * LANES)
     share = dot(inner_scratch[:, :whole], inner_weight_ref[:, :whole], 1, 1)
-    left = jnp.concatenate([inner_scratch[:, whole:], step_ref[...]], axis=1)
     right = jnp.concatenate([inner_weight_ref[:, whole:], step_weight_ref[...]], axis=1)
-    share = share + dot(left, right, 1, 1)
+    share = share + dot(inner_scratch[:, whole:], right, 1, 1)
     share = share + dot(mixer_scratch[...], mixer_weight_ref[...], 1, 1)
     share = share.astype(BF16)
     for target in range(count):
@@ -484,23 +527,21 @@
         out_ref[target] = share[span]
 
 
-def turn(relative, place_ref, *refs):
+def turn(place_ref, *refs):
     column_refs, out_ref, columns = refs[:-2], refs[-2], refs[-1]
-    seq_place = place_ref[0]
     chan_place = place_ref[2]
     chan_count = len(column_refs)
     seq_count, rows, _ = column_refs[0].shape
     length = chan_count * rows
     for hop in range(seq_count):
-        source = lax.rem(seq_place - hop + seq_count, seq_count) if relative else hop
         for chan_hop in range(chan_count):
             chan_source = lax.rem(chan_place - chan_hop + chan_count, chan_count)
             start = pl.multiple_of(hop * length + chan_source * rows, rows)
-            columns[pl.ds(start, rows)] = column_refs[chan_hop][source]
+            columns[pl.ds(start, rows)] = column_refs[chan_hop][hop]
     out_ref[...] = columns[...].T
 
 
-def arrange(relative, taps, place_ref, pair_refs, grads, steps):
+def arrange(relative, taps, used, place_ref, pair_refs, grads, steps):
     seq_place = place_ref[0]
     seq_count = len(pair_refs) if relative else pair_refs[0].shape[0]
     length = grads.shape[0] // seq_count
@@ -524,14 +565,16 @@
         grads[start + head : start + length] = ending.astype(BF16)
         packed = pair[length:].astype(F32)
         groups = packed.shape[1] // length
-        lines = [packed[:, group * length : (group + 1) * length] for group in range(groups)]
+        lines = [packed[:used, group * length : (group + 1) * length] for group in range(groups)]
+        spare = steps.shape[0] - used * groups
+        lines = lines + [jnp.zeros((spare, length), F32)]
         steps[:, start : start + length] = jnp.concatenate(lines, axis=0).astype(BF16)
 
 
-def leave(relative, taps, rows, scale, place_ref, *refs):
+def leave(relative, taps, used, rows, scale, place_ref, *refs):
     turned_ref = refs[0]
     out_ref, grads, steps = refs[-3:]
-    arrange(relative, taps, place_ref, refs[1:-3], grads, steps)
+    arrange(relative, taps, used, place_ref, refs[1:-3], grads, steps)
     padded = turned_ref.shape[0] // 2
     chosen = turned_ref[padded : padded + rows]
     out_ref[:rows] = (dot(chosen, grads[...]) * scale).astype(BF16)
@@ -545,6 +588,17 @@
     padded = turned_ref.shape[0] // 2
     out_ref[...] = dot(turned_ref[:rows], grads_ref[...]) * scale
     step_ref[...] = dot(steps_ref[...], turned_ref[:padded], 1, 1) * scale
+
+
+def last(used, kept_ref, step_ref, arrived_ref, out_ref, step_out_ref):
+    rows, _ = kept_ref.shape
+    out_ref[...] = kept_ref[...] + arrived_ref[:rows].astype(F32)
+    step = step_ref[:, :rows] + arrived_ref[rows:, :rows].astype(F32)
+    head_count = step_out_ref.shape[0]
+    groups = -(-head_count // used)
+    for head in range(head_count):
+        line = (head % groups) * used + head // groups
+        step_out_ref[head : head + 1] = step[line : line + 1]
 
 
 def mix(relative, taps, rows, scale, place_ref, *refs):
@@ -568,7 +622,7 @@
             after = (hop + 1) % seq_count
         start = hop * tokens
         head = tokens - PAD
-        columns[start : start + tokens] = column_ref[source]
+        columns[start : start + tokens] = column_ref[hop]
         block = message(hop)
         grads[start : start + head] = block[:head]
         valid = (source < seq_count - 1) & (chan_place == chan_count - 1)
@@ -593,14 +647,17 @@
     return [(source, (source + hop) % count) for source in range(count)]
 
 
-def call(body, place, arrays, out_shape, scratch=(), cost=3, plain=()):
+def call(body, place, arrays, out_shape, scratch=(), cost=3, plain=(), left=()):
     vmem = pltpu.MemorySpace.VMEM
     hbm = pltpu.MemorySpace.HBM
     arrays = [
         pltpu.with_memory_space_constraint(array, hbm if number in plain else vmem)
         for number, array in enumerate(arrays)
     ]
-    in_specs = [pl.BlockSpec(memory_space=pltpu.VMEM)] * len(arrays)
+    in_specs = [
+        pl.BlockSpec(memory_space=hbm if number in left else vmem) for number in range(len(arrays))
+    ]
+    out_specs = [pl.BlockSpec(memory_space=vmem)] * len(out_shape)
     if place is not None:
         in_specs = [pl.BlockSpec(memory_space=pltpu.SMEM)] + in_specs
         arrays = [place] + arrays
@@ -608,7 +665,7 @@
         body,
         out_shape=out_shape,
         in_specs=in_specs,
-        out_specs=[pl.BlockSpec(memory_space=pltpu.VMEM)] * len(out_shape),
+        out_specs=out_specs,
         scratch_shapes=list(scratch),
         cost_estimate=pl.CostEstimate(flops=cost * 10**8, bytes_accessed=0, transcendentals=0),
         compiler_params=pltpu.CompilerParams(vmem_limit_bytes=24 * 2**20),
@@ -618,8 +675,20 @@
 def around(block, axis):
     count = lax.axis_size(axis)
     return [block] + [
-        lax.ppermute(block, axis, ring(axis, hop)) for hop in reversed(range(1, count))
-    ][::-1]
+        lax.ppermute(block, axis, ring(axis, hop)) for hop in range(1, count)
+    ]
+
+
+def spread_out(block, axis):
+    count = lax.axis_size(axis)
+    parts = {0: block}
+    bit = count // 2
+    while bit:
+        pairs = [(source, source ^ bit) for source in range(count)]
+        for number in list(parts):
+            parts[number | bit] = lax.ppermute(parts[number], axis, pairs)
+        bit //= 2
+    return [parts[number] for number in range(count)]
 
 
 def body(
@@ -651,29 +720,55 @@
     grad_rows = model // (dp_count * seq_count)
     padded = -(-grad_rows // LANES) * LANES
     taps = conv_inner.shape[0] - 1
+    parts = next(count for count in (4, 2, 1) if model % (count * LANES) == 0)
     places = [place, lax.axis_index("dp"), lax.axis_index("chan")]
     places = jnp.stack(places).astype(jnp.int32)
     norm_factor = 1.0 / math.sqrt(length * seq_count * dp_count)
 
-    gathered = around(own, "chan")
-    sorted_columns, head_rows, step_near, step_far = call(
-        functools.partial(blocks, grad_rows, padded, dp_count),
+    gathered = spread_out(own, "chan")
+    if relative:
+        column_shapes = [shape(rows, dp_count * padded, dtype=BF16)] * seq_count
+    else:
+        column_shapes = [shape(seq_count, rows, dp_count * padded, dtype=BF16)]
+    own_near, step_near, head_rows, inner_near, mixer_near, *sorted_columns = call(
+        functools.partial(blocks, grad_rows, padded, dp_count, relative),
         places,
-        [own, step_weight.T, step_bias[None], decay_log[None], skip_gain[None]],
-        [
-            shape(seq_count, rows, dp_count * padded, dtype=BF16),
+        [
+            own,
+            step_weight.T,
+            step_bias[None],
+            decay_log[None],
+            skip_gain[None],
+            inner_weight,
+            mixer_weight,
+        ],
+        [
+            shape(rows, model, dtype=BF16),
+            shape(model, LANES, dtype=BF16),
             shape(PAD, LANES),
-            shape(model, LANES, dtype=BF16),
-            jax.ShapeDtypeStruct((model, LANES), BF16),
+            shape(model, width, dtype=BF16),
+            shape(model, mixed, dtype=BF16),
+        ]
+        + column_shapes,
+        [
+            pltpu.VMEM((seq_count, rows, dp_count * padded), BF16),
+            pltpu.VMEM((LANES, model), F32),
+            pltpu.SemaphoreType.DMA((2, parts)),
         ],
-        [pltpu.VMEM((LANES, model), F32)],
-        cost=2,
-    )
-    columns = lax.all_to_all(sorted_columns, "seq", split_axis=0, concat_axis=0)
+        cost=1,
+        plain=range(7),
+        left=(5, 6),
+    )
+    if relative:
+        columns = [sorted_columns[0]]
+        for hop, block in enumerate(sorted_columns[1:], 1):
+            columns.append(lax.ppermute(block, "seq", ring("seq", hop)))
+    else:
+        columns = lax.all_to_all(sorted_columns[0], "seq", split_axis=0, concat_axis=0)
     inner_proj, mixer_proj, step_raw, tail = call(
         functools.partial(project, chan_count),
         places,
-        gathered + [inner_weight, mixer_weight, step_near],
+        [own_near] + gathered[1:] + [inner_near, mixer_near, step_near],
         [
             shape(length, width, dtype=BF16),
             shape(length, mixed, dtype=BF16),
@@ -710,22 +805,45 @@
         ]
     else:
         received = [lax.all_to_all(messages[0], "seq", split_axis=0, concat_axis=0)]
-    inner_part, mixer_part, row_part, column_part = call(
+    inner_part, mixer_part, row_part, column_part, inner_back, mixer_back = call(
         functools.partial(within, head_dim),
         None,
-        [inner_pre, mixer_pre, step, decay, head_rows, upstream],
-        [shape(length, width), shape(length, mixed), shape(length, LANES), shape(LANES, length)],
-    )
+        [
+            inner_pre,
+            mixer_pre,
+            step,
+            decay,
+            head_rows,
+            upstream,
+            inner_weight,
+            mixer_weight,
+        ],
+        [
+            shape(length, width),
+            shape(length, mixed),
+            shape(length, LANES),
+            shape(LANES, length),
+            shape(model, width, dtype=BF16),
+            shape(model, mixed, dtype=BF16),
+        ],
+        [pltpu.SemaphoreType.DMA((2,))],
+        plain=(6, 7),
+        left=(6, 7),
+    )
+    if relative:
+        (columns,) = call(
+            pack, None, columns, [shape(seq_count, rows, dp_count * padded, dtype=BF16)], cost=1
+        )
     all_columns = around(columns, "chan")
     (turned,) = call(
-        functools.partial(turn, relative),
+        turn,
         places,
         all_columns,
         [shape(dp_count * padded, seq_count * length, dtype=BF16)],
         [pltpu.VMEM((seq_count * length, dp_count * padded), BF16)],
     )
 
-    pair, mixer_local, step_grad, *mixer_sent = call(
+    pair, mixer_local, step_grad, early, *mixer_sent = call(
         functools.partial(finish, head_dim, relative, seq_count, chan_count),
         places,
         received
@@ -748,6 +866,7 @@
             shape(length + PAD, width, dtype=BF16),
             shape(length, mixed, dtype=BF16),
             shape(length, LANES, dtype=BF16),
+            shape(PAD, width + mixed),
         ]
         + [shape(rows + PAD, mixed, dtype=BF16)] * chan_count,
         [pltpu.VMEM((length + 2 * PAD, width), F32), pltpu.VMEM((length + 2 * PAD, mixed), F32)],
@@ -759,14 +878,10 @@
             return around(block, "seq")
         return [lax.all_gather(block, "seq")]
 
+    backward_pairs = [(source + 1, source) for source in range(seq_count - 1)]
+    late = lax.ppermute(early, "seq", backward_pairs)
     pairs = over_seq(pair)
-    if relative:
-        following = pairs[-1]
-    else:
-        following = lax.rem(place + 1, seq_count)
-        following = lax.dynamic_index_in_dim(pairs[0], following, 0, False)
-
-    mixer_rows = mixer_sent[:1] + [
+    mixer_rows = list(mixer_sent[:1]) + [
         lax.ppermute(block, "chan", ring("chan", hop))
         for hop, block in enumerate(mixer_sent[1:], 1)
     ]
@@ -774,20 +889,20 @@
     mixers = over_seq(mixer_rows)
 
     (sent,) = call(
-        functools.partial(project_back, taps, seq_count),
-        places,
-        [pair, following, mixer_local, step_grad, inner_weight, mixer_weight, step_far],
+        project_back,
+        None,
+        [pair, late, mixer_local, step_grad, inner_back, mixer_back, step_near],
         [shape(chan_count, rows, model, dtype=BF16)],
-        [pltpu.VMEM((length, width), BF16), pltpu.VMEM((length, mixed), BF16)],
+        [pltpu.VMEM((length, width + LANES), BF16), pltpu.VMEM((length, mixed), BF16)],
         cost=4,
-        plain=(4, 5, 6),
     )
     taken = lax.all_to_all(sent, "chan", split_axis=0, concat_axis=0)
 
     groups = width // length
-    step_lines = PAD * groups
+    used = -(-head_count // groups)
+    step_lines = -(-used * groups // (2 * PAD)) * (2 * PAD)
     leaving, grads, steps = call(
-        functools.partial(leave, relative, taps, grad_rows, norm_factor),
+        functools.partial(leave, relative, taps, used, grad_rows, norm_factor),
         places,
         [turned] + pairs,
         [
@@ -818,12 +933,23 @@
     mixer_blocks = lax.all_to_all(
         mixer_blocks, ("dp", "chan"), split_axis=0, concat_axis=0
     )
-    mixer_weight_grad = jnp.sum(mixer_blocks.astype(F32), axis=0)
-    input_grad = jnp.sum(taken.astype(F32), axis=0).astype(BF16)
-    inner_weight_grad = kept + arrived[:grad_rows].astype(F32)
-    kept_step = kept_step[:, :grad_rows] + arrived[grad_rows:, :grad_rows].astype(F32)
-    lines = [kept_step[(head % groups) * PAD + head // groups] for head in range(head_count)]
-    step_weight_grad = jnp.stack(lines, axis=1)
+    (mixer_weight_grad,) = call(
+        add_parts, None, [mixer_blocks], [jax.ShapeDtypeStruct(mixer_blocks.shape[1:], F32)], cost=1
+    )
+    (input_grad,) = call(
+        add_parts, None, [taken], [jax.ShapeDtypeStruct((rows, model), BF16)], cost=1
+    )
+    inner_weight_grad, step_weight_grad = call(
+        functools.partial(last, used),
+        None,
+        [kept, kept_step, arrived],
+        [
+            jax.ShapeDtypeStruct((grad_rows, width), F32),
+            jax.ShapeDtypeStruct((head_count, grad_rows), F32),
+        ],
+        cost=1,
+    )
+    step_weight_grad = step_weight_grad.T
     return (input_grad[None], inner_weight_grad, mixer_weight_grad, step_weight_grad)
 
 

time: 111 us -> 103 us (0.928)
  local copies, waits for them, and re-layouts: 10 us -> 0.02 us
  waiting for transfers between devices: 34.6 us -> 39.3 us
  other arithmetic: 4.25 us -> 0.08 us
  Pallas kernels: 18.9 us -> 20.8 us
    ppermute x0 -> x7, waiting for transfers between devices: none -> 12.1 us  [the longest x1 5.61 us: body(): late = lax.ppermute(early, 'seq', backward_pairs)]
    unnamed x24 -> x6, local copies, waits for them, and re-layouts: 8.77 us -> 0.02 us
    ppermute x0 -> x7, starting transfers between devices: none -> 6.95 us  [the longest x3 3.04 us: spread_out(): parts[number | bit] = lax.ppermute(parts[number], axis, pairs)]
    ppermute x3, waiting for transfers between devices: 7.39 us -> 2.04 us  [body(): lax.ppermute(block, 'chan', ring('chan', hop))]
    all_to_all x1 -> x0, starting transfers between devices: 5 us -> none  [body(): columns = lax.all_to_all(sorted_columns, 'seq', split_axis=0, concat_axis=0)]
    ppermute x12 -> x9, waiting for transfers between devices: 16.5 us -> 13 us  [around(): lax.ppermute(block, axis, ring(axis, hop))]
    add x2 -> x0, other arithmetic: 2.72 us -> none  [the longest x1 1.96 us: body(): inner_weight_grad = kept + arrived[:grad_rows].astype(F32)]
    pallas_call x11 -> x15, Pallas kernels: 18.9 us -> 20.8 us  [call(): pl.pallas_call(body, out_shape=out_shape, in_specs=in_specs, out_specs=ou...]
  transfers between devices with their start and end apart: 23 -> 26, of which waited for: 11 -> 14; matrix products, arithmetic and copies ran while one was open for 4% -> 0% of each run, Pallas kernels for 16% -> 17%
where the time goes in v2:
time: 103 us
  starting transfers between devices  41.6 us (40%)
  waiting for transfers between devices  39.3 us (38%)
  Pallas kernels  20.8 us (20%)
    pallas_call x15, Pallas kernels, call(): pl.pallas_call(body, out_shape=out_shape, in_specs=in_specs, out_specs=ou...  20.8 us
    ppermute x9, starting transfers between devices, around(): lax.ppermute(block, axis, ring(axis, hop))  14.4 us
    ppermute x9, waiting for transfers between devices, around(): lax.ppermute(block, axis, ring(axis, hop))  13 us
    ppermute x3, starting transfers between devices, body(): lax.ppermute(message, 'seq', ring('seq', hop))  6.31 us
    ppermute x1, waiting for transfers between devices, body(): late = lax.ppermute(early, 'seq', backward_pairs)  5.61 us
    ppermute x3, waiting for transfers between devices, body(): lax.ppermute(message, 'seq', ring('seq', hop))  5.35 us
    all_to_all x1, waiting for transfers between devices, body(): lax.all_to_all(mixer_blocks, ('dp', 'chan'), split_axis=0, concat_axis=0)  5.29 us
    ppermute x3, waiting for transfers between devices, spread_out(): parts[number | bit] = lax.ppermute(parts[number], axis, pairs)  4.41 us
  transfers between devices with their start and end apart: 26, of which 14 were waited for; matrix products, arithmetic and copies ran while one was open for 0% of the time, Pallas kernels for 17%

profile of v2, /device:TPU:0, one launch (start us, length us, event | category | flops | bytes accessed | tf_op | source)
XLA Modules:
  0.0 102.6 jit_solution(5460892943957101625)
XLA Ops:
  0.6 3.0 %collective-permute-start.1 = (bf16[32,2560]{1,0:T(8,128)(2,1)}, bf16[32,2560]{1,0:T(8,128)(2,1)S(1)}, u32[]{:S(2)}, u32[]{:S(2)}) collective-permute-start(bf16[32,2560]{1,0:T(8,128)(2,1)} %bitcast.14), channel_id=1, source_target_pairs={{0,2},{1,3},{2,0},{3,1},{4,6},{5,7},{6,4},{7,5},{8,10},{9,11},{10,... | collective-permute-start | bytes 491528 | tf_op jit(solution)/shard_map/ppermute | solution.py:689
  3.7 4.4 %collective-permute-done.1.refs_2_ = bf16[32,2560]{1,0:T(8,128)(2,1)S(1)} collective-permute-done((bf16[32,2560]{1,0:T(8,128)(2,1)}, bf16[32,2560]{1,0:T(8,128)(2,1)S(1)}, u32[]{:S(2)}, u32[]{:S(2)}) %collective-permute-start.1) | collective-permute-done | bytes 163872 | tf_op jit(solution)/shard_map/ppermute | solution.py:689
  8.2 3.5 %shard_map.129 = (bf16[32,2560]{1,0:T(8,128)(2,1)S(1)}, bf16[2560,128]{1,0:T(8,128)(2,1)S(1)}, f32[8,128]{1,0:T(8,128)S(1)}, bf16[2560,640]{1,0:T(8,128)(2,1)S(1...) custom-call(s32[3]{0:T(128)S(1)} %pad_add_fusion.place_ref, ...), custom_call_target="tpu_custom_call" | custom-call | flops 100000000 | tf_op jit(solution)/shard_map/pallas_call | solution.py:664
  11.7 1.5 %shard_map.130 = (bf16[128,640]{1,0:T(8,128)(2,1)S(1)}, bf16[128,256]{1,0:T(8,128)(2,1)S(1)}, f32[128,128]{1,0:T(8,128)S(1)}, bf16[16,896]{1,0:T(8,128)(2,1)S(1)}) custom-call(s32[3]{0:T(128)S(1)} %pad_add_fusion.place_ref, bf16[32,2560]{1,0:T(8,128)(2,1)S(1)} %get-tuple-element.47.refs_0_, bf16[32,2560]{1,0:T(8,128)(2,1)S(1)} %collective-permute-done.refs_1_, ...), custom_call_target="tpu_custom_call" | custom-call | flops 400000000 | tf_op jit(solution)/shard_map/pallas_call | solution.py:664
  13.2 3.7 %collective-permute-start.3 = (bf16[16,896]{1,0:T(8,128)(2,1)S(1)}, bf16[16,896]{1,0:T(8,128)(2,1)S(1)}, u32[]{:S(2)}, u32[]{:S(2)}) collective-permute-start(bf16[16,896]{1,0:T(8,128)(2,1)S(1)} %get-tuple-element.53), channel_id=1, source_target_pairs={{0,4},{4,8},{8,12},{1,5},{5,9},{9,13},{2,6},{6,10},{10,14},{3,7},{... | collective-permute-start | bytes 86024 | tf_op jit(solution)/shard_map/ppermute | solution.py:782
  16.9 1.5 %collective-permute-done.3.refs_2_ = bf16[16,896]{1,0:T(8,128)(2,1)S(1)} collective-permute-done((bf16[16,896]{1,0:T(8,128)(2,1)S(1)}, bf16[16,896]{1,0:T(8,128)(2,1)S(1)}, u32[]{:S(2)}, u32[]{:S(2)}) %collective-permute-start.3) | collective-permute-done | bytes 28704 | tf_op jit(solution)/shard_map/ppermute | solution.py:782
  18.5 1.6 %shard_map.131 = (f32[128,640]{1,0:T(8,128)S(1)}, f32[128,256]{1,0:T(8,128)S(1)}, f32[128,128]{1,0:T(8,128)S(1)}, f32[128,128]{1,0:T(8,128)S(1)}, bf16[136,640]{...) custom-call(s32[3]{0:T(128)S(1)} %pad_add_fusion.place_ref, ...), custom_call_target="tpu_custom_call" | custom-call | flops 300000000 | tf_op jit(solution)/shard_map/pallas_call | solution.py:664
  20.1 2.4 %collective-permute-start.4 = (bf16[136,640]{1,0:T(8,128)(2,1)S(1)}, bf16[136,640]{1,0:T(8,128)(2,1)S(1)}, u32[]{:S(2)}, u32[]{:S(2)}) collective-permute-start(bf16[136,640]{1,0:T(8,128)(2,1)S(1)} %get-tuple-element.56), channel_id=1, source_target_pairs={{0,4},{4,8},{8,12},{12,0},{1,5},{5,9},{9,13},{13,1},{2,6},{6,10},{... | collective-permute-start | bytes 522248 | tf_op jit(solution)/shard_map/ppermute | solution.py:803
  22.5 2.6 %collective-permute-start.5 = (bf16[136,640]{1,0:T(8,128)(2,1)S(1)}, bf16[136,640]{1,0:T(8,128)(2,1)S(1)}, u32[]{:S(2)}, u32[]{:S(2)}) collective-permute-start(bf16[136,640]{1,0:T(8,128)(2,1)S(1)} %get-tuple-element.57), channel_id=1, source_target_pairs={{0,8},{4,12},{8,0},{12,4},{1,9},{5,13},{9,1},{13,5},{2,10},{6,14},... | collective-permute-start | bytes 522248 | tf_op jit(solution)/shard_map/ppermute | solution.py:803
  25.1 1.3 %collective-permute-start.6 = (bf16[136,640]{1,0:T(8,128)(2,1)S(1)}, bf16[136,640]{1,0:T(8,128)(2,1)S(1)}, u32[]{:S(2)}, u32[]{:S(2)}) collective-permute-start(bf16[136,640]{1,0:T(8,128)(2,1)S(1)} %get-tuple-element.58), channel_id=1, source_target_pairs={{0,12},{4,0},{8,4},{12,8},{1,13},{5,1},{9,5},{13,9},{2,14},{6,2},{... | collective-permute-start | bytes 522248 | tf_op jit(solution)/shard_map/ppermute | solution.py:803
  26.4 0.7 collective-permute-start.8
  27.1 0.3 collective-permute-start.9
  27.4 2.5 %collective-permute-done.4.refs_0_ = bf16[136,640]{1,0:T(8,128)(2,1)S(1)} collective-permute-done((bf16[136,640]{1,0:T(8,128)(2,1)S(1)}, bf16[136,640]{1,0:T(8,128)(2,1)S(1)}, u32[]{:S(2)}, u32[]{:S(2)}) %collective-permute-start.4) | collective-permute-done | bytes 174112 | tf_op jit(solution)/shard_map/ppermute | solution.py:803
  29.9 1.6 %collective-permute-start.10 = (bf16[32,768]{1,0:T(8,128)(2,1)S(1)}, bf16[32,768]{1,0:T(8,128)(2,1)S(1)}, u32[]{:S(2)}, u32[]{:S(2)}) collective-permute-start(bf16[32,768]{1,0:T(8,128)(2,1)S(1)} %get-tuple-element.76), channel_id=1, source_target_pairs={{0,12},{4,0},{8,4},{12,8},{1,13},{5,1},{9,5},{13,9},{2,14},{6,2},{... | collective-permute-start | bytes 147464 | tf_op jit(solution)/shard_map/ppermute | solution.py:765
  31.5 2.7 %shard_map.132 = (f32[128,640]{1,0:T(8,128)S(1)}, f32[128,256]{1,0:T(8,128)S(1)}, f32[128,128]{1,0:T(8,128)S(1)}, f32[128,128]{1,0:T(8,128)S(1)}, bf16[2560,640]...) custom-call(f32[128,640]{1,0:T(8,128)S(1)} %get-tuple-element.59.inner_pre_ref.refs_3_, ...), custom_call_target="tpu_custom_call" | custom-call | flops 300000000 | tf_op jit(solution)/shard_map/pallas_call | solution.py:664
  34.2 2.9 %collective-permute-done.5.refs_1_ = bf16[136,640]{1,0:T(8,128)(2,1)S(1)} collective-permute-done((bf16[136,640]{1,0:T(8,128)(2,1)S(1)}, bf16[136,640]{1,0:T(8,128)(2,1)S(1)}, u32[]{:S(2)}, u32[]{:S(2)}) %collective-permute-start.5) | collective-permute-done | bytes 174112 | tf_op jit(solution)/shard_map/ppermute | solution.py:803
  37.1 2.4 %shard_map.133 = (bf16[136,640]{1,0:T(8,128)(2,1)S(1)}, bf16[128,256]{1,0:T(8,128)(2,1)S(1)}, bf16[128,128]{1,0:T(8,128)(2,1)S(1)}, f32[8,896]{1,0:T(8,128)S(1)}...) custom-call(s32[3]{0:T(128)S(1)} %pad_add_fusion.place_ref, ...), custom_call_target="tpu_custom_call" | custom-call | flops 500000000 | tf_op jit(solution)/shard_map/pallas_call | solution.py:664
  39.5 1.3 %collective-permute-start.7 = (f32[8,896]{1,0:T(8,128)S(1)}, f32[8,896]{1,0:T(8,128)S(1)}, u32[]{:S(2)}, u32[]{:S(2)}) collective-permute-start(f32[8,896]{1,0:T(8,128)S(1)} %get-tuple-element.68), channel_id=1, source_target_pairs={{4,0},{8,4},{12,8},{5,1},{9,5},{13,9},{6,2},{10,6},{14,10},{7,3},{... | collective-permute-start | bytes 86024 | tf_op jit(solution)/shard_map/ppermute | solution.py:882
  40.8 2.1 %collective-permute-done.9.refs_2_ = bf16[32,768]{1,0:T(8,128)(2,1)S(1)} collective-permute-done((bf16[32,768]{1,0:T(8,128)(2,1)S(1)}, bf16[32,768]{1,0:T(8,128)(2,1)S(1)}, u32[]{:S(2)}, u32[]{:S(2)}) %collective-permute-start.9) | collective-permute-done | bytes 49184 | tf_op jit(solution)/shard_map/ppermute | solution.py:765
  43.0 5.6 %collective-permute-done.7.late_ref = f32[8,896]{1,0:T(8,128)S(1)} collective-permute-done((f32[8,896]{1,0:T(8,128)S(1)}, f32[8,896]{1,0:T(8,128)S(1)}, u32[]{:S(2)}, u32[]{:S(2)}) %collective-permute-start.7) | collective-permute-done | bytes 28704 | tf_op jit(solution)/shard_map/ppermute | solution.py:882
  48.6 2.7 %shard_map.134 = bf16[4,32,2560]{2,1,0:T(8,128)(2,1)} custom-call(bf16[136,640]{1,0:T(8,128)(2,1)S(1)} %get-tuple-element.67.pair_ref.refs_1_, f32[8,896]{1,0:T(8,128)S(1)} %collective-permute-done.7.late_ref, bf16[128,256]{1,0:T(8,128)(2,1)S(1)} %get-tuple-element.69.mixer_ref, bf16[128,128]{1,0:T(8,128)(2,1)S(1)} %get-tuple-element.70.step_ref, ...), custom_call_target="tpu_custom_call" | custom-call | flops 400000000 | tf_op jit(solution)/shard_map/pallas_call | solution.py:664
  51.3 3.5 %all-to-all-start = ((bf16[4,32,2560]{2,1,0:T(8,128)(2,1)}), bf16[4,32,2560]{2,1,0:T(8,128)(2,1)S(1)}, u32[]{:S(2)}, u32[]{:S(2)}) async-start(bf16[4,32,2560]{2,1,0:T(8,128)(2,1)} %shard_map.134), calls=%async_computation | async-start | bytes 1310720 | tf_op jit(solution)/shard_map/all_to_all | solution.py:899
  54.7 2.0 %collective-permute-start.18 = (bf16[4,32,768]{2,1,0:T(8,128)(2,1)S(1)}, bf16[4,32,768]{2,1,0:T(8,128)(2,1)S(1)}, u32[]{:S(2)}, u32[]{:S(2)}) collective-permute-start(bf16[4,32,768]{2,1,0:T(8,128)(2,1)S(1)} %shard_map.135.refs_0_), channel_id=1, source_target_pairs={{0,2},{1,3},{2,0},{3,1},{4,6},{5,7},{6,4},{7,5},{8,10},{9,11},{10,... | collective-permute-start | bytes 589832 | tf_op jit(solution)/shard_map/ppermute | solution.py:678
  56.7 2.0 %collective-permute-start.20 = (bf16[136,640]{1,0:T(8,128)(2,1)S(1)}, bf16[136,640]{1,0:T(8,128)(2,1)S(1)}, u32[]{:S(2)}, u32[]{:S(2)}) collective-permute-start(bf16[136,640]{1,0:T(8,128)(2,1)S(1)} %get-tuple-element.67.pair_ref.refs_1_), channel_id=1, source_target_pairs={{0,4},{4,8},{8,12},{12,0},{1,5},{5,9},{9,13},{13,1},{2,6},{6,10},{... | collective-permute-start | bytes 522248 | tf_op jit(solution)/shard_map/ppermute | solution.py:678
  58.8 0.7 collective-permute-start.21
  59.4 2.9 %collective-permute-start.22 = (bf16[136,640]{1,0:T(8,128)(2,1)S(1)}, bf16[136,640]{1,0:T(8,128)(2,1)S(1)}, u32[]{:S(2)}, u32[]{:S(2)}) collective-permute-start(bf16[136,640]{1,0:T(8,128)(2,1)S(1)} %get-tuple-element.67.pair_ref.refs_1_), channel_id=1, source_target_pairs={{0,12},{4,0},{8,4},{12,8},{1,13},{5,1},{9,5},{13,9},{2,14},{6,2},{... | collective-permute-start | bytes 522248 | tf_op jit(solution)/shard_map/ppermute | solution.py:678
  62.4 6.8 %collective-permute-done.18.refs_2_ = bf16[4,32,768]{2,1,0:T(8,128)(2,1)S(1)} collective-permute-done((bf16[4,32,768]{2,1,0:T(8,128)(2,1)S(1)}, bf16[4,32,768]{2,1,0:T(8,128)(2,1)S(1)}, u32[]{:S(2)}, u32[]{:S(2)}) %collective-permute-start.18) | collective-permute-done | bytes 196640 | tf_op jit(solution)/shard_map/ppermute | solution.py:678
  69.2 0.9 shard_map.139.refs_0_.turned_ref
  70.0 2.9 %collective-permute-done.21.refs_3_ = bf16[136,640]{1,0:T(8,128)(2,1)S(1)} collective-permute-done((bf16[136,640]{1,0:T(8,128)(2,1)S(1)}, bf16[136,640]{1,0:T(8,128)(2,1)S(1)}, u32[]{:S(2)}, u32[]{:S(2)}) %collective-permute-start.21) | collective-permute-done | bytes 174112 | tf_op jit(solution)/shard_map/ppermute | solution.py:678
  72.9 1.1 %shard_map.140 = (bf16[336,640]{1,0:T(8,128)(2,1)S(1)}, bf16[512,640]{1,0:T(8,128)(2,1)S(1)}, bf16[16,512]{1,0:T(8,128)(2,1)S(1)}) custom-call(s32[3]{0:T(128)S(1)} %pad_add_fusion.place_ref, bf16[768,512]{1,0:T(8,128)(2,1)S(1)} %shard_map.139.refs_0_.turned_ref, bf16[136,640]{1,0:T(8,128)(2,1)S(1)} %get-tuple-element.67.pair_ref.refs_1_, ...), custom_call_target="tpu_custom_call" | custom-call | flops 300000000 | tf_op jit(solution)/shard_map/pallas_call | solution.py:664
  74.0 1.6 %collective-permute-start.23 = (bf16[336,640]{1,0:T(8,128)(2,1)S(1)}, bf16[336,640]{1,0:T(8,128)(2,1)S(1)}, u32[]{:S(2)}, u32[]{:S(2)}) collective-permute-start(bf16[336,640]{1,0:T(8,128)(2,1)S(1)} %get-tuple-element.86), channel_id=1, source_target_pairs={{0,16},{16,0},{1,17},{17,1},{2,18},{18,2},{3,19},{19,3},{4,20},{20... | collective-permute-start | bytes 1290248 | tf_op jit(solution)/shard_map/ppermute | solution.py:914
  75.6 0.1 collective-permute-start.12
  75.7 1.7 %collective-permute-start.13 = (bf16[40,256]{1,0:T(8,128)(2,1)S(1)}, bf16[40,256]{1,0:T(8,128)(2,1)S(1)}, u32[]{:S(2)}, u32[]{:S(2)}) collective-permute-start(bf16[40,256]{1,0:T(8,128)(2,1)S(1)} %get-tuple-element.80), channel_id=1, source_target_pairs={{0,3},{1,0},{2,1},{3,2},{4,7},{5,4},{6,5},{7,6},{8,11},{9,8},{10,9... | collective-permute-start | bytes 61448 | tf_op jit(solution)/shard_map/ppermute | solution.py:885
  77.4 1.5 %collective-permute-done.11.refs_1_ = bf16[40,256]{1,0:T(8,128)(2,1)S(1)} collective-permute-done((bf16[40,256]{1,0:T(8,128)(2,1)S(1)}, bf16[40,256]{1,0:T(8,128)(2,1)S(1)}, u32[]{:S(2)}, u32[]{:S(2)}) %collective-permute-start.11) | collective-permute-done | bytes 20512 | tf_op jit(solution)/shard_map/ppermute | solution.py:885
  78.8 0.6 collective-permute-done.12.refs_2_
  79.4 4.3 %collective-permute-start.14 = (bf16[40,256]{1,0:T(8,128)(2,1)S(1)}, bf16[40,256]{1,0:T(8,128)(2,1)S(1)}, u32[]{:S(2)}, u32[]{:S(2)}) collective-permute-start(bf16[40,256]{1,0:T(8,128)(2,1)S(1)} %shard_map.136.refs_1_), channel_id=1, source_target_pairs={{0,4},{4,8},{8,12},{12,0},{1,5},{5,9},{9,13},{13,1},{2,6},{6,10},{... | collective-permute-start | bytes 61448 | tf_op jit(solution)/shard_map/ppermute | solution.py:678
  83.7 1.7 %collective-permute-start.15 = (bf16[40,256]{1,0:T(8,128)(2,1)S(1)}, bf16[40,256]{1,0:T(8,128)(2,1)S(1)}, u32[]{:S(2)}, u32[]{:S(2)}) collective-permute-start(bf16[40,256]{1,0:T(8,128)(2,1)S(1)} %shard_map.136.refs_1_), channel_id=1, source_target_pairs={{0,8},{4,12},{8,0},{12,4},{1,9},{5,13},{9,1},{13,5},{2,10},{6,14},... | collective-permute-start | bytes 61448 | tf_op jit(solution)/shard_map/ppermute | solution.py:678
  85.4 0.7 collective-permute-start.16
  86.1 0.5 collective-permute-done.14.refs_2_
  86.6 1.8 %collective-permute-done.15.refs_3_ = bf16[40,256]{1,0:T(8,128)(2,1)S(1)} collective-permute-done((bf16[40,256]{1,0:T(8,128)(2,1)S(1)}, bf16[40,256]{1,0:T(8,128)(2,1)S(1)}, u32[]{:S(2)}, u32[]{:S(2)}) %collective-permute-start.15) | collective-permute-done | bytes 20512 | tf_op jit(solution)/shard_map/ppermute | solution.py:678
  88.4 1.0 %collective-permute-done.16.refs_4_ = bf16[40,256]{1,0:T(8,128)(2,1)S(1)} collective-permute-done((bf16[40,256]{1,0:T(8,128)(2,1)S(1)}, bf16[40,256]{1,0:T(8,128)(2,1)S(1)}, u32[]{:S(2)}, u32[]{:S(2)}) %collective-permute-start.16) | collective-permute-done | bytes 20512 | tf_op jit(solution)/shard_map/ppermute | solution.py:678
  89.4 1.5 %shard_map.137 = bf16[8,80,256]{2,1,0:T(8,128)(2,1)} custom-call(s32[3]{0:T(128)S(1)} %pad_add_fusion.place_ref, bf16[4,32,768]{2,1,0:T(8,128)(2,1)S(1)} %shard_map.135.refs_0_, bf16[40,256]{1,0:T(8,128)(2,1)S(1)} %shard_map.136.refs_1_, bf16[40,256]{1,0:T(8,128)(2,1)S(1)} %collective-permute-done.14.refs_2_, ...), custom_call_target="tpu_custom_call" | custom-call | flops 200000000 | tf_op jit(solution)/shard_map/pallas_call | solution.py:664
  91.0 3.4 %all-to-all-start.1 = ((bf16[8,80,256]{2,1,0:T(8,128)(2,1)}), bf16[8,80,256]{2,1,0:T(8,128)(2,1)S(1)}, u32[]{:S(2)}, u32[]{:S(2)}) async-start(bf16[8,80,256]{2,1,0:T(8,128)(2,1)} %shard_map.137), calls=%async_computation.1 | async-start | bytes 655360 | tf_op jit(solution)/shard_map/all_to_all | solution.py:933
  94.4 0.5 shard_map.141
  94.9 0.8 shard_map.138
  95.7 1.0 shard_map.142
  96.6 5.3 %all-to-all-done.1.parts_ref = bf16[8,80,256]{2,1,0:T(8,128)(2,1)S(1)} async-done(((bf16[8,80,256]{2,1,0:T(8,128)(2,1)}), bf16[8,80,256]{2,1,0:T(8,128)(2,1)S(1)}, u32[]{:S(2)}, u32[]{:S(2)}) %all-to-all-start.1) | async-done | bytes 327712 | tf_op jit(solution)/shard_map/all_to_all | solution.py:933
  101.9 0.7 shard_map.143
  (26 shorter events, 0.2 us)
Async XLA Ops:
  0.6 7.4 %collective-permute-start.1 = (bf16[32,2560]{1,0:T(8,128)(2,1)}, bf16[32,2560]{1,0:T(8,128)(2,1)S(1)}, u32[]{:S(2)}, u32[]{:S(2)}) collective-permute-start(bf16[32,2560]{1,0:T(8,128)(2,1)} %bitcast.14), channel_id=1, source_target_pairs={{0,2},{1,3},{2,0},{3,1},{4,6},{5,7},{6,4},{7,5},{8,10},{9,11},{10,... | collective-permute-start | bytes 491528 | tf_op jit(solution)/shard_map/ppermute | solution.py:689
  3.7 8.0 %collective-permute-start = (bf16[32,2560]{1,0:T(8,128)(2,1)}, bf16[32,2560]{1,0:T(8,128)(2,1)S(1)}, u32[]{:S(2)}, u32[]{:S(2)}) collective-permute-start(bf16[32,2560]{1,0:T(8,128)(2,1)} %bitcast.15), channel_id=1, source_target_pairs={{0,1},{1,0},{2,3},{3,2},{4,5},{5,4},{6,7},{7,6},{8,9},{9,8},{10,11... | collective-permute-start | bytes 491528 | tf_op jit(solution)/shard_map/ppermute | solution.py:689
  8.1 3.6 %collective-permute-start.2 = (bf16[32,2560]{1,0:T(8,128)(2,1)S(1)}, bf16[32,2560]{1,0:T(8,128)(2,1)S(1)}, u32[]{:S(2)}, u32[]{:S(2)}) collective-permute-start(bf16[32,2560]{1,0:T(8,128)(2,1)S(1)} %collective-permute-done.1.refs_2_), channel_id=1, source_target_pairs={{0,1},{1,0},{2,3},{3,2},{4,5},{5,4},{6,7},{7,6},{8,9},{9,8},{10,11... | collective-permute-start | bytes 491528 | tf_op jit(solution)/shard_map/ppermute | solution.py:689
  11.6 6.8 %copy-start = (bf16[1,128,640]{2,1,0:T(8,128)(2,1)S(1)}, bf16[1,128,640]{2,1,0:T(8,128)(2,1)}, u32[]{:S(2)}) copy-start(bf16[1,128,640]{2,1,0:T(8,128)(2,1)} %param.19) | copy-start | bytes 491524
  11.6 6.8 %copy-start.1 = (f32[4,640]{1,0:T(4,128)S(1)}, f32[4,640]{1,0:T(4,128)}, u32[]{:S(2)}) copy-start(f32[4,640]{1,0:T(4,128)} %refs_10_.1) | copy-start | bytes 30724
  11.7 6.8 %copy-start.2 = (f32[4,256]{1,0:T(4,128)S(1)}, f32[4,256]{1,0:T(4,128)}, u32[]{:S(2)}) copy-start(f32[4,256]{1,0:T(4,128)} %refs_11_.1) | copy-start | bytes 12292
  13.2 5.3 %collective-permute-start.3 = (bf16[16,896]{1,0:T(8,128)(2,1)S(1)}, bf16[16,896]{1,0:T(8,128)(2,1)S(1)}, u32[]{:S(2)}, u32[]{:S(2)}) collective-permute-start(bf16[16,896]{1,0:T(8,128)(2,1)S(1)} %get-tuple-element.53), channel_id=1, source_target_pairs={{0,4},{4,8},{8,12},{1,5},{5,9},{9,13},{2,6},{6,10},{10,14},{3,7},{... | collective-permute-start | bytes 86024 | tf_op jit(solution)/shard_map/ppermute | solution.py:782
  20.1 9.8 %collective-permute-start.4 = (bf16[136,640]{1,0:T(8,128)(2,1)S(1)}, bf16[136,640]{1,0:T(8,128)(2,1)S(1)}, u32[]{:S(2)}, u32[]{:S(2)}) collective-permute-start(bf16[136,640]{1,0:T(8,128)(2,1)S(1)} %get-tuple-element.56), channel_id=1, source_target_pairs={{0,4},{4,8},{8,12},{12,0},{1,5},{5,9},{9,13},{13,1},{2,6},{6,10},{... | collective-permute-start | bytes 522248 | tf_op jit(solution)/shard_map/ppermute | solution.py:803
  22.5 14.6 %collective-permute-start.5 = (bf16[136,640]{1,0:T(8,128)(2,1)S(1)}, bf16[136,640]{1,0:T(8,128)(2,1)S(1)}, u32[]{:S(2)}, u32[]{:S(2)}) collective-permute-start(bf16[136,640]{1,0:T(8,128)(2,1)S(1)} %get-tuple-element.57), channel_id=1, source_target_pairs={{0,8},{4,12},{8,0},{12,4},{1,9},{5,13},{9,1},{13,5},{2,10},{6,14},... | collective-permute-start | bytes 522248 | tf_op jit(solution)/shard_map/ppermute | solution.py:803
  25.1 12.0 %collective-permute-start.6 = (bf16[136,640]{1,0:T(8,128)(2,1)S(1)}, bf16[136,640]{1,0:T(8,128)(2,1)S(1)}, u32[]{:S(2)}, u32[]{:S(2)}) collective-permute-start(bf16[136,640]{1,0:T(8,128)(2,1)S(1)} %get-tuple-element.58), channel_id=1, source_target_pairs={{0,12},{4,0},{8,4},{12,8},{1,13},{5,1},{9,5},{13,9},{2,14},{6,2},{... | collective-permute-start | bytes 522248 | tf_op jit(solution)/shard_map/ppermute | solution.py:803
  26.4 14.4 %collective-permute-start.8 = (bf16[32,768]{1,0:T(8,128)(2,1)S(1)}, bf16[32,768]{1,0:T(8,128)(2,1)S(1)}, u32[]{:S(2)}, u32[]{:S(2)}) collective-permute-start(bf16[32,768]{1,0:T(8,128)(2,1)S(1)} %get-tuple-element.74), channel_id=1, source_target_pairs={{0,4},{4,8},{8,12},{12,0},{1,5},{5,9},{9,13},{13,1},{2,6},{6,10},{... | collective-permute-start | bytes 147464 | tf_op jit(solution)/shard_map/ppermute | solution.py:765
  27.1 15.8 %collective-permute-start.9 = (bf16[32,768]{1,0:T(8,128)(2,1)S(1)}, bf16[32,768]{1,0:T(8,128)(2,1)S(1)}, u32[]{:S(2)}, u32[]{:S(2)}) collective-permute-start(bf16[32,768]{1,0:T(8,128)(2,1)S(1)} %get-tuple-element.75), channel_id=1, source_target_pairs={{0,8},{4,12},{8,0},{12,4},{1,9},{5,13},{9,1},{13,5},{2,10},{6,14},... | collective-permute-start | bytes 147464 | tf_op jit(solution)/shard_map/ppermute | solution.py:765
  29.9 13.0 %collective-permute-start.10 = (bf16[32,768]{1,0:T(8,128)(2,1)S(1)}, bf16[32,768]{1,0:T(8,128)(2,1)S(1)}, u32[]{:S(2)}, u32[]{:S(2)}) collective-permute-start(bf16[32,768]{1,0:T(8,128)(2,1)S(1)} %get-tuple-element.76), channel_id=1, source_target_pairs={{0,12},{4,0},{8,4},{12,8},{1,13},{5,1},{9,5},{13,9},{2,14},{6,2},{... | collective-permute-start | bytes 147464 | tf_op jit(solution)/shard_map/ppermute | solution.py:765
  39.5 9.1 %collective-permute-start.7 = (f32[8,896]{1,0:T(8,128)S(1)}, f32[8,896]{1,0:T(8,128)S(1)}, u32[]{:S(2)}, u32[]{:S(2)}) collective-permute-start(f32[8,896]{1,0:T(8,128)S(1)} %get-tuple-element.68), channel_id=1, source_target_pairs={{4,0},{8,4},{12,8},{5,1},{9,5},{13,9},{6,2},{10,6},{14,10},{7,3},{... | collective-permute-start | bytes 86024 | tf_op jit(solution)/shard_map/ppermute | solution.py:882
  42.9 16.5 %collective-permute-start.17 = (bf16[4,32,768]{2,1,0:T(8,128)(2,1)S(1)}, bf16[4,32,768]{2,1,0:T(8,128)(2,1)S(1)}, u32[]{:S(2)}, u32[]{:S(2)}) collective-permute-start(bf16[4,32,768]{2,1,0:T(8,128)(2,1)S(1)} %shard_map.135.refs_0_), channel_id=1, source_target_pairs={{0,1},{1,2},{2,3},{3,0},{4,5},{5,6},{6,7},{7,4},{8,9},{9,10},{10,1... | collective-permute-start | bytes 589832 | tf_op jit(solution)/shard_map/ppermute | solution.py:678
  51.3 39.7 %all-to-all-start = ((bf16[4,32,2560]{2,1,0:T(8,128)(2,1)}), bf16[4,32,2560]{2,1,0:T(8,128)(2,1)S(1)}, u32[]{:S(2)}, u32[]{:S(2)}) async-start(bf16[4,32,2560]{2,1,0:T(8,128)(2,1)} %shard_map.134), calls=%async_computation | async-start | bytes 1310720 | tf_op jit(solution)/shard_map/all_to_all | solution.py:899
  54.7 14.4 %collective-permute-start.18 = (bf16[4,32,768]{2,1,0:T(8,128)(2,1)S(1)}, bf16[4,32,768]{2,1,0:T(8,128)(2,1)S(1)}, u32[]{:S(2)}, u32[]{:S(2)}) collective-permute-start(bf16[4,32,768]{2,1,0:T(8,128)(2,1)S(1)} %shard_map.135.refs_0_), channel_id=1, source_target_pairs={{0,2},{1,3},{2,0},{3,1},{4,6},{5,7},{6,4},{7,5},{8,10},{9,11},{10,... | collective-permute-start | bytes 589832 | tf_op jit(solution)/shard_map/ppermute | solution.py:678
  56.7 12.4 %collective-permute-start.19 = (bf16[4,32,768]{2,1,0:T(8,128)(2,1)S(1)}, bf16[4,32,768]{2,1,0:T(8,128)(2,1)S(1)}, u32[]{:S(2)}, u32[]{:S(2)}) collective-permute-start(bf16[4,32,768]{2,1,0:T(8,128)(2,1)S(1)} %shard_map.135.refs_0_), channel_id=1, source_target_pairs={{0,3},{1,0},{2,1},{3,2},{4,7},{5,4},{6,5},{7,6},{8,11},{9,8},{10,9... | collective-permute-start | bytes 589832 | tf_op jit(solution)/shard_map/ppermute | solution.py:678
  56.7 13.3 %collective-permute-start.20 = (bf16[136,640]{1,0:T(8,128)(2,1)S(1)}, bf16[136,640]{1,0:T(8,128)(2,1)S(1)}, u32[]{:S(2)}, u32[]{:S(2)}) collective-permute-start(bf16[136,640]{1,0:T(8,128)(2,1)S(1)} %get-tuple-element.67.pair_ref.refs_1_), channel_id=1, source_target_pairs={{0,4},{4,8},{8,12},{12,0},{1,5},{5,9},{9,13},{13,1},{2,6},{6,10},{... | collective-permute-start | bytes 522248 | tf_op jit(solution)/shard_map/ppermute | solution.py:678
  58.8 14.2 %collective-permute-start.21 = (bf16[136,640]{1,0:T(8,128)(2,1)S(1)}, bf16[136,640]{1,0:T(8,128)(2,1)S(1)}, u32[]{:S(2)}, u32[]{:S(2)}) collective-permute-start(bf16[136,640]{1,0:T(8,128)(2,1)S(1)} %get-tuple-element.67.pair_ref.refs_1_), channel_id=1, source_target_pairs={{0,8},{4,12},{8,0},{12,4},{1,9},{5,13},{9,1},{13,5},{2,10},{6,14},... | collective-permute-start | bytes 522248 | tf_op jit(solution)/shard_map/ppermute | solution.py:678
  59.4 13.5 %collective-permute-start.22 = (bf16[136,640]{1,0:T(8,128)(2,1)S(1)}, bf16[136,640]{1,0:T(8,128)(2,1)S(1)}, u32[]{:S(2)}, u32[]{:S(2)}) collective-permute-start(bf16[136,640]{1,0:T(8,128)(2,1)S(1)} %get-tuple-element.67.pair_ref.refs_1_), channel_id=1, source_target_pairs={{0,12},{4,0},{8,4},{12,8},{1,13},{5,1},{9,5},{13,9},{2,14},{6,2},{... | collective-permute-start | bytes 522248 | tf_op jit(solution)/shard_map/ppermute | solution.py:678
  74.0 21.7 %collective-permute-start.23 = (bf16[336,640]{1,0:T(8,128)(2,1)S(1)}, bf16[336,640]{1,0:T(8,128)(2,1)S(1)}, u32[]{:S(2)}, u32[]{:S(2)}) collective-permute-start(bf16[336,640]{1,0:T(8,128)(2,1)S(1)} %get-tuple-element.86), channel_id=1, source_target_pairs={{0,16},{16,0},{1,17},{17,1},{2,18},{18,2},{3,19},{19,3},{4,20},{20... | collective-permute-start | bytes 1290248 | tf_op jit(solution)/shard_map/ppermute | solution.py:914
  75.6 3.2 %collective-permute-start.11 = (bf16[40,256]{1,0:T(8,128)(2,1)S(1)}, bf16[40,256]{1,0:T(8,128)(2,1)S(1)}, u32[]{:S(2)}, u32[]{:S(2)}) collective-permute-start(bf16[40,256]{1,0:T(8,128)(2,1)S(1)} %get-tuple-element.78), channel_id=1, source_target_pairs={{0,1},{1,2},{2,3},{3,0},{4,5},{5,6},{6,7},{7,4},{8,9},{9,10},{10,1... | collective-permute-start | bytes 61448 | tf_op jit(solution)/shard_map/ppermute | solution.py:885
  75.6 3.8 %collective-permute-start.12 = (bf16[40,256]{1,0:T(8,128)(2,1)S(1)}, bf16[40,256]{1,0:T(8,128)(2,1)S(1)}, u32[]{:S(2)}, u32[]{:S(2)}) collective-permute-start(bf16[40,256]{1,0:T(8,128)(2,1)S(1)} %get-tuple-element.79), channel_id=1, source_target_pairs={{0,2},{1,3},{2,0},{3,1},{4,6},{5,7},{6,4},{7,5},{8,10},{9,11},{10,... | collective-permute-start | bytes 61448 | tf_op jit(solution)/shard_map/ppermute | solution.py:885
  75.7 3.7 %collective-permute-start.13 = (bf16[40,256]{1,0:T(8,128)(2,1)S(1)}, bf16[40,256]{1,0:T(8,128)(2,1)S(1)}, u32[]{:S(2)}, u32[]{:S(2)}) collective-permute-start(bf16[40,256]{1,0:T(8,128)(2,1)S(1)} %get-tuple-element.80), channel_id=1, source_target_pairs={{0,3},{1,0},{2,1},{3,2},{4,7},{5,4},{6,5},{7,6},{8,11},{9,8},{10,9... | collective-permute-start | bytes 61448 | tf_op jit(solution)/shard_map/ppermute | solution.py:885
  79.4 7.2 %collective-permute-start.14 = (bf16[40,256]{1,0:T(8,128)(2,1)S(1)}, bf16[40,256]{1,0:T(8,128)(2,1)S(1)}, u32[]{:S(2)}, u32[]{:S(2)}) collective-permute-start(bf16[40,256]{1,0:T(8,128)(2,1)S(1)} %shard_map.136.refs_1_), channel_id=1, source_target_pairs={{0,4},{4,8},{8,12},{12,0},{1,5},{5,9},{9,13},{13,1},{2,6},{6,10},{... | collective-permute-start | bytes 61448 | tf_op jit(solution)/shard_map/ppermute | solution.py:678
  83.7 4.7 %collective-permute-start.15 = (bf16[40,256]{1,0:T(8,128)(2,1)S(1)}, bf16[40,256]{1,0:T(8,128)(2,1)S(1)}, u32[]{:S(2)}, u32[]{:S(2)}) collective-permute-start(bf16[40,256]{1,0:T(8,128)(2,1)S(1)} %shard_map.136.refs_1_), channel_id=1, source_target_pairs={{0,8},{4,12},{8,0},{12,4},{1,9},{5,13},{9,1},{13,5},{2,10},{6,14},... | collective-permute-start | bytes 61448 | tf_op jit(solution)/shard_map/ppermute | solution.py:678
  85.4 4.0 %collective-permute-start.16 = (bf16[40,256]{1,0:T(8,128)(2,1)S(1)}, bf16[40,256]{1,0:T(8,128)(2,1)S(1)}, u32[]{:S(2)}, u32[]{:S(2)}) collective-permute-start(bf16[40,256]{1,0:T(8,128)(2,1)S(1)} %shard_map.136.refs_1_), channel_id=1, source_target_pairs={{0,12},{4,0},{8,4},{12,8},{1,13},{5,1},{9,5},{13,9},{2,14},{6,2},{... | collective-permute-start | bytes 61448 | tf_op jit(solution)/shard_map/ppermute | solution.py:678
  91.0 11.0 %all-to-all-start.1 = ((bf16[8,80,256]{2,1,0:T(8,128)(2,1)}), bf16[8,80,256]{2,1,0:T(8,128)(2,1)S(1)}, u32[]{:S(2)}, u32[]{:S(2)}) async-start(bf16[8,80,256]{2,1,0:T(8,128)(2,1)} %shard_map.137), calls=%async_computation.1 | async-start | bytes 655360 | tf_op jit(solution)/shard_map/all_to_all | solution.py:933

commit v3 on v2

--- a/solution.py
+++ b/solution.py
@@ -41,6 +41,14 @@
     lefts = jnp.concatenate([left_high, left_low, left_high], axis=left_dim)
     rights = jnp.concatenate([right_high, right_high, right_low], axis=right_dim)
     return dot(lefts, rights, left_dim, right_dim)
+
+
+def half_fine(left, right, left_dim=1, right_dim=0):
+    high = left.astype(BF16)
+    low = (left - high.astype(F32)).astype(BF16)
+    rounded = right.astype(BF16)
+    lefts = jnp.concatenate([high, low], axis=left_dim)
+    return dot(lefts, jnp.concatenate([rounded, rounded], axis=right_dim), left_dim, right_dim)
 
 
 def masked_sum(mask, values, values_dim=0):
@@ -166,13 +174,6 @@
     return copies
 
 
-def add_parts(parts_ref, out_ref):
-    total = parts_ref[0].astype(F32)
-    for part in range(1, parts_ref.shape[0]):
-        total = total + parts_ref[part].astype(F32)
-    out_ref[...] = total.astype(out_ref.dtype)
-
-
 def pack(*refs):
     for number, ref in enumerate(refs[:-1]):
         refs[-1][number] = ref[...]
@@ -247,8 +248,8 @@
     tail = spread(jnp.exp(last - decay) * step, heads)
     lead = spread(jnp.exp(decay), heads)
     upstream = upstream_ref[...].astype(F32)
-    forward = fine(mixer_act[:, :state].T, tail * inner_act).astype(BF16)
-    backward = fine(mixer_act[:, state:].T, lead * upstream).astype(BF16)
+    forward = half_fine(mixer_act[:, :state].T, tail * inner_act).astype(BF16)
+    backward = half_fine(mixer_act[:, state:].T, lead * upstream).astype(BF16)
     high, middle, low = pieces(last)
     kinds = (high.astype(F32), middle.astype(F32), low.astype(F32))
     index = lax.broadcasted_iota(jnp.int32, (PAD, LANES), 0)
@@ -282,6 +283,8 @@
     mixer_grad_ref,
     row_ref,
     column_ref,
+    lead_ref,
+    tail_ref,
     inner_near_ref,
     mixer_near_ref,
     sems,
@@ -304,6 +307,8 @@
     heads = head_map(width, head_dim)
     skip = spread(head_ref[...], heads)[2:3]
     step_wide = spread(step, heads)
+    lead_ref[...] = spread(jnp.exp(decay), heads)
+    tail_ref[...] = spread(jnp.exp(decay[length - 1 : length] - decay) * step, heads)
     group_heads = LANES // head_dim
     lane = lax.broadcasted_iota(jnp.int32, (length, LANES), 1)
     mixed = jnp.zeros((length, length), F32)
@@ -373,6 +378,8 @@
         mixer_grad_ref,
         row_ref,
         column_ref,
+        lead_ref,
+        tail_ref,
         pair_ref,
         mixer_out_ref,
         step_out_ref,
@@ -434,13 +441,13 @@
     last = decay[length - 1 : length]
     lead = jnp.exp(decay)
     rest = jnp.exp(last - decay)
-    lead_wide = spread(lead, heads)
-    tail_wide = spread(rest * step, heads)
-    from_end = fine(input_mix, end)
-    from_start = fine(output_mix, start)
+    lead_wide = lead_ref[...]
+    tail_wide = tail_ref[...]
+    from_end = half_fine(input_mix, end)
+    from_start = half_fine(output_mix, start)
     inner_grad = inner_grad_ref[...] + tail_wide * from_end
-    input_grad = mixer_grad_ref[:, :state] + fine(tail_wide * inner_act, end, 1, 1)
-    output_grad = mixer_grad_ref[:, state:] + fine(lead_wide * upstream, start, 1, 1)
+    input_grad = mixer_grad_ref[:, :state] + half_fine(tail_wide * inner_act, end, 1, 1)
+    output_grad = mixer_grad_ref[:, state:] + half_fine(lead_wide * upstream, start, 1, 1)
     end_part = rest * collect(inner_act * from_end, heads)
     start_part = lead * collect(upstream * from_start, heads)
     product = jnp.sum(end * start, axis=0, keepdims=True)
@@ -492,43 +499,69 @@
 
 
 def project_back(
+    chan_count,
+    place_ref,
     pair_ref,
-    late_ref,
+    early_ref,
     mixer_ref,
     step_ref,
     inner_weight_ref,
     mixer_weight_ref,
     step_weight_ref,
-    out_ref,
-    inner_scratch,
-    mixer_scratch,
+    *refs,
 ):
-    count, rows, _ = out_ref.shape
-    length, _ = mixer_ref.shape
+    out_refs = refs[:chan_count]
+    inner_scratch, mixer_scratch, share_scratch = refs[chan_count:]
+    length, mixed = mixer_ref.shape
     width = pair_ref.shape[1]
-    head = length - PAD
+    rows = length // chan_count
     whole = width // (2 * LANES) * (2 * LANES)
-
-    late = late_ref[...]
-    inner_scratch[:head, :width] = pair_ref[:head]
-    ending = pair_ref[head:length].astype(F32) + late[:, :width]
-    inner_scratch[head:, :width] = ending.astype(BF16)
-    inner_scratch[:, width:] = step_ref[...]
-    mixer_scratch[:head] = mixer_ref[:head]
-    ending = mixer_ref[head:].astype(F32) + late[:, width:]
-    mixer_scratch[head:] = ending.astype(BF16)
+    fill = jnp.zeros((PAD, width + mixed), F32)
+    early = jnp.concatenate([early_ref[...], fill], axis=0).astype(BF16)
+    inner_scratch[:length, :width] = pair_ref[:length]
+    inner_scratch[:length, width:] = step_ref[...]
+    inner_scratch[length:, :width] = early[:, :width]
+    inner_scratch[length:, width:] = jnp.zeros((2 * PAD, LANES), BF16)
+    mixer_scratch[:length] = mixer_ref[...]
+    mixer_scratch[length:] = early[:, width:]
     share = dot(inner_scratch[:, :whole], inner_weight_ref[:, :whole], 1, 1)
     right = jnp.concatenate([inner_weight_ref[:, whole:], step_weight_ref[...]], axis=1)
     share = share + dot(inner_scratch[:, whole:], right, 1, 1)
     share = share + dot(mixer_scratch[...], mixer_weight_ref[...], 1, 1)
-    share = share.astype(BF16)
-    for target in range(count):
-        span = slice(target * rows, (target + 1) * rows)
-        out_ref[target] = share[span]
+    share_scratch[...] = share.astype(BF16)
+    for hop, out_ref in enumerate(out_refs):
+        target = lax.rem(place_ref[2] + hop, chan_count)
+        start = pl.multiple_of(target * rows, rows)
+        out_ref[:rows] = share_scratch[pl.ds(start, rows)]
+        out_ref[rows:] = share_scratch[length : length + PAD]
+
+
+def gather_share(*refs):
+    total_ref, ending_ref, back_ref = refs[-3:]
+    total = refs[0][...].astype(F32)
+    for part in refs[1:-3]:
+        total = total + part[...].astype(F32)
+    rows = total_ref.shape[0]
+    total_ref[...] = total[:rows].astype(BF16)
+    ending_ref[...] = total[rows - PAD : rows]
+    back_ref[...] = total[rows:].astype(BF16)
+
+
+def close_share(
+    taps, chan_count, place_ref, total_ref, ending_ref, late_ref, out_ref, scratch, done
+):
+    del total_ref
+    valid = place_ref[2] == chan_count - 1
+    ending = add_late(ending_ref[...], late_ref[...].astype(F32), taps, valid)
+    scratch[...] = ending.astype(BF16)
+    head = out_ref.shape[0] - PAD
+    copy = pltpu.make_async_copy(scratch, out_ref.at[pl.ds(head, PAD)], done)
+    copy.start()
+    copy.wait()
 
 
 def turn(place_ref, *refs):
-    column_refs, out_ref, columns = refs[:-2], refs[-2], refs[-1]
+    column_refs, out_ref, own_ref, columns = refs[:-3], refs[-3], refs[-2], refs[-1]
     chan_place = place_ref[2]
     chan_count = len(column_refs)
     seq_count, rows, _ = column_refs[0].shape
@@ -539,6 +572,8 @@
             start = pl.multiple_of(hop * length + chan_source * rows, rows)
             columns[pl.ds(start, rows)] = column_refs[chan_hop][hop]
     out_ref[...] = columns[...].T
+    own = [column_refs[0][hop] for hop in range(seq_count)]
+    own_ref[...] = jnp.concatenate(own, axis=0).T
 
 
 def arrange(relative, taps, used, place_ref, pair_refs, grads, steps):
@@ -601,14 +636,15 @@
         step_out_ref[head : head + 1] = step[line : line + 1]
 
 
-def mix(relative, taps, rows, scale, place_ref, *refs):
-    column_ref, out_ref, columns, grads = refs[0], refs[-3], refs[-2], refs[-1]
-    grad_refs = refs[1:-3]
+def mix(relative, taps, rows, scale, chan_count, place_ref, *refs):
+    column_ref, scratch, grads = refs[0], refs[-2], refs[-1]
+    grad_refs = refs[1 : -2 - chan_count]
+    out_refs = refs[-2 - chan_count : -2]
     seq_place = place_ref[0]
-    dp_place = place_ref[1]
     chan_place = place_ref[2]
-    seq_count, tokens, wide = column_ref.shape
-    chan_count = out_ref.shape[0] // 2
+    wide = column_ref.shape[0]
+    seq_count = len(grad_refs) if relative else grad_refs[0].shape[0]
+    tokens = grads.shape[0] // seq_count
 
     def message(hop):
         return grad_refs[hop][...] if relative else grad_refs[0][hop]
@@ -622,7 +658,6 @@
             after = (hop + 1) % seq_count
         start = hop * tokens
         head = tokens - PAD
-        columns[start : start + tokens] = column_ref[hop]
         block = message(hop)
         grads[start : start + head] = block[:head]
         valid = (source < seq_count - 1) & (chan_place == chan_count - 1)
@@ -630,12 +665,27 @@
         ending = add_late(block[head:tokens].astype(F32), extra, taps, valid)
         grads[start + head : start + tokens] = ending.astype(BF16)
     padded = wide // 2
-    term = (dot(columns[...], grads[...], 0, 0) * scale).astype(BF16)
-    for hop in range(2):
-        target = lax.rem(dp_place + hop, 2)
-        for chan in range(chan_count):
-            start = hop * padded + chan * rows
-            out_ref[target * chan_count + chan] = term[start : start + rows]
+    scratch[...] = dot(column_ref[...], grads[...]) * scale
+    for hop, out_ref in enumerate(out_refs):
+        target = lax.rem(chan_place + hop, chan_count)
+        for dp_hop in range(2):
+            start = pl.multiple_of(dp_hop * padded + target * rows, PAD)
+            part = scratch[pl.ds(start, rows)]
+            out_ref[dp_hop * rows : (dp_hop + 1) * rows] = part.astype(BF16)
+
+
+def add_chan(*refs):
+    kept_ref, leaving_ref = refs[-2:]
+    total = refs[0][...].astype(F32)
+    for part in refs[1:-2]:
+        total = total + part[...].astype(F32)
+    rows = kept_ref.shape[0]
+    kept_ref[...] = total[:rows]
+    leaving_ref[...] = total[rows:].astype(BF16)
+
+
+def add_pair(kept_ref, arrived_ref, out_ref):
+    out_ref[...] = kept_ref[...] + arrived_ref[...].astype(F32)
 
 
 def shape(*dims, dtype=F32):
@@ -647,7 +697,7 @@
     return [(source, (source + hop) % count) for source in range(count)]
 
 
-def call(body, place, arrays, out_shape, scratch=(), cost=3, plain=(), left=()):
+def call(body, place, arrays, out_shape, scratch=(), cost=3, plain=(), left=(), in_place=False):
     vmem = pltpu.MemorySpace.VMEM
     hbm = pltpu.MemorySpace.HBM
     arrays = [
@@ -657,7 +707,7 @@
     in_specs = [
         pl.BlockSpec(memory_space=hbm if number in left else vmem) for number in range(len(arrays))
     ]
-    out_specs = [pl.BlockSpec(memory_space=vmem)] * len(out_shape)
+    out_specs = [pl.BlockSpec(memory_space=hbm if in_place else vmem)] * len(out_shape)
     if place is not None:
         in_specs = [pl.BlockSpec(memory_space=pltpu.SMEM)] + in_specs
         arrays = [place] + arrays
@@ -667,6 +717,7 @@
         in_specs=in_specs,
         out_specs=out_specs,
         scratch_shapes=list(scratch),
+        input_output_aliases={1: 0} if in_place else {},
         cost_estimate=pl.CostEstimate(flops=cost * 10**8, bytes_accessed=0, transcendentals=0),
         compiler_params=pltpu.CompilerParams(vmem_limit_bytes=24 * 2**20),
     )(*arrays)
@@ -718,7 +769,7 @@
     state = mixed // 2
     upstream = output_grad[0]
     grad_rows = model // (dp_count * seq_count)
-    padded = -(-grad_rows // LANES) * LANES
+    padded = -(-grad_rows // (2 * PAD)) * (2 * PAD)
     taps = conv_inner.shape[0] - 1
     parts = next(count for count in (4, 2, 1) if model % (count * LANES) == 0)
     places = [place, lax.axis_index("dp"), lax.axis_index("chan")]
@@ -805,7 +856,7 @@
         ]
     else:
         received = [lax.all_to_all(messages[0], "seq", split_axis=0, concat_axis=0)]
-    inner_part, mixer_part, row_part, column_part, inner_back, mixer_back = call(
+    *inside, inner_back, mixer_back = call(
         functools.partial(within, head_dim),
         None,
         [
@@ -823,6 +874,8 @@
             shape(length, mixed),
             shape(length, LANES),
             shape(LANES, length),
+            shape(length, width),
+            shape(length, width),
             shape(model, width, dtype=BF16),
             shape(model, mixed, dtype=BF16),
         ],
@@ -835,11 +888,14 @@
             pack, None, columns, [shape(seq_count, rows, dp_count * padded, dtype=BF16)], cost=1
         )
     all_columns = around(columns, "chan")
-    (turned,) = call(
+    turned, own_turned = call(
         turn,
         places,
         all_columns,
-        [shape(dp_count * padded, seq_count * length, dtype=BF16)],
+        [
+            shape(dp_count * padded, seq_count * length, dtype=BF16),
+            shape(dp_count * padded, seq_count * rows, dtype=BF16),
+        ],
         [pltpu.VMEM((seq_count * length, dp_count * padded), BF16)],
     )
 
@@ -847,21 +903,8 @@
         functools.partial(finish, head_dim, relative, seq_count, chan_count),
         places,
         received
-        + [
-            inner_pre,
-            mixer_pre,
-            step,
-            decay,
-            step_raw,
-            head_rows,
-            upstream,
-            conv_inner,
-            conv_mixer,
-            inner_part,
-            mixer_part,
-            row_part,
-            column_part,
-        ],
+        + [inner_pre, mixer_pre, step, decay, step_raw, head_rows, upstream, conv_inner, conv_mixer]
+        + list(inside),
         [
             shape(length + PAD, width, dtype=BF16),
             shape(length, mixed, dtype=BF16),
@@ -878,8 +921,6 @@
             return around(block, "seq")
         return [lax.all_gather(block, "seq")]
 
-    backward_pairs = [(source + 1, source) for source in range(seq_count - 1)]
-    late = lax.ppermute(early, "seq", backward_pairs)
     pairs = over_seq(pair)
     mixer_rows = list(mixer_sent[:1]) + [
         lax.ppermute(block, "chan", ring("chan", hop))
@@ -888,15 +929,22 @@
     (mixer_rows,) = call(add_up, None, mixer_rows, [shape(rows + PAD, mixed, dtype=BF16)], cost=1)
     mixers = over_seq(mixer_rows)
 
-    (sent,) = call(
-        project_back,
-        None,
-        [pair, late, mixer_local, step_grad, inner_back, mixer_back, step_near],
-        [shape(chan_count, rows, model, dtype=BF16)],
-        [pltpu.VMEM((length, width + LANES), BF16), pltpu.VMEM((length, mixed), BF16)],
+    sent = call(
+        functools.partial(project_back, chan_count),
+        places,
+        [pair, early, mixer_local, step_grad, inner_back, mixer_back, step_near],
+        [shape(rows + PAD, model, dtype=BF16)] * chan_count,
+        [
+            pltpu.VMEM((length + 2 * PAD, width + LANES), BF16),
+            pltpu.VMEM((length + 2 * PAD, mixed), BF16),
+            pltpu.VMEM((length + 2 * PAD, model), BF16),
+        ],
         cost=4,
     )
-    taken = lax.all_to_all(sent, "chan", split_axis=0, concat_axis=0)
+    taken = list(sent[:1]) + [
+        lax.ppermute(block, "chan", ring("chan", hop))
+        for hop, block in enumerate(sent[1:], 1)
+    ]
 
     groups = width // length
     used = -(-head_count // groups)
@@ -918,26 +966,56 @@
         [turned, grads, steps],
         [shape(grad_rows, width), shape(step_lines, padded)],
     )
-    (mixer_blocks,) = call(
-        functools.partial(mix, relative, taps, grad_rows // chan_count, norm_factor),
+    mixer_blocks = call(
+        functools.partial(mix, relative, taps, grad_rows // chan_count, norm_factor, chan_count),
         places,
-        [columns] + mixers,
-        [shape(dp_count * chan_count, grad_rows // chan_count, mixed, dtype=BF16)],
-        [
-            pltpu.VMEM((seq_count * rows, dp_count * padded), BF16),
-            pltpu.VMEM((seq_count * rows, mixed), BF16),
+        [own_turned] + mixers,
+        [shape(grad_rows // chan_count * dp_count, mixed, dtype=BF16)] * chan_count,
+        [pltpu.VMEM((dp_count * padded, mixed), F32), pltpu.VMEM((seq_count * rows, mixed), BF16)],
+        cost=2,
+    )
+    mixer_blocks = list(mixer_blocks[:1]) + [
+        lax.ppermute(block, "chan", ring("chan", hop))
+        for hop, block in enumerate(mixer_blocks[1:], 1)
+    ]
+    mixer_kept, mixer_leaving = call(
+        add_chan,
+        None,
+        mixer_blocks,
+        [shape(grad_rows // chan_count, mixed), shape(grad_rows // chan_count, mixed, dtype=BF16)],
+        cost=1,
+    )
+    mixer_arrived = lax.ppermute(mixer_leaving, "dp", ring("dp", 1))
+    (mixer_weight_grad,) = call(
+        add_pair,
+        None,
+        [mixer_kept, mixer_arrived],
+        [jax.ShapeDtypeStruct((grad_rows // chan_count, mixed), F32)],
+        cost=1,
+    )
+    total, ending, back = call(
+        gather_share,
+        None,
+        taken,
+        [
+            jax.ShapeDtypeStruct((rows, model), BF16),
+            shape(PAD, model),
+            shape(PAD, model, dtype=BF16),
         ],
-        cost=2,
-    )
-    taken, mixer_blocks = lax.optimization_barrier((taken, mixer_blocks))
-    mixer_blocks = lax.all_to_all(
-        mixer_blocks, ("dp", "chan"), split_axis=0, concat_axis=0
-    )
-    (mixer_weight_grad,) = call(
-        add_parts, None, [mixer_blocks], [jax.ShapeDtypeStruct(mixer_blocks.shape[1:], F32)], cost=1
-    )
+        cost=1,
+    )
+    backward_pairs = [(source + 1, source) for source in range(seq_count - 1)]
+    late = lax.ppermute(back, "seq", backward_pairs)
     (input_grad,) = call(
-        add_parts, None, [taken], [jax.ShapeDtypeStruct((rows, model), BF16)], cost=1
+        functools.partial(close_share, taps, chan_count),
+        places,
+        [total, ending, late],
+        [jax.ShapeDtypeStruct((rows, model), BF16)],
+        [pltpu.VMEM((PAD, model), BF16), pltpu.SemaphoreType.DMA],
+        cost=1,
+        plain=(0,),
+        left=(0,),
+        in_place=True,
     )
     inner_weight_grad, step_weight_grad = call(
         functools.partial(last, used),

time: 103 us -> 109 us (1.058)
  waiting for transfers between devices: 39.3 us -> 46.1 us
    ppermute x3 -> x9, waiting for transfers between devices: 2.04 us -> 13.5 us  [body(): lax.ppermute(block, 'chan', ring('chan', hop))]
    ppermute x3, waiting for transfers between devices: 2.09 us -> 11.8 us  [body(): columns.append(lax.ppermute(block, 'seq', ring('seq', hop)))]
    all_to_all x2 -> x0, starting transfers between devices: 6.92 us -> none  [the longest x1 3.48 us: body(): taken = lax.all_to_all(sent, 'chan', split_axis=0, concat_axis=0)]
    ppermute x3, waiting for transfers between devices: 5.35 us -> 0.01 us  [body(): lax.ppermute(message, 'seq', ring('seq', hop))]
    all_to_all x2 -> x0, waiting for transfers between devices: 5.29 us -> none  [the longest x1 5.29 us: body(): lax.all_to_all(mixer_blocks, ('dp', 'chan'), split_axis=0, concat_axis=0)]
    ppermute x3 -> x9, starting transfers between devices: 1.75 us -> 6.51 us  [body(): lax.ppermute(block, 'chan', ring('chan', hop))]
    ppermute x3, starting transfers between devices: 2.62 us -> 4.97 us  [body(): columns.append(lax.ppermute(block, 'seq', ring('seq', hop)))]
    ppermute x1 -> x2, waiting for transfers between devices: 5.61 us -> 3.9 us  [the longest x1 2.3 us: body(): late = lax.ppermute(back, 'seq', backward_pairs)]
  transfers between devices with their start and end apart: 26 -> 31, of which waited for: 14 -> 12; matrix products, arithmetic and copies ran while one was open for 0% -> 0% of each run, Pallas kernels for 17% -> 15%
where the time goes in v3:
time: 109 us
  waiting for transfers between devices  46.1 us (42%)
  starting transfers between devices  41.5 us (38%)
  Pallas kernels  20.4 us (19%)
    pallas_call x17, Pallas kernels, call(): pl.pallas_call(body, out_shape=out_shape, in_specs=in_specs, out_specs=ou...  20.4 us
    ppermute x9, starting transfers between devices, around(): lax.ppermute(block, axis, ring(axis, hop))  13.6 us
    ppermute x9, waiting for transfers between devices, body(): lax.ppermute(block, 'chan', ring('chan', hop))  13.5 us
    ppermute x9, waiting for transfers between devices, around(): lax.ppermute(block, axis, ring(axis, hop))  12.5 us
    ppermute x3, waiting for transfers between devices, body(): columns.append(lax.ppermute(block, 'seq', ring('seq', hop)))  11.8 us
    ppermute x9, starting transfers between devices, body(): lax.ppermute(block, 'chan', ring('chan', hop))  6.51 us
    ppermute x3, starting transfers between devices, body(): lax.ppermute(message, 'seq', ring('seq', hop))  6.19 us
    ppermute x3, starting transfers between devices, body(): columns.append(lax.ppermute(block, 'seq', ring('seq', hop)))  4.97 us
  transfers between devices with their start and end apart: 31, of which 12 were waited for; matrix products, arithmetic and copies ran while one was open for 0% of the time, Pallas kernels for 15%

profile of v3, /device:TPU:0, one launch (start us, length us, event | category | flops | bytes accessed | tf_op | source)
XLA Modules:
  0.0 108.9 jit_solution(3230234747598669281)
XLA Ops:
  0.6 3.0 %collective-permute-start.1 = (bf16[32,2560]{1,0:T(8,128)(2,1)}, bf16[32,2560]{1,0:T(8,128)(2,1)S(1)}, u32[]{:S(2)}, u32[]{:S(2)}) collective-permute-start(bf16[32,2560]{1,0:T(8,128)(2,1)} %bitcast.14), channel_id=1, source_target_pairs={{0,2},{1,3},{2,0},{3,1},{4,6},{5,7},{6,4},{7,5},{8,10},{9,11},{10,... | collective-permute-start | bytes 491528 | tf_op jit(solution)/shard_map/ppermute | solution.py:740
  3.7 4.4 %collective-permute-done.1.refs_2_ = bf16[32,2560]{1,0:T(8,128)(2,1)S(1)} collective-permute-done((bf16[32,2560]{1,0:T(8,128)(2,1)}, bf16[32,2560]{1,0:T(8,128)(2,1)S(1)}, u32[]{:S(2)}, u32[]{:S(2)}) %collective-permute-start.1) | collective-permute-done | bytes 163872 | tf_op jit(solution)/shard_map/ppermute | solution.py:740
  8.2 3.4 %shard_map.129 = (bf16[32,2560]{1,0:T(8,128)(2,1)S(1)}, bf16[2560,128]{1,0:T(8,128)(2,1)S(1)}, f32[8,128]{1,0:T(8,128)S(1)}, bf16[2560,640]{1,0:T(8,128)(2,1)S(1...) custom-call(s32[3]{0:T(128)S(1)} %pad_add_fusion.place_ref, ...), custom_call_target="tpu_custom_call" | custom-call | flops 100000000 | tf_op jit(solution)/shard_map/pallas_call | solution.py:714
  11.6 1.5 %shard_map.130 = (bf16[128,640]{1,0:T(8,128)(2,1)S(1)}, bf16[128,256]{1,0:T(8,128)(2,1)S(1)}, f32[128,128]{1,0:T(8,128)S(1)}, bf16[16,896]{1,0:T(8,128)(2,1)S(1)}) custom-call(s32[3]{0:T(128)S(1)} %pad_add_fusion.place_ref, bf16[32,2560]{1,0:T(8,128)(2,1)S(1)} %get-tuple-element.62.refs_0_, bf16[32,2560]{1,0:T(8,128)(2,1)S(1)} %collective-permute-done.refs_1_, ...), custom_call_target="tpu_custom_call" | custom-call | flops 400000000 | tf_op jit(solution)/shard_map/pallas_call | solution.py:714
  13.1 3.7 %collective-permute-start.3 = (bf16[16,896]{1,0:T(8,128)(2,1)S(1)}, bf16[16,896]{1,0:T(8,128)(2,1)S(1)}, u32[]{:S(2)}, u32[]{:S(2)}) collective-permute-start(bf16[16,896]{1,0:T(8,128)(2,1)S(1)} %get-tuple-element.68), channel_id=1, source_target_pairs={{0,4},{4,8},{8,12},{1,5},{5,9},{9,13},{2,6},{6,10},{10,14},{3,7},{... | collective-permute-start | bytes 86024 | tf_op jit(solution)/shard_map/ppermute | solution.py:833
  16.8 1.6 %collective-permute-start.11 = (bf16[32,640]{1,0:T(8,128)(2,1)S(1)}, bf16[32,640]{1,0:T(8,128)(2,1)S(1)}, u32[]{:S(2)}, u32[]{:S(2)}) collective-permute-start(bf16[32,640]{1,0:T(8,128)(2,1)S(1)} %get-tuple-element.98), channel_id=1, source_target_pairs={{0,4},{4,8},{8,12},{12,0},{1,5},{5,9},{9,13},{13,1},{2,6},{6,10},{... | collective-permute-start | bytes 122888 | tf_op jit(solution)/shard_map/ppermute | solution.py:816
  18.5 1.6 %shard_map.131 = (f32[128,640]{1,0:T(8,128)S(1)}, f32[128,256]{1,0:T(8,128)S(1)}, f32[128,128]{1,0:T(8,128)S(1)}, f32[128,128]{1,0:T(8,128)S(1)}, bf16[136,640]{...) custom-call(s32[3]{0:T(128)S(1)} %pad_add_fusion.place_ref, ...), custom_call_target="tpu_custom_call" | custom-call | flops 300000000 | tf_op jit(solution)/shard_map/pallas_call | solution.py:714
  20.0 2.3 %collective-permute-start.4 = (bf16[136,640]{1,0:T(8,128)(2,1)S(1)}, bf16[136,640]{1,0:T(8,128)(2,1)S(1)}, u32[]{:S(2)}, u32[]{:S(2)}) collective-permute-start(bf16[136,640]{1,0:T(8,128)(2,1)S(1)} %get-tuple-element.71), channel_id=1, source_target_pairs={{0,4},{4,8},{8,12},{12,0},{1,5},{5,9},{9,13},{13,1},{2,6},{6,10},{... | collective-permute-start | bytes 522248 | tf_op jit(solution)/shard_map/ppermute | solution.py:854
  22.3 2.9 %collective-permute-start.5 = (bf16[136,640]{1,0:T(8,128)(2,1)S(1)}, bf16[136,640]{1,0:T(8,128)(2,1)S(1)}, u32[]{:S(2)}, u32[]{:S(2)}) collective-permute-start(bf16[136,640]{1,0:T(8,128)(2,1)S(1)} %get-tuple-element.72), channel_id=1, source_target_pairs={{0,8},{4,12},{8,0},{12,4},{1,9},{5,13},{9,1},{13,5},{2,10},{6,14},... | collective-permute-start | bytes 522248 | tf_op jit(solution)/shard_map/ppermute | solution.py:854
  25.2 1.0 collective-permute-start.6
  26.2 0.5 collective-permute-start.12
  26.7 2.8 %collective-permute-start.13 = (bf16[32,640]{1,0:T(8,128)(2,1)S(1)}, bf16[32,640]{1,0:T(8,128)(2,1)S(1)}, u32[]{:S(2)}, u32[]{:S(2)}) collective-permute-start(bf16[32,640]{1,0:T(8,128)(2,1)S(1)} %get-tuple-element.100), channel_id=1, source_target_pairs={{0,12},{4,0},{8,4},{12,8},{1,13},{5,1},{9,5},{13,9},{2,14},{6,2},{... | collective-permute-start | bytes 122888 | tf_op jit(solution)/shard_map/ppermute | solution.py:816
  29.6 11.7 %collective-permute-done.12.refs_2_ = bf16[32,640]{1,0:T(8,128)(2,1)S(1)} collective-permute-done((bf16[32,640]{1,0:T(8,128)(2,1)S(1)}, bf16[32,640]{1,0:T(8,128)(2,1)S(1)}, u32[]{:S(2)}, u32[]{:S(2)}) %collective-permute-start.12) | collective-permute-done | bytes 40992 | tf_op jit(solution)/shard_map/ppermute | solution.py:816
  41.4 1.5 %collective-permute-start.15 = (bf16[4,32,640]{2,1,0:T(8,128)(2,1)S(1)}, bf16[4,32,640]{2,1,0:T(8,128)(2,1)S(1)}, u32[]{:S(2)}, u32[]{:S(2)}) collective-permute-start(bf16[4,32,640]{2,1,0:T(8,128)(2,1)S(1)} %shard_map.137.refs_0_), channel_id=1, source_target_pairs={{0,2},{1,3},{2,0},{3,1},{4,6},{5,7},{6,4},{7,5},{8,10},{9,11},{10,... | collective-permute-start | bytes 491528 | tf_op jit(solution)/shard_map/ppermute | solution.py:729
  42.9 2.5 %shard_map.132 = (f32[128,640]{1,0:T(8,128)S(1)}, f32[128,256]{1,0:T(8,128)S(1)}, f32[128,128]{1,0:T(8,128)S(1)}, f32[128,128]{1,0:T(8,128)S(1)}, f32[128,640]{1...) custom-call(f32[128,640]{1,0:T(8,128)S(1)} %get-tuple-element.74.inner_pre_ref, ...), custom_call_target="tpu_custom_call" | custom-call | flops 300000000 | tf_op jit(solution)/shard_map/pallas_call | solution.py:714
  45.5 1.4 %collective-permute-start.16 = (bf16[4,32,640]{2,1,0:T(8,128)(2,1)S(1)}, bf16[4,32,640]{2,1,0:T(8,128)(2,1)S(1)}, u32[]{:S(2)}, u32[]{:S(2)}) collective-permute-start(bf16[4,32,640]{2,1,0:T(8,128)(2,1)S(1)} %shard_map.137.refs_0_), channel_id=1, source_target_pairs={{0,3},{1,0},{2,1},{3,2},{4,7},{5,4},{6,5},{7,6},{8,11},{9,8},{10,9... | collective-permute-start | bytes 491528 | tf_op jit(solution)/shard_map/ppermute | solution.py:729
  46.9 2.2 %shard_map.133 = (bf16[136,640]{1,0:T(8,128)(2,1)S(1)}, bf16[128,256]{1,0:T(8,128)(2,1)S(1)}, bf16[128,128]{1,0:T(8,128)(2,1)S(1)}, f32[8,896]{1,0:T(8,128)S(1)}...) custom-call(s32[3]{0:T(128)S(1)} %pad_add_fusion.place_ref, ...), custom_call_target="tpu_custom_call" | custom-call | flops 500000000 | tf_op jit(solution)/shard_map/pallas_call | solution.py:714
  49.1 1.4 %collective-permute-start.17 = (bf16[136,640]{1,0:T(8,128)(2,1)S(1)}, bf16[136,640]{1,0:T(8,128)(2,1)S(1)}, u32[]{:S(2)}, u32[]{:S(2)}) collective-permute-start(bf16[136,640]{1,0:T(8,128)(2,1)S(1)} %get-tuple-element.84.pair_ref.refs_1_), channel_id=1, source_target_pairs={{0,4},{4,8},{8,12},{12,0},{1,5},{5,9},{9,13},{13,1},{2,6},{6,10},{... | collective-permute-start | bytes 522248 | tf_op jit(solution)/shard_map/ppermute | solution.py:729
  50.5 1.6 %collective-permute-start.18 = (bf16[136,640]{1,0:T(8,128)(2,1)S(1)}, bf16[136,640]{1,0:T(8,128)(2,1)S(1)}, u32[]{:S(2)}, u32[]{:S(2)}) collective-permute-start(bf16[136,640]{1,0:T(8,128)(2,1)S(1)} %get-tuple-element.84.pair_ref.refs_1_), channel_id=1, source_target_pairs={{0,8},{4,12},{8,0},{12,4},{1,9},{5,13},{9,1},{13,5},{2,10},{6,14},... | collective-permute-start | bytes 522248 | tf_op jit(solution)/shard_map/ppermute | solution.py:729
  52.1 0.9 collective-permute-start.19
  53.0 0.9 shard_map.138
  53.9 4.4 %collective-permute-done.17.refs_2_ = bf16[136,640]{1,0:T(8,128)(2,1)S(1)} collective-permute-done((bf16[136,640]{1,0:T(8,128)(2,1)S(1)}, bf16[136,640]{1,0:T(8,128)(2,1)S(1)}, u32[]{:S(2)}, u32[]{:S(2)}) %collective-permute-start.17) | collective-permute-done | bytes 174112 | tf_op jit(solution)/shard_map/ppermute | solution.py:729
  58.3 5.6 %collective-permute-done.18.refs_3_ = bf16[136,640]{1,0:T(8,128)(2,1)S(1)} collective-permute-done((bf16[136,640]{1,0:T(8,128)(2,1)S(1)}, bf16[136,640]{1,0:T(8,128)(2,1)S(1)}, u32[]{:S(2)}, u32[]{:S(2)}) %collective-permute-start.18) | collective-permute-done | bytes 174112 | tf_op jit(solution)/shard_map/ppermute | solution.py:729
  63.9 1.0 shard_map.139
  65.0 1.6 %collective-permute-start.20 = (bf16[336,640]{1,0:T(8,128)(2,1)S(1)}, bf16[336,640]{1,0:T(8,128)(2,1)S(1)}, u32[]{:S(2)}, u32[]{:S(2)}) collective-permute-start(bf16[336,640]{1,0:T(8,128)(2,1)S(1)} %get-tuple-element.106), channel_id=1, source_target_pairs={{0,16},{16,0},{1,17},{17,1},{2,18},{18,2},{3,19},{19,3},{4,20},{20... | collective-permute-start | bytes 1290248 | tf_op jit(solution)/shard_map/ppermute | solution.py:962
  66.6 1.4 %collective-permute-start.22 = (bf16[40,256]{1,0:T(8,128)(2,1)S(1)}, bf16[40,256]{1,0:T(8,128)(2,1)S(1)}, u32[]{:S(2)}, u32[]{:S(2)}) collective-permute-start(bf16[40,256]{1,0:T(8,128)(2,1)S(1)} %get-tuple-element.111), channel_id=1, source_target_pairs={{0,2},{1,3},{2,0},{3,1},{4,6},{5,7},{6,4},{7,5},{8,10},{9,11},{10,... | collective-permute-start | bytes 61448 | tf_op jit(solution)/shard_map/ppermute | solution.py:926
  67.9 1.5 %collective-permute-start.23 = (bf16[40,256]{1,0:T(8,128)(2,1)S(1)}, bf16[40,256]{1,0:T(8,128)(2,1)S(1)}, u32[]{:S(2)}, u32[]{:S(2)}) collective-permute-start(bf16[40,256]{1,0:T(8,128)(2,1)S(1)} %get-tuple-element.112), channel_id=1, source_target_pairs={{0,3},{1,0},{2,1},{3,2},{4,7},{5,4},{6,5},{7,6},{8,11},{9,8},{10,9... | collective-permute-start | bytes 61448 | tf_op jit(solution)/shard_map/ppermute | solution.py:926
  69.8 0.6 collective-permute-done.22.refs_2_
  70.3 0.5 collective-permute-done.23.refs_3_
  70.9 4.2 %collective-permute-start.24 = (bf16[40,256]{1,0:T(8,128)(2,1)S(1)}, bf16[40,256]{1,0:T(8,128)(2,1)S(1)}, u32[]{:S(2)}, u32[]{:S(2)}) collective-permute-start(bf16[40,256]{1,0:T(8,128)(2,1)S(1)} %shard_map.142.refs_1_), channel_id=1, source_target_pairs={{0,4},{4,8},{8,12},{12,0},{1,5},{5,9},{9,13},{13,1},{2,6},{6,10},{... | collective-permute-start | bytes 61448 | tf_op jit(solution)/shard_map/ppermute | solution.py:729
  75.3 2.3 %collective-permute-start.26 = (bf16[40,256]{1,0:T(8,128)(2,1)S(1)}, bf16[40,256]{1,0:T(8,128)(2,1)S(1)}, u32[]{:S(2)}, u32[]{:S(2)}) collective-permute-start(bf16[40,256]{1,0:T(8,128)(2,1)S(1)} %shard_map.142.refs_1_), channel_id=1, source_target_pairs={{0,12},{4,0},{8,4},{12,8},{1,13},{5,1},{9,5},{13,9},{2,14},{6,2},{... | collective-permute-start | bytes 61448 | tf_op jit(solution)/shard_map/ppermute | solution.py:729
  77.6 2.5 %collective-permute-done.25.refs_3_ = bf16[40,256]{1,0:T(8,128)(2,1)S(1)} collective-permute-done((bf16[40,256]{1,0:T(8,128)(2,1)S(1)}, bf16[40,256]{1,0:T(8,128)(2,1)S(1)}, u32[]{:S(2)}, u32[]{:S(2)}) %collective-permute-start.25) | collective-permute-done | bytes 20512 | tf_op jit(solution)/shard_map/ppermute | solution.py:729
  80.0 0.8 shard_map.143
  81.0 2.4 %shard_map.134 = (bf16[40,2560]{1,0:T(8,128)(2,1)S(1)}, bf16[40,2560]{1,0:T(8,128)(2,1)S(1)}, bf16[40,2560]{1,0:T(8,128)(2,1)S(1)}, bf16[40,2560]{1,0:T(8,128)(2,1)S(1)}) custom-call(s32[3]{0:T(128)S(1)} %pad_add_fusion.place_ref, bf16[136,640]{1,0:T(8,128)(2,1)S(1)} %get-tuple-element.84.pair_ref.refs_1_, f32[8,896]{1,0:T(8,128)S(1)} %get-tuple-element.85.early_ref, ...), custom_call_target="tpu_custom_call" | custom-call | flops 400000000 | tf_op jit(solution)/shard_map/pallas_call | solution.py:714
  83.4 1.0 collective-permute-start.7
  84.4 1.1 %collective-permute-start.8 = (bf16[40,2560]{1,0:T(8,128)(2,1)S(1)}, bf16[40,2560]{1,0:T(8,128)(2,1)S(1)}, u32[]{:S(2)}, u32[]{:S(2)}) collective-permute-start(bf16[40,2560]{1,0:T(8,128)(2,1)S(1)} %get-tuple-element.92), channel_id=1, source_target_pairs={{0,2},{1,3},{2,0},{3,1},{4,6},{5,7},{6,4},{7,5},{8,10},{9,11},{10,... | collective-permute-start | bytes 614408 | tf_op jit(solution)/shard_map/ppermute | solution.py:945
  86.0 1.0 collective-permute-start.28
  87.0 10.0 %collective-permute-done.28.refs_2_ = bf16[160,256]{1,0:T(8,128)(2,1)S(1)} collective-permute-done((bf16[160,256]{1,0:T(8,128)(2,1)S(1)}, bf16[160,256]{1,0:T(8,128)(2,1)S(1)}, u32[]{:S(2)}, u32[]{:S(2)}) %collective-permute-start.28) | collective-permute-done | bytes 81952 | tf_op jit(solution)/shard_map/ppermute | solution.py:978
  96.9 2.1 %collective-permute-done.29.refs_3_ = bf16[160,256]{1,0:T(8,128)(2,1)S(1)} collective-permute-done((bf16[160,256]{1,0:T(8,128)(2,1)S(1)}, bf16[160,256]{1,0:T(8,128)(2,1)S(1)}, u32[]{:S(2)}, u32[]{:S(2)}) %collective-permute-start.29) | collective-permute-done | bytes 81952 | tf_op jit(solution)/shard_map/ppermute | solution.py:978
  99.1 0.6 collective-permute-start.30
  99.6 0.8 shard_map.135
  100.4 1.3 %collective-permute-start.10 = (bf16[8,2560]{1,0:T(8,128)(2,1)S(1)}, bf16[8,2560]{1,0:T(8,128)(2,1)S(1)}, u32[]{:S(2)}, u32[]{:S(2)}) collective-permute-start(bf16[8,2560]{1,0:T(8,128)(2,1)S(1)} %get-tuple-element.96), channel_id=1, source_target_pairs={{4,0},{8,4},{12,8},{5,1},{9,5},{13,9},{6,2},{10,6},{14,10},{7,3},{... | collective-permute-start | bytes 122888 | tf_op jit(solution)/shard_map/ppermute | solution.py:1008
  101.7 1.6 %collective-permute-done.30.arrived_ref = bf16[80,256]{1,0:T(8,128)(2,1)S(1)} collective-permute-done((bf16[80,256]{1,0:T(8,128)(2,1)S(1)}, bf16[80,256]{1,0:T(8,128)(2,1)S(1)}, u32[]{:S(2)}, u32[]{:S(2)}) %collective-permute-start.30) | collective-permute-done | bytes 40992 | tf_op jit(solution)/shard_map/ppermute | solution.py:988
  103.3 0.6 shard_map.145
  103.9 0.5 shard_map.140
  104.4 2.3 %collective-permute-done.10.late_ref = bf16[8,2560]{1,0:T(8,128)(2,1)S(1)} collective-permute-done((bf16[8,2560]{1,0:T(8,128)(2,1)S(1)}, bf16[8,2560]{1,0:T(8,128)(2,1)S(1)}, u32[]{:S(2)}, u32[]{:S(2)}) %collective-permute-start.10) | collective-permute-done | bytes 40992 | tf_op jit(solution)/shard_map/ppermute | solution.py:1008
  106.7 1.2 %shard_map.136 = bf16[32,2560]{1,0:T(8,128)(2,1)} custom-call(s32[3]{0:T(128)S(1)} %pad_add_fusion.place_ref, bf16[32,2560]{1,0:T(8,128)(2,1)} %get-tuple-element.94.total_ref, f32[8,2560]{1,0:T(8,128)S(1)} %get-tuple-element.95.ending_ref, bf16[8,2560]{1,0:T(8,128)(2,1)S(1)} %collective-permute-done.10.late_ref), custom_call_target="tpu_custom_call", output_to_operand_aliasing={{}: (1, {})} | custom-call | flops 100000000 | tf_op jit(solution)/shard_map/pallas_call | solution.py:714
  107.9 1.0 shard_map.141
  (38 shorter events, 1.3 us)
Async XLA Ops:
  0.6 7.4 %collective-permute-start.1 = (bf16[32,2560]{1,0:T(8,128)(2,1)}, bf16[32,2560]{1,0:T(8,128)(2,1)S(1)}, u32[]{:S(2)}, u32[]{:S(2)}) collective-permute-start(bf16[32,2560]{1,0:T(8,128)(2,1)} %bitcast.14), channel_id=1, source_target_pairs={{0,2},{1,3},{2,0},{3,1},{4,6},{5,7},{6,4},{7,5},{8,10},{9,11},{10,... | collective-permute-start | bytes 491528 | tf_op jit(solution)/shard_map/ppermute | solution.py:740
  3.7 7.9 %collective-permute-start = (bf16[32,2560]{1,0:T(8,128)(2,1)}, bf16[32,2560]{1,0:T(8,128)(2,1)S(1)}, u32[]{:S(2)}, u32[]{:S(2)}) collective-permute-start(bf16[32,2560]{1,0:T(8,128)(2,1)} %bitcast.15), channel_id=1, source_target_pairs={{0,1},{1,0},{2,3},{3,2},{4,5},{5,4},{6,7},{7,6},{8,9},{9,8},{10,11... | collective-permute-start | bytes 491528 | tf_op jit(solution)/shard_map/ppermute | solution.py:740
  8.1 3.5 %collective-permute-start.2 = (bf16[32,2560]{1,0:T(8,128)(2,1)S(1)}, bf16[32,2560]{1,0:T(8,128)(2,1)S(1)}, u32[]{:S(2)}, u32[]{:S(2)}) collective-permute-start(bf16[32,2560]{1,0:T(8,128)(2,1)S(1)} %collective-permute-done.1.refs_2_), channel_id=1, source_target_pairs={{0,1},{1,0},{2,3},{3,2},{4,5},{5,4},{6,7},{7,6},{8,9},{9,8},{10,11... | collective-permute-start | bytes 491528 | tf_op jit(solution)/shard_map/ppermute | solution.py:740
  11.5 6.9 %copy-start = (bf16[1,128,640]{2,1,0:T(8,128)(2,1)S(1)}, bf16[1,128,640]{2,1,0:T(8,128)(2,1)}, u32[]{:S(2)}) copy-start(bf16[1,128,640]{2,1,0:T(8,128)(2,1)} %param.19) | copy-start | bytes 491524
  11.5 6.9 %copy-start.1 = (f32[4,640]{1,0:T(4,128)S(1)}, f32[4,640]{1,0:T(4,128)}, u32[]{:S(2)}) copy-start(f32[4,640]{1,0:T(4,128)} %refs_10_.1) | copy-start | bytes 30724
  11.6 6.9 %copy-start.2 = (f32[4,256]{1,0:T(4,128)S(1)}, f32[4,256]{1,0:T(4,128)}, u32[]{:S(2)}) copy-start(f32[4,256]{1,0:T(4,128)} %refs_11_.1) | copy-start | bytes 12292
  13.1 5.4 %collective-permute-start.3 = (bf16[16,896]{1,0:T(8,128)(2,1)S(1)}, bf16[16,896]{1,0:T(8,128)(2,1)S(1)}, u32[]{:S(2)}, u32[]{:S(2)}) collective-permute-start(bf16[16,896]{1,0:T(8,128)(2,1)S(1)} %get-tuple-element.68), channel_id=1, source_target_pairs={{0,4},{4,8},{8,12},{1,5},{5,9},{9,13},{2,6},{6,10},{10,14},{3,7},{... | collective-permute-start | bytes 86024 | tf_op jit(solution)/shard_map/ppermute | solution.py:833
  16.8 9.9 %collective-permute-start.11 = (bf16[32,640]{1,0:T(8,128)(2,1)S(1)}, bf16[32,640]{1,0:T(8,128)(2,1)S(1)}, u32[]{:S(2)}, u32[]{:S(2)}) collective-permute-start(bf16[32,640]{1,0:T(8,128)(2,1)S(1)} %get-tuple-element.98), channel_id=1, source_target_pairs={{0,4},{4,8},{8,12},{12,0},{1,5},{5,9},{9,13},{13,1},{2,6},{6,10},{... | collective-permute-start | bytes 122888 | tf_op jit(solution)/shard_map/ppermute | solution.py:816
  20.0 25.5 %collective-permute-start.4 = (bf16[136,640]{1,0:T(8,128)(2,1)S(1)}, bf16[136,640]{1,0:T(8,128)(2,1)S(1)}, u32[]{:S(2)}, u32[]{:S(2)}) collective-permute-start(bf16[136,640]{1,0:T(8,128)(2,1)S(1)} %get-tuple-element.71), channel_id=1, source_target_pairs={{0,4},{4,8},{8,12},{12,0},{1,5},{5,9},{9,13},{13,1},{2,6},{6,10},{... | collective-permute-start | bytes 522248 | tf_op jit(solution)/shard_map/ppermute | solution.py:854
  22.3 24.7 %collective-permute-start.5 = (bf16[136,640]{1,0:T(8,128)(2,1)S(1)}, bf16[136,640]{1,0:T(8,128)(2,1)S(1)}, u32[]{:S(2)}, u32[]{:S(2)}) collective-permute-start(bf16[136,640]{1,0:T(8,128)(2,1)S(1)} %get-tuple-element.72), channel_id=1, source_target_pairs={{0,8},{4,12},{8,0},{12,4},{1,9},{5,13},{9,1},{13,5},{2,10},{6,14},... | collective-permute-start | bytes 522248 | tf_op jit(solution)/shard_map/ppermute | solution.py:854
  25.2 21.8 %collective-permute-start.6 = (bf16[136,640]{1,0:T(8,128)(2,1)S(1)}, bf16[136,640]{1,0:T(8,128)(2,1)S(1)}, u32[]{:S(2)}, u32[]{:S(2)}) collective-permute-start(bf16[136,640]{1,0:T(8,128)(2,1)S(1)} %get-tuple-element.73), channel_id=1, source_target_pairs={{0,12},{4,0},{8,4},{12,8},{1,13},{5,1},{9,5},{13,9},{2,14},{6,2},{... | collective-permute-start | bytes 522248 | tf_op jit(solution)/shard_map/ppermute | solution.py:854
  26.2 15.1 %collective-permute-start.12 = (bf16[32,640]{1,0:T(8,128)(2,1)S(1)}, bf16[32,640]{1,0:T(8,128)(2,1)S(1)}, u32[]{:S(2)}, u32[]{:S(2)}) collective-permute-start(bf16[32,640]{1,0:T(8,128)(2,1)S(1)} %get-tuple-element.99), channel_id=1, source_target_pairs={{0,8},{4,12},{8,0},{12,4},{1,9},{5,13},{9,1},{13,5},{2,10},{6,14},... | collective-permute-start | bytes 122888 | tf_op jit(solution)/shard_map/ppermute | solution.py:816
  26.7 14.6 %collective-permute-start.13 = (bf16[32,640]{1,0:T(8,128)(2,1)S(1)}, bf16[32,640]{1,0:T(8,128)(2,1)S(1)}, u32[]{:S(2)}, u32[]{:S(2)}) collective-permute-start(bf16[32,640]{1,0:T(8,128)(2,1)S(1)} %get-tuple-element.100), channel_id=1, source_target_pairs={{0,12},{4,0},{8,4},{12,8},{1,13},{5,1},{9,5},{13,9},{2,14},{6,2},{... | collective-permute-start | bytes 122888 | tf_op jit(solution)/shard_map/ppermute | solution.py:816
  41.3 10.8 %collective-permute-start.14 = (bf16[4,32,640]{2,1,0:T(8,128)(2,1)S(1)}, bf16[4,32,640]{2,1,0:T(8,128)(2,1)S(1)}, u32[]{:S(2)}, u32[]{:S(2)}) collective-permute-start(bf16[4,32,640]{2,1,0:T(8,128)(2,1)S(1)} %shard_map.137.refs_0_), channel_id=1, source_target_pairs={{0,1},{1,2},{2,3},{3,0},{4,5},{5,6},{6,7},{7,4},{8,9},{9,10},{10,1... | collective-permute-start | bytes 491528 | tf_op jit(solution)/shard_map/ppermute | solution.py:729
  41.4 11.6 %collective-permute-start.15 = (bf16[4,32,640]{2,1,0:T(8,128)(2,1)S(1)}, bf16[4,32,640]{2,1,0:T(8,128)(2,1)S(1)}, u32[]{:S(2)}, u32[]{:S(2)}) collective-permute-start(bf16[4,32,640]{2,1,0:T(8,128)(2,1)S(1)} %shard_map.137.refs_0_), channel_id=1, source_target_pairs={{0,2},{1,3},{2,0},{3,1},{4,6},{5,7},{6,4},{7,5},{8,10},{9,11},{10,... | collective-permute-start | bytes 491528 | tf_op jit(solution)/shard_map/ppermute | solution.py:729
  45.5 7.5 %collective-permute-start.16 = (bf16[4,32,640]{2,1,0:T(8,128)(2,1)S(1)}, bf16[4,32,640]{2,1,0:T(8,128)(2,1)S(1)}, u32[]{:S(2)}, u32[]{:S(2)}) collective-permute-start(bf16[4,32,640]{2,1,0:T(8,128)(2,1)S(1)} %shard_map.137.refs_0_), channel_id=1, source_target_pairs={{0,3},{1,0},{2,1},{3,2},{4,7},{5,4},{6,5},{7,6},{8,11},{9,8},{10,9... | collective-permute-start | bytes 491528 | tf_op jit(solution)/shard_map/ppermute | solution.py:729
  49.1 9.2 %collective-permute-start.17 = (bf16[136,640]{1,0:T(8,128)(2,1)S(1)}, bf16[136,640]{1,0:T(8,128)(2,1)S(1)}, u32[]{:S(2)}, u32[]{:S(2)}) collective-permute-start(bf16[136,640]{1,0:T(8,128)(2,1)S(1)} %get-tuple-element.84.pair_ref.refs_1_), channel_id=1, source_target_pairs={{0,4},{4,8},{8,12},{12,0},{1,5},{5,9},{9,13},{13,1},{2,6},{6,10},{... | collective-permute-start | bytes 522248 | tf_op jit(solution)/shard_map/ppermute | solution.py:729
  50.5 13.5 %collective-permute-start.18 = (bf16[136,640]{1,0:T(8,128)(2,1)S(1)}, bf16[136,640]{1,0:T(8,128)(2,1)S(1)}, u32[]{:S(2)}, u32[]{:S(2)}) collective-permute-start(bf16[136,640]{1,0:T(8,128)(2,1)S(1)} %get-tuple-element.84.pair_ref.refs_1_), channel_id=1, source_target_pairs={{0,8},{4,12},{8,0},{12,4},{1,9},{5,13},{9,1},{13,5},{2,10},{6,14},... | collective-permute-start | bytes 522248 | tf_op jit(solution)/shard_map/ppermute | solution.py:729
  52.1 11.8 %collective-permute-start.19 = (bf16[136,640]{1,0:T(8,128)(2,1)S(1)}, bf16[136,640]{1,0:T(8,128)(2,1)S(1)}, u32[]{:S(2)}, u32[]{:S(2)}) collective-permute-start(bf16[136,640]{1,0:T(8,128)(2,1)S(1)} %get-tuple-element.84.pair_ref.refs_1_), channel_id=1, source_target_pairs={{0,12},{4,0},{8,4},{12,8},{1,13},{5,1},{9,5},{13,9},{2,14},{6,2},{... | collective-permute-start | bytes 522248 | tf_op jit(solution)/shard_map/ppermute | solution.py:729
  65.0 42.9 %collective-permute-start.20 = (bf16[336,640]{1,0:T(8,128)(2,1)S(1)}, bf16[336,640]{1,0:T(8,128)(2,1)S(1)}, u32[]{:S(2)}, u32[]{:S(2)}) collective-permute-start(bf16[336,640]{1,0:T(8,128)(2,1)S(1)} %get-tuple-element.106), channel_id=1, source_target_pairs={{0,16},{16,0},{1,17},{17,1},{2,18},{18,2},{3,19},{19,3},{4,20},{20... | collective-permute-start | bytes 1290248 | tf_op jit(solution)/shard_map/ppermute | solution.py:962
  66.6 3.2 %collective-permute-start.21 = (bf16[40,256]{1,0:T(8,128)(2,1)S(1)}, bf16[40,256]{1,0:T(8,128)(2,1)S(1)}, u32[]{:S(2)}, u32[]{:S(2)}) collective-permute-start(bf16[40,256]{1,0:T(8,128)(2,1)S(1)} %get-tuple-element.110), channel_id=1, source_target_pairs={{0,1},{1,2},{2,3},{3,0},{4,5},{5,6},{6,7},{7,4},{8,9},{9,10},{10,1... | collective-permute-start | bytes 61448 | tf_op jit(solution)/shard_map/ppermute | solution.py:926
  66.6 3.8 %collective-permute-start.22 = (bf16[40,256]{1,0:T(8,128)(2,1)S(1)}, bf16[40,256]{1,0:T(8,128)(2,1)S(1)}, u32[]{:S(2)}, u32[]{:S(2)}) collective-permute-start(bf16[40,256]{1,0:T(8,128)(2,1)S(1)} %get-tuple-element.111), channel_id=1, source_target_pairs={{0,2},{1,3},{2,0},{3,1},{4,6},{5,7},{6,4},{7,5},{8,10},{9,11},{10,... | collective-permute-start | bytes 61448 | tf_op jit(solution)/shard_map/ppermute | solution.py:926
  67.9 2.9 %collective-permute-start.23 = (bf16[40,256]{1,0:T(8,128)(2,1)S(1)}, bf16[40,256]{1,0:T(8,128)(2,1)S(1)}, u32[]{:S(2)}, u32[]{:S(2)}) collective-permute-start(bf16[40,256]{1,0:T(8,128)(2,1)S(1)} %get-tuple-element.112), channel_id=1, source_target_pairs={{0,3},{1,0},{2,1},{3,2},{4,7},{5,4},{6,5},{7,6},{8,11},{9,8},{10,9... | collective-permute-start | bytes 61448 | tf_op jit(solution)/shard_map/ppermute | solution.py:926
  70.9 6.7 %collective-permute-start.24 = (bf16[40,256]{1,0:T(8,128)(2,1)S(1)}, bf16[40,256]{1,0:T(8,128)(2,1)S(1)}, u32[]{:S(2)}, u32[]{:S(2)}) collective-permute-start(bf16[40,256]{1,0:T(8,128)(2,1)S(1)} %shard_map.142.refs_1_), channel_id=1, source_target_pairs={{0,4},{4,8},{8,12},{12,0},{1,5},{5,9},{9,13},{13,1},{2,6},{6,10},{... | collective-permute-start | bytes 61448 | tf_op jit(solution)/shard_map/ppermute | solution.py:729
  75.1 4.9 %collective-permute-start.25 = (bf16[40,256]{1,0:T(8,128)(2,1)S(1)}, bf16[40,256]{1,0:T(8,128)(2,1)S(1)}, u32[]{:S(2)}, u32[]{:S(2)}) collective-permute-start(bf16[40,256]{1,0:T(8,128)(2,1)S(1)} %shard_map.142.refs_1_), channel_id=1, source_target_pairs={{0,8},{4,12},{8,0},{12,4},{1,9},{5,13},{9,1},{13,5},{2,10},{6,14},... | collective-permute-start | bytes 61448 | tf_op jit(solution)/shard_map/ppermute | solution.py:729
  75.3 4.8 %collective-permute-start.26 = (bf16[40,256]{1,0:T(8,128)(2,1)S(1)}, bf16[40,256]{1,0:T(8,128)(2,1)S(1)}, u32[]{:S(2)}, u32[]{:S(2)}) collective-permute-start(bf16[40,256]{1,0:T(8,128)(2,1)S(1)} %shard_map.142.refs_1_), channel_id=1, source_target_pairs={{0,12},{4,0},{8,4},{12,8},{1,13},{5,1},{9,5},{13,9},{2,14},{6,2},{... | collective-permute-start | bytes 61448 | tf_op jit(solution)/shard_map/ppermute | solution.py:729
  80.9 5.1 %collective-permute-start.27 = (bf16[160,256]{1,0:T(8,128)(2,1)S(1)}, bf16[160,256]{1,0:T(8,128)(2,1)S(1)}, u32[]{:S(2)}, u32[]{:S(2)}) collective-permute-start(bf16[160,256]{1,0:T(8,128)(2,1)S(1)} %get-tuple-element.114), channel_id=1, source_target_pairs={{0,1},{1,2},{2,3},{3,0},{4,5},{5,6},{6,7},{7,4},{8,9},{9,10},{10,1... | collective-permute-start | bytes 245768 | tf_op jit(solution)/shard_map/ppermute | solution.py:978
  83.4 16.3 %collective-permute-start.7 = (bf16[40,2560]{1,0:T(8,128)(2,1)S(1)}, bf16[40,2560]{1,0:T(8,128)(2,1)S(1)}, u32[]{:S(2)}, u32[]{:S(2)}) collective-permute-start(bf16[40,2560]{1,0:T(8,128)(2,1)S(1)} %get-tuple-element.91), channel_id=1, source_target_pairs={{0,1},{1,2},{2,3},{3,0},{4,5},{5,6},{6,7},{7,4},{8,9},{9,10},{10,1... | collective-permute-start | bytes 614408 | tf_op jit(solution)/shard_map/ppermute | solution.py:945
  84.4 15.2 %collective-permute-start.8 = (bf16[40,2560]{1,0:T(8,128)(2,1)S(1)}, bf16[40,2560]{1,0:T(8,128)(2,1)S(1)}, u32[]{:S(2)}, u32[]{:S(2)}) collective-permute-start(bf16[40,2560]{1,0:T(8,128)(2,1)S(1)} %get-tuple-element.92), channel_id=1, source_target_pairs={{0,2},{1,3},{2,0},{3,1},{4,6},{5,7},{6,4},{7,5},{8,10},{9,11},{10,... | collective-permute-start | bytes 614408 | tf_op jit(solution)/shard_map/ppermute | solution.py:945
  85.6 14.1 %collective-permute-start.9 = (bf16[40,2560]{1,0:T(8,128)(2,1)S(1)}, bf16[40,2560]{1,0:T(8,128)(2,1)S(1)}, u32[]{:S(2)}, u32[]{:S(2)}) collective-permute-start(bf16[40,2560]{1,0:T(8,128)(2,1)S(1)} %get-tuple-element.93), channel_id=1, source_target_pairs={{0,3},{1,0},{2,1},{3,2},{4,7},{5,4},{6,5},{7,6},{8,11},{9,8},{10,9... | collective-permute-start | bytes 614408 | tf_op jit(solution)/shard_map/ppermute | solution.py:945
  86.0 11.0 %collective-permute-start.28 = (bf16[160,256]{1,0:T(8,128)(2,1)S(1)}, bf16[160,256]{1,0:T(8,128)(2,1)S(1)}, u32[]{:S(2)}, u32[]{:S(2)}) collective-permute-start(bf16[160,256]{1,0:T(8,128)(2,1)S(1)} %get-tuple-element.115), channel_id=1, source_target_pairs={{0,2},{1,3},{2,0},{3,1},{4,6},{5,7},{6,4},{7,5},{8,10},{9,11},{10,... | collective-permute-start | bytes 245768 | tf_op jit(solution)/shard_map/ppermute | solution.py:978
  96.9 2.1 %collective-permute-start.29 = (bf16[160,256]{1,0:T(8,128)(2,1)S(1)}, bf16[160,256]{1,0:T(8,128)(2,1)S(1)}, u32[]{:S(2)}, u32[]{:S(2)}) collective-permute-start(bf16[160,256]{1,0:T(8,128)(2,1)S(1)} %get-tuple-element.116), channel_id=1, source_target_pairs={{0,3},{1,0},{2,1},{3,2},{4,7},{5,4},{6,5},{7,6},{8,11},{9,8},{10,9... | collective-permute-start | bytes 245768 | tf_op jit(solution)/shard_map/ppermute | solution.py:978
  99.1 4.2 %collective-permute-start.30 = (bf16[80,256]{1,0:T(8,128)(2,1)S(1)}, bf16[80,256]{1,0:T(8,128)(2,1)S(1)}, u32[]{:S(2)}, u32[]{:S(2)}) collective-permute-start(bf16[80,256]{1,0:T(8,128)(2,1)S(1)} %get-tuple-element.118), channel_id=1, source_target_pairs={{0,16},{16,0},{1,17},{17,1},{2,18},{18,2},{3,19},{19,3},{4,20},{20... | collective-permute-start | bytes 122888 | tf_op jit(solution)/shard_map/ppermute | solution.py:988
  100.4 6.3 %collective-permute-start.10 = (bf16[8,2560]{1,0:T(8,128)(2,1)S(1)}, bf16[8,2560]{1,0:T(8,128)(2,1)S(1)}, u32[]{:S(2)}, u32[]{:S(2)}) collective-permute-start(bf16[8,2560]{1,0:T(8,128)(2,1)S(1)} %get-tuple-element.96), channel_id=1, source_target_pairs={{4,0},{8,4},{12,8},{5,1},{9,5},{13,9},{6,2},{10,6},{14,10},{7,3},{... | collective-permute-start | bytes 122888 | tf_op jit(solution)/shard_map/ppermute | solution.py:1008

commit v4 on v3

--- a/solution.py
+++ b/solution.py
@@ -547,16 +547,42 @@
     back_ref[...] = total[rows:].astype(BF16)
 
 
-def close_share(
-    taps, chan_count, place_ref, total_ref, ending_ref, late_ref, out_ref, scratch, done
+def close(
+    taps,
+    chan_count,
+    used,
+    place_ref,
+    kept_ref,
+    step_ref,
+    arrived_ref,
+    total_ref,
+    ending_ref,
+    late_ref,
+    mixer_kept_ref,
+    mixer_arrived_ref,
+    inner_out_ref,
+    step_out_ref,
+    input_out_ref,
+    mixer_out_ref,
+    scratch,
+    done,
 ):
     del total_ref
     valid = place_ref[2] == chan_count - 1
     ending = add_late(ending_ref[...], late_ref[...].astype(F32), taps, valid)
     scratch[...] = ending.astype(BF16)
-    head = out_ref.shape[0] - PAD
-    copy = pltpu.make_async_copy(scratch, out_ref.at[pl.ds(head, PAD)], done)
+    head = input_out_ref.shape[0] - PAD
+    copy = pltpu.make_async_copy(scratch, input_out_ref.at[pl.ds(head, PAD)], done)
     copy.start()
+    rows = kept_ref.shape[0]
+    inner_out_ref[...] = kept_ref[...] + arrived_ref[:rows].astype(F32)
+    mixer_out_ref[...] = mixer_kept_ref[...] + mixer_arrived_ref[...].astype(F32)
+    step = step_ref[:, :rows] + arrived_ref[rows:, :rows].astype(F32)
+    head_count = step_out_ref.shape[0]
+    groups = -(-head_count // used)
+    for head in range(head_count):
+        line = (head % groups) * used + head // groups
+        step_out_ref[head : head + 1] = step[line : line + 1]
     copy.wait()
 
 
@@ -623,17 +649,6 @@
     padded = turned_ref.shape[0] // 2
     out_ref[...] = dot(turned_ref[:rows], grads_ref[...]) * scale
     step_ref[...] = dot(steps_ref[...], turned_ref[:padded], 1, 1) * scale
-
-
-def last(used, kept_ref, step_ref, arrived_ref, out_ref, step_out_ref):
-    rows, _ = kept_ref.shape
-    out_ref[...] = kept_ref[...] + arrived_ref[:rows].astype(F32)
-    step = step_ref[:, :rows] + arrived_ref[rows:, :rows].astype(F32)
-    head_count = step_out_ref.shape[0]
-    groups = -(-head_count // used)
-    for head in range(head_count):
-        line = (head % groups) * used + head // groups
-        step_out_ref[head : head + 1] = step[line : line + 1]
 
 
 def mix(relative, taps, rows, scale, chan_count, place_ref, *refs):
@@ -684,10 +699,6 @@
     leaving_ref[...] = total[rows:].astype(BF16)
 
 
-def add_pair(kept_ref, arrived_ref, out_ref):
-    out_ref[...] = kept_ref[...] + arrived_ref[...].astype(F32)
-
-
 def shape(*dims, dtype=F32):
     return pltpu.VMEM(dims, dtype)
 
@@ -697,7 +708,7 @@
     return [(source, (source + hop) % count) for source in range(count)]
 
 
-def call(body, place, arrays, out_shape, scratch=(), cost=3, plain=(), left=(), in_place=False):
+def call(body, place, arrays, out_shape, scratch=(), cost=3, plain=(), left=(), in_place=None):
     vmem = pltpu.MemorySpace.VMEM
     hbm = pltpu.MemorySpace.HBM
     arrays = [
@@ -707,7 +718,10 @@
     in_specs = [
         pl.BlockSpec(memory_space=hbm if number in left else vmem) for number in range(len(arrays))
     ]
-    out_specs = [pl.BlockSpec(memory_space=hbm if in_place else vmem)] * len(out_shape)
+    out_specs = [
+        pl.BlockSpec(memory_space=hbm if in_place and in_place[1] == number else vmem)
+        for number in range(len(out_shape))
+    ]
     if place is not None:
         in_specs = [pl.BlockSpec(memory_space=pltpu.SMEM)] + in_specs
         arrays = [place] + arrays
@@ -717,7 +731,7 @@
         in_specs=in_specs,
         out_specs=out_specs,
         scratch_shapes=list(scratch),
-        input_output_aliases={1: 0} if in_place else {},
+        input_output_aliases={in_place[0] + 1: in_place[1]} if in_place else {},
         cost_estimate=pl.CostEstimate(flops=cost * 10**8, bytes_accessed=0, transcendentals=0),
         compiler_params=pltpu.CompilerParams(vmem_limit_bytes=24 * 2**20),
     )(*arrays)
@@ -986,13 +1000,6 @@
         cost=1,
     )
     mixer_arrived = lax.ppermute(mixer_leaving, "dp", ring("dp", 1))
-    (mixer_weight_grad,) = call(
-        add_pair,
-        None,
-        [mixer_kept, mixer_arrived],
-        [jax.ShapeDtypeStruct((grad_rows // chan_count, mixed), F32)],
-        cost=1,
-    )
     total, ending, back = call(
         gather_share,
         None,
@@ -1006,26 +1013,21 @@
     )
     backward_pairs = [(source + 1, source) for source in range(seq_count - 1)]
     late = lax.ppermute(back, "seq", backward_pairs)
-    (input_grad,) = call(
-        functools.partial(close_share, taps, chan_count),
+    inner_weight_grad, step_weight_grad, input_grad, mixer_weight_grad = call(
+        functools.partial(close, taps, chan_count, used),
         places,
-        [total, ending, late],
-        [jax.ShapeDtypeStruct((rows, model), BF16)],
+        [kept, kept_step, arrived, total, ending, late, mixer_kept, mixer_arrived],
+        [
+            jax.ShapeDtypeStruct((grad_rows, width), F32),
+            jax.ShapeDtypeStruct((head_count, grad_rows), F32),
+            jax.ShapeDtypeStruct((rows, model), BF16),
+            jax.ShapeDtypeStruct((grad_rows // chan_count, mixed), F32),
+        ],
         [pltpu.VMEM((PAD, model), BF16), pltpu.SemaphoreType.DMA],
         cost=1,
-        plain=(0,),
-        left=(0,),
-        in_place=True,
-    )
-    inner_weight_grad, step_weight_grad = call(
-        functools.partial(last, used),
-        None,
-        [kept, kept_step, arrived],
-        [
-            jax.ShapeDtypeStruct((grad_rows, width), F32),
-            jax.ShapeDtypeStruct((head_count, grad_rows), F32),
-        ],
-        cost=1,
+        plain=(3,),
+        left=(3,),
+        in_place=(3, 2),
     )
     step_weight_grad = step_weight_grad.T
     return (input_grad[None], inner_weight_grad, mixer_weight_grad, step_weight_grad)

time: 109 us -> 109 us (level)
    ppermute x1, waiting for transfers between devices: 2.3 us -> 3.43 us  [body(): late = lax.ppermute(back, 'seq', backward_pairs)]
    pallas_call x17 -> x15, Pallas kernels: 20.4 us -> 19.6 us  [call(): pl.pallas_call(body, out_shape=out_shape, in_specs=in_specs, out_specs=ou...]
  transfers between devices with their start and end apart: 31 -> 31, of which waited for: 12 -> 12; matrix products, arithmetic and copies ran while one was open for 0% -> 0% of each run, Pallas kernels for 15% -> 14%
where the time goes in v4:
time: 109 us
  waiting for transfers between devices  46.8 us (43%)
  starting transfers between devices  41.5 us (38%)
  Pallas kernels  19.6 us (18%)
    pallas_call x15, Pallas kernels, call(): pl.pallas_call(body, out_shape=out_shape, in_specs=in_specs, out_specs=ou...  19.6 us
    ppermute x9, starting transfers between devices, around(): lax.ppermute(block, axis, ring(axis, hop))  13.6 us
    ppermute x9, waiting for transfers between devices, body(): lax.ppermute(block, 'chan', ring('chan', hop))  13.5 us
    ppermute x9, waiting for transfers between devices, around(): lax.ppermute(block, axis, ring(axis, hop))  12.5 us
    ppermute x3, waiting for transfers between devices, body(): columns.append(lax.ppermute(block, 'seq', ring('seq', hop)))  11.8 us
    ppermute x9, starting transfers between devices, body(): lax.ppermute(block, 'chan', ring('chan', hop))  6.51 us
    ppermute x3, starting transfers between devices, body(): lax.ppermute(message, 'seq', ring('seq', hop))  6.19 us
    ppermute x3, starting transfers between devices, body(): columns.append(lax.ppermute(block, 'seq', ring('seq', hop)))  4.97 us
  transfers between devices with their start and end apart: 31, of which 12 were waited for; matrix products, arithmetic and copies ran while one was open for 0% of the time, Pallas kernels for 14%

profile of v4, /device:TPU:0, one launch (start us, length us, event | category | flops | bytes accessed | tf_op | source)
XLA Modules:
  0.0 108.8 jit_solution(16617900021057743627)
XLA Ops:
  0.6 3.0 %collective-permute-start.7 = (bf16[32,2560]{1,0:T(8,128)(2,1)}, bf16[32,2560]{1,0:T(8,128)(2,1)S(1)}, u32[]{:S(2)}, u32[]{:S(2)}) collective-permute-start(bf16[32,2560]{1,0:T(8,128)(2,1)} %bitcast.14), channel_id=1, source_target_pairs={{0,2},{1,3},{2,0},{3,1},{4,6},{5,7},{6,4},{7,5},{8,10},{9,11},{10,... | collective-permute-start | bytes 491528 | tf_op jit(solution)/shard_map/ppermute | solution.py:754
  3.7 4.4 %collective-permute-done.7.refs_2_ = bf16[32,2560]{1,0:T(8,128)(2,1)S(1)} collective-permute-done((bf16[32,2560]{1,0:T(8,128)(2,1)}, bf16[32,2560]{1,0:T(8,128)(2,1)S(1)}, u32[]{:S(2)}, u32[]{:S(2)}) %collective-permute-start.7) | collective-permute-done | bytes 163872 | tf_op jit(solution)/shard_map/ppermute | solution.py:754
  8.2 3.4 %shard_map.129 = (bf16[32,2560]{1,0:T(8,128)(2,1)S(1)}, bf16[2560,128]{1,0:T(8,128)(2,1)S(1)}, f32[8,128]{1,0:T(8,128)S(1)}, bf16[2560,640]{1,0:T(8,128)(2,1)S(1...) custom-call(s32[3]{0:T(128)S(1)} %pad_add_fusion.place_ref, ...), custom_call_target="tpu_custom_call" | custom-call | flops 100000000 | tf_op jit(solution)/shard_map/pallas_call | solution.py:728
  11.6 1.5 %shard_map.132 = (bf16[128,640]{1,0:T(8,128)(2,1)S(1)}, bf16[128,256]{1,0:T(8,128)(2,1)S(1)}, f32[128,128]{1,0:T(8,128)S(1)}, bf16[16,896]{1,0:T(8,128)(2,1)S(1)}) custom-call(s32[3]{0:T(128)S(1)} %pad_add_fusion.place_ref, bf16[32,2560]{1,0:T(8,128)(2,1)S(1)} %get-tuple-element.69.refs_0_, bf16[32,2560]{1,0:T(8,128)(2,1)S(1)} %collective-permute-done.6.refs_1_, ...), custom_call_target="tpu_custom_call" | custom-call | flops 400000000 | tf_op jit(solution)/shard_map/pallas_call | solution.py:728
  13.1 3.7 %collective-permute-start.9 = (bf16[16,896]{1,0:T(8,128)(2,1)S(1)}, bf16[16,896]{1,0:T(8,128)(2,1)S(1)}, u32[]{:S(2)}, u32[]{:S(2)}) collective-permute-start(bf16[16,896]{1,0:T(8,128)(2,1)S(1)} %get-tuple-element.75), channel_id=1, source_target_pairs={{0,4},{4,8},{8,12},{1,5},{5,9},{9,13},{2,6},{6,10},{10,14},{3,7},{... | collective-permute-start | bytes 86024 | tf_op jit(solution)/shard_map/ppermute | solution.py:847
  16.8 1.6 %collective-permute-start = (bf16[32,640]{1,0:T(8,128)(2,1)S(1)}, bf16[32,640]{1,0:T(8,128)(2,1)S(1)}, u32[]{:S(2)}, u32[]{:S(2)}) collective-permute-start(bf16[32,640]{1,0:T(8,128)(2,1)S(1)} %get-tuple-element.65), channel_id=1, source_target_pairs={{0,4},{4,8},{8,12},{12,0},{1,5},{5,9},{9,13},{13,1},{2,6},{6,10},{... | collective-permute-start | bytes 122888 | tf_op jit(solution)/shard_map/ppermute | solution.py:830
  18.5 1.6 %shard_map.133 = (f32[128,640]{1,0:T(8,128)S(1)}, f32[128,256]{1,0:T(8,128)S(1)}, f32[128,128]{1,0:T(8,128)S(1)}, f32[128,128]{1,0:T(8,128)S(1)}, bf16[136,640]{...) custom-call(s32[3]{0:T(128)S(1)} %pad_add_fusion.place_ref, ...), custom_call_target="tpu_custom_call" | custom-call | flops 300000000 | tf_op jit(solution)/shard_map/pallas_call | solution.py:728
  20.0 2.3 %collective-permute-start.10 = (bf16[136,640]{1,0:T(8,128)(2,1)S(1)}, bf16[136,640]{1,0:T(8,128)(2,1)S(1)}, u32[]{:S(2)}, u32[]{:S(2)}) collective-permute-start(bf16[136,640]{1,0:T(8,128)(2,1)S(1)} %get-tuple-element.78), channel_id=1, source_target_pairs={{0,4},{4,8},{8,12},{12,0},{1,5},{5,9},{9,13},{13,1},{2,6},{6,10},{... | collective-permute-start | bytes 522248 | tf_op jit(solution)/shard_map/ppermute | solution.py:868
  22.3 2.9 %collective-permute-start.11 = (bf16[136,640]{1,0:T(8,128)(2,1)S(1)}, bf16[136,640]{1,0:T(8,128)(2,1)S(1)}, u32[]{:S(2)}, u32[]{:S(2)}) collective-permute-start(bf16[136,640]{1,0:T(8,128)(2,1)S(1)} %get-tuple-element.79), channel_id=1, source_target_pairs={{0,8},{4,12},{8,0},{12,4},{1,9},{5,13},{9,1},{13,5},{2,10},{6,14},... | collective-permute-start | bytes 522248 | tf_op jit(solution)/shard_map/ppermute | solution.py:868
  25.2 1.0 collective-permute-start.12
  26.2 0.5 collective-permute-start.1
  26.7 2.8 %collective-permute-start.2 = (bf16[32,640]{1,0:T(8,128)(2,1)S(1)}, bf16[32,640]{1,0:T(8,128)(2,1)S(1)}, u32[]{:S(2)}, u32[]{:S(2)}) collective-permute-start(bf16[32,640]{1,0:T(8,128)(2,1)S(1)} %get-tuple-element.67), channel_id=1, source_target_pairs={{0,12},{4,0},{8,4},{12,8},{1,13},{5,1},{9,5},{13,9},{2,14},{6,2},{... | collective-permute-start | bytes 122888 | tf_op jit(solution)/shard_map/ppermute | solution.py:830
  29.6 11.7 %collective-permute-done.1.refs_2_ = bf16[32,640]{1,0:T(8,128)(2,1)S(1)} collective-permute-done((bf16[32,640]{1,0:T(8,128)(2,1)S(1)}, bf16[32,640]{1,0:T(8,128)(2,1)S(1)}, u32[]{:S(2)}, u32[]{:S(2)}) %collective-permute-start.1) | collective-permute-done | bytes 40992 | tf_op jit(solution)/shard_map/ppermute | solution.py:830
  41.4 1.5 %collective-permute-start.4 = (bf16[4,32,640]{2,1,0:T(8,128)(2,1)S(1)}, bf16[4,32,640]{2,1,0:T(8,128)(2,1)S(1)}, u32[]{:S(2)}, u32[]{:S(2)}) collective-permute-start(bf16[4,32,640]{2,1,0:T(8,128)(2,1)S(1)} %shard_map.130.refs_0_), channel_id=1, source_target_pairs={{0,2},{1,3},{2,0},{3,1},{4,6},{5,7},{6,4},{7,5},{8,10},{9,11},{10,... | collective-permute-start | bytes 491528 | tf_op jit(solution)/shard_map/ppermute | solution.py:743
  42.9 2.5 %shard_map.134 = (f32[128,640]{1,0:T(8,128)S(1)}, f32[128,256]{1,0:T(8,128)S(1)}, f32[128,128]{1,0:T(8,128)S(1)}, f32[128,128]{1,0:T(8,128)S(1)}, f32[128,640]{1...) custom-call(f32[128,640]{1,0:T(8,128)S(1)} %get-tuple-element.81.inner_pre_ref, ...), custom_call_target="tpu_custom_call" | custom-call | flops 300000000 | tf_op jit(solution)/shard_map/pallas_call | solution.py:728
  45.5 1.4 %collective-permute-start.5 = (bf16[4,32,640]{2,1,0:T(8,128)(2,1)S(1)}, bf16[4,32,640]{2,1,0:T(8,128)(2,1)S(1)}, u32[]{:S(2)}, u32[]{:S(2)}) collective-permute-start(bf16[4,32,640]{2,1,0:T(8,128)(2,1)S(1)} %shard_map.130.refs_0_), channel_id=1, source_target_pairs={{0,3},{1,0},{2,1},{3,2},{4,7},{5,4},{6,5},{7,6},{8,11},{9,8},{10,9... | collective-permute-start | bytes 491528 | tf_op jit(solution)/shard_map/ppermute | solution.py:743
  46.9 2.2 %shard_map.135 = (bf16[136,640]{1,0:T(8,128)(2,1)S(1)}, bf16[128,256]{1,0:T(8,128)(2,1)S(1)}, bf16[128,128]{1,0:T(8,128)(2,1)S(1)}, f32[8,896]{1,0:T(8,128)S(1)}...) custom-call(s32[3]{0:T(128)S(1)} %pad_add_fusion.place_ref, ...), custom_call_target="tpu_custom_call" | custom-call | flops 500000000 | tf_op jit(solution)/shard_map/pallas_call | solution.py:728
  49.1 1.4 %collective-permute-start.13 = (bf16[136,640]{1,0:T(8,128)(2,1)S(1)}, bf16[136,640]{1,0:T(8,128)(2,1)S(1)}, u32[]{:S(2)}, u32[]{:S(2)}) collective-permute-start(bf16[136,640]{1,0:T(8,128)(2,1)S(1)} %get-tuple-element.91.refs_1_.pair_ref), channel_id=1, source_target_pairs={{0,4},{4,8},{8,12},{12,0},{1,5},{5,9},{9,13},{13,1},{2,6},{6,10},{... | collective-permute-start | bytes 522248 | tf_op jit(solution)/shard_map/ppermute | solution.py:743
  50.5 1.6 %collective-permute-start.14 = (bf16[136,640]{1,0:T(8,128)(2,1)S(1)}, bf16[136,640]{1,0:T(8,128)(2,1)S(1)}, u32[]{:S(2)}, u32[]{:S(2)}) collective-permute-start(bf16[136,640]{1,0:T(8,128)(2,1)S(1)} %get-tuple-element.91.refs_1_.pair_ref), channel_id=1, source_target_pairs={{0,8},{4,12},{8,0},{12,4},{1,9},{5,13},{9,1},{13,5},{2,10},{6,14},... | collective-permute-start | bytes 522248 | tf_op jit(solution)/shard_map/ppermute | solution.py:743
  52.1 0.9 collective-permute-start.15
  53.0 0.9 shard_map.131
  53.9 4.4 %collective-permute-done.13.refs_2_ = bf16[136,640]{1,0:T(8,128)(2,1)S(1)} collective-permute-done((bf16[136,640]{1,0:T(8,128)(2,1)S(1)}, bf16[136,640]{1,0:T(8,128)(2,1)S(1)}, u32[]{:S(2)}, u32[]{:S(2)}) %collective-permute-start.13) | collective-permute-done | bytes 174112 | tf_op jit(solution)/shard_map/ppermute | solution.py:743
  58.3 5.6 %collective-permute-done.14.refs_3_ = bf16[136,640]{1,0:T(8,128)(2,1)S(1)} collective-permute-done((bf16[136,640]{1,0:T(8,128)(2,1)S(1)}, bf16[136,640]{1,0:T(8,128)(2,1)S(1)}, u32[]{:S(2)}, u32[]{:S(2)}) %collective-permute-start.14) | collective-permute-done | bytes 174112 | tf_op jit(solution)/shard_map/ppermute | solution.py:743
  63.9 1.0 shard_map.136
  65.0 1.6 %collective-permute-start.16 = (bf16[336,640]{1,0:T(8,128)(2,1)S(1)}, bf16[336,640]{1,0:T(8,128)(2,1)S(1)}, u32[]{:S(2)}, u32[]{:S(2)}) collective-permute-start(bf16[336,640]{1,0:T(8,128)(2,1)S(1)} %get-tuple-element.96), channel_id=1, source_target_pairs={{0,16},{16,0},{1,17},{17,1},{2,18},{18,2},{3,19},{19,3},{4,20},{20... | collective-permute-start | bytes 1290248 | tf_op jit(solution)/shard_map/ppermute | solution.py:976
  66.6 1.4 %collective-permute-start.22 = (bf16[40,256]{1,0:T(8,128)(2,1)S(1)}, bf16[40,256]{1,0:T(8,128)(2,1)S(1)}, u32[]{:S(2)}, u32[]{:S(2)}) collective-permute-start(bf16[40,256]{1,0:T(8,128)(2,1)S(1)} %get-tuple-element.112), channel_id=1, source_target_pairs={{0,2},{1,3},{2,0},{3,1},{4,6},{5,7},{6,4},{7,5},{8,10},{9,11},{10,... | collective-permute-start | bytes 61448 | tf_op jit(solution)/shard_map/ppermute | solution.py:940
  67.9 1.5 %collective-permute-start.23 = (bf16[40,256]{1,0:T(8,128)(2,1)S(1)}, bf16[40,256]{1,0:T(8,128)(2,1)S(1)}, u32[]{:S(2)}, u32[]{:S(2)}) collective-permute-start(bf16[40,256]{1,0:T(8,128)(2,1)S(1)} %get-tuple-element.113), channel_id=1, source_target_pairs={{0,3},{1,0},{2,1},{3,2},{4,7},{5,4},{6,5},{7,6},{8,11},{9,8},{10,9... | collective-permute-start | bytes 61448 | tf_op jit(solution)/shard_map/ppermute | solution.py:940
  69.4 0.4 collective-permute-done.21.refs_1_
  69.8 0.6 collective-permute-done.22.refs_2_
  70.3 0.5 collective-permute-done.23.refs_3_
  70.9 4.2 %collective-permute-start.24 = (bf16[40,256]{1,0:T(8,128)(2,1)S(1)}, bf16[40,256]{1,0:T(8,128)(2,1)S(1)}, u32[]{:S(2)}, u32[]{:S(2)}) collective-permute-start(bf16[40,256]{1,0:T(8,128)(2,1)S(1)} %shard_map.140.refs_1_), channel_id=1, source_target_pairs={{0,4},{4,8},{8,12},{12,0},{1,5},{5,9},{9,13},{13,1},{2,6},{6,10},{... | collective-permute-start | bytes 61448 | tf_op jit(solution)/shard_map/ppermute | solution.py:743
  75.3 2.3 %collective-permute-start.26 = (bf16[40,256]{1,0:T(8,128)(2,1)S(1)}, bf16[40,256]{1,0:T(8,128)(2,1)S(1)}, u32[]{:S(2)}, u32[]{:S(2)}) collective-permute-start(bf16[40,256]{1,0:T(8,128)(2,1)S(1)} %shard_map.140.refs_1_), channel_id=1, source_target_pairs={{0,12},{4,0},{8,4},{12,8},{1,13},{5,1},{9,5},{13,9},{2,14},{6,2},{... | collective-permute-start | bytes 61448 | tf_op jit(solution)/shard_map/ppermute | solution.py:743
  77.6 2.5 %collective-permute-done.25.refs_3_ = bf16[40,256]{1,0:T(8,128)(2,1)S(1)} collective-permute-done((bf16[40,256]{1,0:T(8,128)(2,1)S(1)}, bf16[40,256]{1,0:T(8,128)(2,1)S(1)}, u32[]{:S(2)}, u32[]{:S(2)}) %collective-permute-start.25) | collective-permute-done | bytes 20512 | tf_op jit(solution)/shard_map/ppermute | solution.py:743
  80.0 0.8 shard_map.141
  81.0 2.4 %shard_map.138 = (bf16[40,2560]{1,0:T(8,128)(2,1)S(1)}, bf16[40,2560]{1,0:T(8,128)(2,1)S(1)}, bf16[40,2560]{1,0:T(8,128)(2,1)S(1)}, bf16[40,2560]{1,0:T(8,128)(2,1)S(1)}) custom-call(s32[3]{0:T(128)S(1)} %pad_add_fusion.place_ref, bf16[136,640]{1,0:T(8,128)(2,1)S(1)} %get-tuple-element.91.refs_1_.pair_ref, f32[8,896]{1,0:T(8,128)S(1)} %get-tuple-element.97.early_ref, ...), custom_call_target="tpu_custom_call" | custom-call | flops 400000000 | tf_op jit(solution)/shard_map/pallas_call | solution.py:728
  83.4 1.0 collective-permute-start.17
  84.4 1.1 %collective-permute-start.18 = (bf16[40,2560]{1,0:T(8,128)(2,1)S(1)}, bf16[40,2560]{1,0:T(8,128)(2,1)S(1)}, u32[]{:S(2)}, u32[]{:S(2)}) collective-permute-start(bf16[40,2560]{1,0:T(8,128)(2,1)S(1)} %get-tuple-element.104), channel_id=1, source_target_pairs={{0,2},{1,3},{2,0},{3,1},{4,6},{5,7},{6,4},{7,5},{8,10},{9,11},{10,... | collective-permute-start | bytes 614408 | tf_op jit(solution)/shard_map/ppermute | solution.py:959
  85.6 0.4 collective-permute-start.19
  86.0 1.0 collective-permute-start.28
  87.0 10.0 %collective-permute-done.28.refs_2_ = bf16[160,256]{1,0:T(8,128)(2,1)S(1)} collective-permute-done((bf16[160,256]{1,0:T(8,128)(2,1)S(1)}, bf16[160,256]{1,0:T(8,128)(2,1)S(1)}, u32[]{:S(2)}, u32[]{:S(2)}) %collective-permute-start.28) | collective-permute-done | bytes 81952 | tf_op jit(solution)/shard_map/ppermute | solution.py:992
  96.9 2.1 %collective-permute-done.29.refs_3_ = bf16[160,256]{1,0:T(8,128)(2,1)S(1)} collective-permute-done((bf16[160,256]{1,0:T(8,128)(2,1)S(1)}, bf16[160,256]{1,0:T(8,128)(2,1)S(1)}, u32[]{:S(2)}, u32[]{:S(2)}) %collective-permute-start.29) | collective-permute-done | bytes 81952 | tf_op jit(solution)/shard_map/ppermute | solution.py:992
  99.1 0.6 collective-permute-start.30
  99.6 0.8 shard_map.139
  100.4 1.3 %collective-permute-start.20 = (bf16[8,2560]{1,0:T(8,128)(2,1)S(1)}, bf16[8,2560]{1,0:T(8,128)(2,1)S(1)}, u32[]{:S(2)}, u32[]{:S(2)}) collective-permute-start(bf16[8,2560]{1,0:T(8,128)(2,1)S(1)} %get-tuple-element.108), channel_id=1, source_target_pairs={{4,0},{8,4},{12,8},{5,1},{9,5},{13,9},{6,2},{10,6},{14,10},{7,3},{... | collective-permute-start | bytes 122888 | tf_op jit(solution)/shard_map/ppermute | solution.py:1015
  101.7 0.5 shard_map.137
  102.2 1.1 %collective-permute-done.30.mixer_arrived_ref = bf16[80,256]{1,0:T(8,128)(2,1)S(1)} collective-permute-done((bf16[80,256]{1,0:T(8,128)(2,1)S(1)}, bf16[80,256]{1,0:T(8,128)(2,1)S(1)}, u32[]{:S(2)}, u32[]{:S(2)}) %collective-permute-start.30) | collective-permute-done | bytes 40992 | tf_op jit(solution)/shard_map/ppermute | solution.py:1002
  103.3 3.4 %collective-permute-done.20.late_ref = bf16[8,2560]{1,0:T(8,128)(2,1)S(1)} collective-permute-done((bf16[8,2560]{1,0:T(8,128)(2,1)S(1)}, bf16[8,2560]{1,0:T(8,128)(2,1)S(1)}, u32[]{:S(2)}, u32[]{:S(2)}) %collective-permute-start.20) | collective-permute-done | bytes 40992 | tf_op jit(solution)/shard_map/ppermute | solution.py:1015
  106.7 2.1 %shard_map.143 = (f32[320,640]{1,0:T(8,128)}, f32[10,320]{1,0:T(8,128)}, bf16[32,2560]{1,0:T(8,128)(2,1)}, f32[80,256]{1,0:T(8,128)}) custom-call(s32[3]{0:T(128)S(1)} %pad_add_fusion.place_ref, f32[320,640]{1,0:T(8,128)S(1)} %get-tuple-element.94.kept_ref, f32[16,320]{1,0:T(8,128)S(1)} %get-tuple-element.95.step_ref, ...), custom_call_target="tpu_custom_call", output_to_operand_aliasing={{2}: (4, {})} | custom-call | flops 100000000 | tf_op jit(solution)/shard_map/pallas_call | solution.py:728
  (36 shorter events, 0.5 us)
Async XLA Ops:
  0.6 7.4 %collective-permute-start.7 = (bf16[32,2560]{1,0:T(8,128)(2,1)}, bf16[32,2560]{1,0:T(8,128)(2,1)S(1)}, u32[]{:S(2)}, u32[]{:S(2)}) collective-permute-start(bf16[32,2560]{1,0:T(8,128)(2,1)} %bitcast.14), channel_id=1, source_target_pairs={{0,2},{1,3},{2,0},{3,1},{4,6},{5,7},{6,4},{7,5},{8,10},{9,11},{10,... | collective-permute-start | bytes 491528 | tf_op jit(solution)/shard_map/ppermute | solution.py:754
  3.7 7.9 %collective-permute-start.6 = (bf16[32,2560]{1,0:T(8,128)(2,1)}, bf16[32,2560]{1,0:T(8,128)(2,1)S(1)}, u32[]{:S(2)}, u32[]{:S(2)}) collective-permute-start(bf16[32,2560]{1,0:T(8,128)(2,1)} %bitcast.15), channel_id=1, source_target_pairs={{0,1},{1,0},{2,3},{3,2},{4,5},{5,4},{6,7},{7,6},{8,9},{9,8},{10,11... | collective-permute-start | bytes 491528 | tf_op jit(solution)/shard_map/ppermute | solution.py:754
  8.1 3.5 %collective-permute-start.8 = (bf16[32,2560]{1,0:T(8,128)(2,1)S(1)}, bf16[32,2560]{1,0:T(8,128)(2,1)S(1)}, u32[]{:S(2)}, u32[]{:S(2)}) collective-permute-start(bf16[32,2560]{1,0:T(8,128)(2,1)S(1)} %collective-permute-done.7.refs_2_), channel_id=1, source_target_pairs={{0,1},{1,0},{2,3},{3,2},{4,5},{5,4},{6,7},{7,6},{8,9},{9,8},{10,11... | collective-permute-start | bytes 491528 | tf_op jit(solution)/shard_map/ppermute | solution.py:754
  11.5 6.9 %copy-start = (bf16[1,128,640]{2,1,0:T(8,128)(2,1)S(1)}, bf16[1,128,640]{2,1,0:T(8,128)(2,1)}, u32[]{:S(2)}) copy-start(bf16[1,128,640]{2,1,0:T(8,128)(2,1)} %param.19) | copy-start | bytes 491524
  11.5 6.9 %copy-start.1 = (f32[4,640]{1,0:T(4,128)S(1)}, f32[4,640]{1,0:T(4,128)}, u32[]{:S(2)}) copy-start(f32[4,640]{1,0:T(4,128)} %refs_10_.1) | copy-start | bytes 30724
  11.6 6.9 %copy-start.2 = (f32[4,256]{1,0:T(4,128)S(1)}, f32[4,256]{1,0:T(4,128)}, u32[]{:S(2)}) copy-start(f32[4,256]{1,0:T(4,128)} %refs_11_.1) | copy-start | bytes 12292
  13.1 5.4 %collective-permute-start.9 = (bf16[16,896]{1,0:T(8,128)(2,1)S(1)}, bf16[16,896]{1,0:T(8,128)(2,1)S(1)}, u32[]{:S(2)}, u32[]{:S(2)}) collective-permute-start(bf16[16,896]{1,0:T(8,128)(2,1)S(1)} %get-tuple-element.75), channel_id=1, source_target_pairs={{0,4},{4,8},{8,12},{1,5},{5,9},{9,13},{2,6},{6,10},{10,14},{3,7},{... | collective-permute-start | bytes 86024 | tf_op jit(solution)/shard_map/ppermute | solution.py:847
  16.8 9.9 %collective-permute-start = (bf16[32,640]{1,0:T(8,128)(2,1)S(1)}, bf16[32,640]{1,0:T(8,128)(2,1)S(1)}, u32[]{:S(2)}, u32[]{:S(2)}) collective-permute-start(bf16[32,640]{1,0:T(8,128)(2,1)S(1)} %get-tuple-element.65), channel_id=1, source_target_pairs={{0,4},{4,8},{8,12},{12,0},{1,5},{5,9},{9,13},{13,1},{2,6},{6,10},{... | collective-permute-start | bytes 122888 | tf_op jit(solution)/shard_map/ppermute | solution.py:830
  20.0 25.5 %collective-permute-start.10 = (bf16[136,640]{1,0:T(8,128)(2,1)S(1)}, bf16[136,640]{1,0:T(8,128)(2,1)S(1)}, u32[]{:S(2)}, u32[]{:S(2)}) collective-permute-start(bf16[136,640]{1,0:T(8,128)(2,1)S(1)} %get-tuple-element.78), channel_id=1, source_target_pairs={{0,4},{4,8},{8,12},{12,0},{1,5},{5,9},{9,13},{13,1},{2,6},{6,10},{... | collective-permute-start | bytes 522248 | tf_op jit(solution)/shard_map/ppermute | solution.py:868
  22.3 24.7 %collective-permute-start.11 = (bf16[136,640]{1,0:T(8,128)(2,1)S(1)}, bf16[136,640]{1,0:T(8,128)(2,1)S(1)}, u32[]{:S(2)}, u32[]{:S(2)}) collective-permute-start(bf16[136,640]{1,0:T(8,128)(2,1)S(1)} %get-tuple-element.79), channel_id=1, source_target_pairs={{0,8},{4,12},{8,0},{12,4},{1,9},{5,13},{9,1},{13,5},{2,10},{6,14},... | collective-permute-start | bytes 522248 | tf_op jit(solution)/shard_map/ppermute | solution.py:868
  25.2 21.8 %collective-permute-start.12 = (bf16[136,640]{1,0:T(8,128)(2,1)S(1)}, bf16[136,640]{1,0:T(8,128)(2,1)S(1)}, u32[]{:S(2)}, u32[]{:S(2)}) collective-permute-start(bf16[136,640]{1,0:T(8,128)(2,1)S(1)} %get-tuple-element.80), channel_id=1, source_target_pairs={{0,12},{4,0},{8,4},{12,8},{1,13},{5,1},{9,5},{13,9},{2,14},{6,2},{... | collective-permute-start | bytes 522248 | tf_op jit(solution)/shard_map/ppermute | solution.py:868
  26.2 15.1 %collective-permute-start.1 = (bf16[32,640]{1,0:T(8,128)(2,1)S(1)}, bf16[32,640]{1,0:T(8,128)(2,1)S(1)}, u32[]{:S(2)}, u32[]{:S(2)}) collective-permute-start(bf16[32,640]{1,0:T(8,128)(2,1)S(1)} %get-tuple-element.66), channel_id=1, source_target_pairs={{0,8},{4,12},{8,0},{12,4},{1,9},{5,13},{9,1},{13,5},{2,10},{6,14},... | collective-permute-start | bytes 122888 | tf_op jit(solution)/shard_map/ppermute | solution.py:830
  26.7 14.6 %collective-permute-start.2 = (bf16[32,640]{1,0:T(8,128)(2,1)S(1)}, bf16[32,640]{1,0:T(8,128)(2,1)S(1)}, u32[]{:S(2)}, u32[]{:S(2)}) collective-permute-start(bf16[32,640]{1,0:T(8,128)(2,1)S(1)} %get-tuple-element.67), channel_id=1, source_target_pairs={{0,12},{4,0},{8,4},{12,8},{1,13},{5,1},{9,5},{13,9},{2,14},{6,2},{... | collective-permute-start | bytes 122888 | tf_op jit(solution)/shard_map/ppermute | solution.py:830
  41.3 10.8 %collective-permute-start.3 = (bf16[4,32,640]{2,1,0:T(8,128)(2,1)S(1)}, bf16[4,32,640]{2,1,0:T(8,128)(2,1)S(1)}, u32[]{:S(2)}, u32[]{:S(2)}) collective-permute-start(bf16[4,32,640]{2,1,0:T(8,128)(2,1)S(1)} %shard_map.130.refs_0_), channel_id=1, source_target_pairs={{0,1},{1,2},{2,3},{3,0},{4,5},{5,6},{6,7},{7,4},{8,9},{9,10},{10,1... | collective-permute-start | bytes 491528 | tf_op jit(solution)/shard_map/ppermute | solution.py:743
  41.4 11.6 %collective-permute-start.4 = (bf16[4,32,640]{2,1,0:T(8,128)(2,1)S(1)}, bf16[4,32,640]{2,1,0:T(8,128)(2,1)S(1)}, u32[]{:S(2)}, u32[]{:S(2)}) collective-permute-start(bf16[4,32,640]{2,1,0:T(8,128)(2,1)S(1)} %shard_map.130.refs_0_), channel_id=1, source_target_pairs={{0,2},{1,3},{2,0},{3,1},{4,6},{5,7},{6,4},{7,5},{8,10},{9,11},{10,... | collective-permute-start | bytes 491528 | tf_op jit(solution)/shard_map/ppermute | solution.py:743
  45.5 7.5 %collective-permute-start.5 = (bf16[4,32,640]{2,1,0:T(8,128)(2,1)S(1)}, bf16[4,32,640]{2,1,0:T(8,128)(2,1)S(1)}, u32[]{:S(2)}, u32[]{:S(2)}) collective-permute-start(bf16[4,32,640]{2,1,0:T(8,128)(2,1)S(1)} %shard_map.130.refs_0_), channel_id=1, source_target_pairs={{0,3},{1,0},{2,1},{3,2},{4,7},{5,4},{6,5},{7,6},{8,11},{9,8},{10,9... | collective-permute-start | bytes 491528 | tf_op jit(solution)/shard_map/ppermute | solution.py:743
  49.1 9.2 %collective-permute-start.13 = (bf16[136,640]{1,0:T(8,128)(2,1)S(1)}, bf16[136,640]{1,0:T(8,128)(2,1)S(1)}, u32[]{:S(2)}, u32[]{:S(2)}) collective-permute-start(bf16[136,640]{1,0:T(8,128)(2,1)S(1)} %get-tuple-element.91.refs_1_.pair_ref), channel_id=1, source_target_pairs={{0,4},{4,8},{8,12},{12,0},{1,5},{5,9},{9,13},{13,1},{2,6},{6,10},{... | collective-permute-start | bytes 522248 | tf_op jit(solution)/shard_map/ppermute | solution.py:743
  50.5 13.5 %collective-permute-start.14 = (bf16[136,640]{1,0:T(8,128)(2,1)S(1)}, bf16[136,640]{1,0:T(8,128)(2,1)S(1)}, u32[]{:S(2)}, u32[]{:S(2)}) collective-permute-start(bf16[136,640]{1,0:T(8,128)(2,1)S(1)} %get-tuple-element.91.refs_1_.pair_ref), channel_id=1, source_target_pairs={{0,8},{4,12},{8,0},{12,4},{1,9},{5,13},{9,1},{13,5},{2,10},{6,14},... | collective-permute-start | bytes 522248 | tf_op jit(solution)/shard_map/ppermute | solution.py:743
  52.1 11.8 %collective-permute-start.15 = (bf16[136,640]{1,0:T(8,128)(2,1)S(1)}, bf16[136,640]{1,0:T(8,128)(2,1)S(1)}, u32[]{:S(2)}, u32[]{:S(2)}) collective-permute-start(bf16[136,640]{1,0:T(8,128)(2,1)S(1)} %get-tuple-element.91.refs_1_.pair_ref), channel_id=1, source_target_pairs={{0,12},{4,0},{8,4},{12,8},{1,13},{5,1},{9,5},{13,9},{2,14},{6,2},{... | collective-permute-start | bytes 522248 | tf_op jit(solution)/shard_map/ppermute | solution.py:743
  65.0 41.7 %collective-permute-start.16 = (bf16[336,640]{1,0:T(8,128)(2,1)S(1)}, bf16[336,640]{1,0:T(8,128)(2,1)S(1)}, u32[]{:S(2)}, u32[]{:S(2)}) collective-permute-start(bf16[336,640]{1,0:T(8,128)(2,1)S(1)} %get-tuple-element.96), channel_id=1, source_target_pairs={{0,16},{16,0},{1,17},{17,1},{2,18},{18,2},{3,19},{19,3},{4,20},{20... | collective-permute-start | bytes 1290248 | tf_op jit(solution)/shard_map/ppermute | solution.py:976
  66.6 3.2 %collective-permute-start.21 = (bf16[40,256]{1,0:T(8,128)(2,1)S(1)}, bf16[40,256]{1,0:T(8,128)(2,1)S(1)}, u32[]{:S(2)}, u32[]{:S(2)}) collective-permute-start(bf16[40,256]{1,0:T(8,128)(2,1)S(1)} %get-tuple-element.111), channel_id=1, source_target_pairs={{0,1},{1,2},{2,3},{3,0},{4,5},{5,6},{6,7},{7,4},{8,9},{9,10},{10,1... | collective-permute-start | bytes 61448 | tf_op jit(solution)/shard_map/ppermute | solution.py:940
  66.6 3.8 %collective-permute-start.22 = (bf16[40,256]{1,0:T(8,128)(2,1)S(1)}, bf16[40,256]{1,0:T(8,128)(2,1)S(1)}, u32[]{:S(2)}, u32[]{:S(2)}) collective-permute-start(bf16[40,256]{1,0:T(8,128)(2,1)S(1)} %get-tuple-element.112), channel_id=1, source_target_pairs={{0,2},{1,3},{2,0},{3,1},{4,6},{5,7},{6,4},{7,5},{8,10},{9,11},{10,... | collective-permute-start | bytes 61448 | tf_op jit(solution)/shard_map/ppermute | solution.py:940
  67.9 2.9 %collective-permute-start.23 = (bf16[40,256]{1,0:T(8,128)(2,1)S(1)}, bf16[40,256]{1,0:T(8,128)(2,1)S(1)}, u32[]{:S(2)}, u32[]{:S(2)}) collective-permute-start(bf16[40,256]{1,0:T(8,128)(2,1)S(1)} %get-tuple-element.113), channel_id=1, source_target_pairs={{0,3},{1,0},{2,1},{3,2},{4,7},{5,4},{6,5},{7,6},{8,11},{9,8},{10,9... | collective-permute-start | bytes 61448 | tf_op jit(solution)/shard_map/ppermute | solution.py:940
  70.9 6.7 %collective-permute-start.24 = (bf16[40,256]{1,0:T(8,128)(2,1)S(1)}, bf16[40,256]{1,0:T(8,128)(2,1)S(1)}, u32[]{:S(2)}, u32[]{:S(2)}) collective-permute-start(bf16[40,256]{1,0:T(8,128)(2,1)S(1)} %shard_map.140.refs_1_), channel_id=1, source_target_pairs={{0,4},{4,8},{8,12},{12,0},{1,5},{5,9},{9,13},{13,1},{2,6},{6,10},{... | collective-permute-start | bytes 61448 | tf_op jit(solution)/shard_map/ppermute | solution.py:743
  75.1 4.9 %collective-permute-start.25 = (bf16[40,256]{1,0:T(8,128)(2,1)S(1)}, bf16[40,256]{1,0:T(8,128)(2,1)S(1)}, u32[]{:S(2)}, u32[]{:S(2)}) collective-permute-start(bf16[40,256]{1,0:T(8,128)(2,1)S(1)} %shard_map.140.refs_1_), channel_id=1, source_target_pairs={{0,8},{4,12},{8,0},{12,4},{1,9},{5,13},{9,1},{13,5},{2,10},{6,14},... | collective-permute-start | bytes 61448 | tf_op jit(solution)/shard_map/ppermute | solution.py:743
  75.3 4.8 %collective-permute-start.26 = (bf16[40,256]{1,0:T(8,128)(2,1)S(1)}, bf16[40,256]{1,0:T(8,128)(2,1)S(1)}, u32[]{:S(2)}, u32[]{:S(2)}) collective-permute-start(bf16[40,256]{1,0:T(8,128)(2,1)S(1)} %shard_map.140.refs_1_), channel_id=1, source_target_pairs={{0,12},{4,0},{8,4},{12,8},{1,13},{5,1},{9,5},{13,9},{2,14},{6,2},{... | collective-permute-start | bytes 61448 | tf_op jit(solution)/shard_map/ppermute | solution.py:743
  80.9 5.1 %collective-permute-start.27 = (bf16[160,256]{1,0:T(8,128)(2,1)S(1)}, bf16[160,256]{1,0:T(8,128)(2,1)S(1)}, u32[]{:S(2)}, u32[]{:S(2)}) collective-permute-start(bf16[160,256]{1,0:T(8,128)(2,1)S(1)} %get-tuple-element.115), channel_id=1, source_target_pairs={{0,1},{1,2},{2,3},{3,0},{4,5},{5,6},{6,7},{7,4},{8,9},{9,10},{10,1... | collective-permute-start | bytes 245768 | tf_op jit(solution)/shard_map/ppermute | solution.py:992
  83.4 16.3 %collective-permute-start.17 = (bf16[40,2560]{1,0:T(8,128)(2,1)S(1)}, bf16[40,2560]{1,0:T(8,128)(2,1)S(1)}, u32[]{:S(2)}, u32[]{:S(2)}) collective-permute-start(bf16[40,2560]{1,0:T(8,128)(2,1)S(1)} %get-tuple-element.103), channel_id=1, source_target_pairs={{0,1},{1,2},{2,3},{3,0},{4,5},{5,6},{6,7},{7,4},{8,9},{9,10},{10,1... | collective-permute-start | bytes 614408 | tf_op jit(solution)/shard_map/ppermute | solution.py:959
  84.4 15.2 %collective-permute-start.18 = (bf16[40,2560]{1,0:T(8,128)(2,1)S(1)}, bf16[40,2560]{1,0:T(8,128)(2,1)S(1)}, u32[]{:S(2)}, u32[]{:S(2)}) collective-permute-start(bf16[40,2560]{1,0:T(8,128)(2,1)S(1)} %get-tuple-element.104), channel_id=1, source_target_pairs={{0,2},{1,3},{2,0},{3,1},{4,6},{5,7},{6,4},{7,5},{8,10},{9,11},{10,... | collective-permute-start | bytes 614408 | tf_op jit(solution)/shard_map/ppermute | solution.py:959
  85.6 14.1 %collective-permute-start.19 = (bf16[40,2560]{1,0:T(8,128)(2,1)S(1)}, bf16[40,2560]{1,0:T(8,128)(2,1)S(1)}, u32[]{:S(2)}, u32[]{:S(2)}) collective-permute-start(bf16[40,2560]{1,0:T(8,128)(2,1)S(1)} %get-tuple-element.105), channel_id=1, source_target_pairs={{0,3},{1,0},{2,1},{3,2},{4,7},{5,4},{6,5},{7,6},{8,11},{9,8},{10,9... | collective-permute-start | bytes 614408 | tf_op jit(solution)/shard_map/ppermute | solution.py:959
  86.0 11.0 %collective-permute-start.28 = (bf16[160,256]{1,0:T(8,128)(2,1)S(1)}, bf16[160,256]{1,0:T(8,128)(2,1)S(1)}, u32[]{:S(2)}, u32[]{:S(2)}) collective-permute-start(bf16[160,256]{1,0:T(8,128)(2,1)S(1)} %get-tuple-element.116), channel_id=1, source_target_pairs={{0,2},{1,3},{2,0},{3,1},{4,6},{5,7},{6,4},{7,5},{8,10},{9,11},{10,... | collective-permute-start | bytes 245768 | tf_op jit(solution)/shard_map/ppermute | solution.py:992
  96.9 2.1 %collective-permute-start.29 = (bf16[160,256]{1,0:T(8,128)(2,1)S(1)}, bf16[160,256]{1,0:T(8,128)(2,1)S(1)}, u32[]{:S(2)}, u32[]{:S(2)}) collective-permute-start(bf16[160,256]{1,0:T(8,128)(2,1)S(1)} %get-tuple-element.117), channel_id=1, source_target_pairs={{0,3},{1,0},{2,1},{3,2},{4,7},{5,4},{6,5},{7,6},{8,11},{9,8},{10,9... | collective-permute-start | bytes 245768 | tf_op jit(solution)/shard_map/ppermute | solution.py:992
  99.1 4.2 %collective-permute-start.30 = (bf16[80,256]{1,0:T(8,128)(2,1)S(1)}, bf16[80,256]{1,0:T(8,128)(2,1)S(1)}, u32[]{:S(2)}, u32[]{:S(2)}) collective-permute-start(bf16[80,256]{1,0:T(8,128)(2,1)S(1)} %get-tuple-element.119), channel_id=1, source_target_pairs={{0,16},{16,0},{1,17},{17,1},{2,18},{18,2},{3,19},{19,3},{4,20},{20... | collective-permute-start | bytes 122888 | tf_op jit(solution)/shard_map/ppermute | solution.py:1002
  100.4 6.3 %collective-permute-start.20 = (bf16[8,2560]{1,0:T(8,128)(2,1)S(1)}, bf16[8,2560]{1,0:T(8,128)(2,1)S(1)}, u32[]{:S(2)}, u32[]{:S(2)}) collective-permute-start(bf16[8,2560]{1,0:T(8,128)(2,1)S(1)} %get-tuple-element.108), channel_id=1, source_target_pairs={{4,0},{8,4},{12,8},{5,1},{9,5},{13,9},{6,2},{10,6},{14,10},{7,3},{... | collective-permute-start | bytes 122888 | tf_op jit(solution)/shard_map/ppermute | solution.py:1015

commit v5 on v4

--- a/solution.py
+++ b/solution.py
@@ -448,10 +448,13 @@
     inner_grad = inner_grad_ref[...] + tail_wide * from_end
     input_grad = mixer_grad_ref[:, :state] + half_fine(tail_wide * inner_act, end, 1, 1)
     output_grad = mixer_grad_ref[:, state:] + half_fine(lead_wide * upstream, start, 1, 1)
-    end_part = rest * collect(inner_act * from_end, heads)
-    start_part = lead * collect(upstream * from_start, heads)
     product = jnp.sum(end * start, axis=0, keepdims=True)
-    product = collect(jnp.broadcast_to(product, (PAD, width)), heads)[0:1]
+    product = jnp.broadcast_to(product, (2 * PAD, width))
+    gathered = jnp.concatenate([inner_act * from_end, upstream * from_start, product], axis=0)
+    gathered = collect(gathered, heads)
+    end_part = rest * gathered[:length]
+    start_part = lead * gathered[length : 2 * length]
+    product = gathered[2 * length : 2 * length + 1]
     step_grad = row_ref[...] + end_part
     sums = start_part - step * step_grad
     total = jnp.sum(step * end_part, axis=0, keepdims=True) + jnp.exp(last) * product

time: 109 us -> 109 us (level)
  no operation moved by 1% of the time
where the time goes in v5:
time: 109 us
  waiting for transfers between devices  46.8 us (43%)
  starting transfers between devices  41.5 us (38%)
  Pallas kernels  19.6 us (18%)
    pallas_call x15, Pallas kernels, call(): pl.pallas_call(body, out_shape=out_shape, in_specs=in_specs, out_specs=ou...  19.6 us
    ppermute x9, starting transfers between devices, around(): lax.ppermute(block, axis, ring(axis, hop))  13.6 us
    ppermute x9, waiting for transfers between devices, body(): lax.ppermute(block, 'chan', ring('chan', hop))  13.5 us
    ppermute x9, waiting for transfers between devices, around(): lax.ppermute(block, axis, ring(axis, hop))  12.5 us
    ppermute x3, waiting for transfers between devices, body(): columns.append(lax.ppermute(block, 'seq', ring('seq', hop)))  11.8 us
    ppermute x9, starting transfers between devices, body(): lax.ppermute(block, 'chan', ring('chan', hop))  6.5 us
    ppermute x3, starting transfers between devices, body(): lax.ppermute(message, 'seq', ring('seq', hop))  6.19 us
    ppermute x3, starting transfers between devices, body(): columns.append(lax.ppermute(block, 'seq', ring('seq', hop)))  4.97 us
  transfers between devices with their start and end apart: 31, of which 12 were waited for; matrix products, arithmetic and copies ran while one was open for 0% of the time, Pallas kernels for 14%

profile of v5, /device:TPU:0, one launch (start us, length us, event | category | flops | bytes accessed | tf_op | source)
XLA Modules:
  0.0 108.8 jit_solution(1339455539213924005)
XLA Ops:
  0.6 3.0 %collective-permute-start.7 = (bf16[32,2560]{1,0:T(8,128)(2,1)}, bf16[32,2560]{1,0:T(8,128)(2,1)S(1)}, u32[]{:S(2)}, u32[]{:S(2)}) collective-permute-start(bf16[32,2560]{1,0:T(8,128)(2,1)} %bitcast.14), channel_id=1, source_target_pairs={{0,2},{1,3},{2,0},{3,1},{4,6},{5,7},{6,4},{7,5},{8,10},{9,11},{10,... | collective-permute-start | bytes 491528 | tf_op jit(solution)/shard_map/ppermute | solution.py:757
  3.7 4.4 %collective-permute-done.7.refs_2_ = bf16[32,2560]{1,0:T(8,128)(2,1)S(1)} collective-permute-done((bf16[32,2560]{1,0:T(8,128)(2,1)}, bf16[32,2560]{1,0:T(8,128)(2,1)S(1)}, u32[]{:S(2)}, u32[]{:S(2)}) %collective-permute-start.7) | collective-permute-done | bytes 163872 | tf_op jit(solution)/shard_map/ppermute | solution.py:757
  8.2 3.4 %shard_map.129 = (bf16[32,2560]{1,0:T(8,128)(2,1)S(1)}, bf16[2560,128]{1,0:T(8,128)(2,1)S(1)}, f32[8,128]{1,0:T(8,128)S(1)}, bf16[2560,640]{1,0:T(8,128)(2,1)S(1...) custom-call(s32[3]{0:T(128)S(1)} %pad_add_fusion.place_ref, ...), custom_call_target="tpu_custom_call" | custom-call | flops 100000000 | tf_op jit(solution)/shard_map/pallas_call | solution.py:731
  11.6 1.5 %shard_map.132 = (bf16[128,640]{1,0:T(8,128)(2,1)S(1)}, bf16[128,256]{1,0:T(8,128)(2,1)S(1)}, f32[128,128]{1,0:T(8,128)S(1)}, bf16[16,896]{1,0:T(8,128)(2,1)S(1)}) custom-call(s32[3]{0:T(128)S(1)} %pad_add_fusion.place_ref, bf16[32,2560]{1,0:T(8,128)(2,1)S(1)} %get-tuple-element.69.refs_0_, bf16[32,2560]{1,0:T(8,128)(2,1)S(1)} %collective-permute-done.6.refs_1_, ...), custom_call_target="tpu_custom_call" | custom-call | flops 400000000 | tf_op jit(solution)/shard_map/pallas_call | solution.py:731
  13.1 3.7 %collective-permute-start.9 = (bf16[16,896]{1,0:T(8,128)(2,1)S(1)}, bf16[16,896]{1,0:T(8,128)(2,1)S(1)}, u32[]{:S(2)}, u32[]{:S(2)}) collective-permute-start(bf16[16,896]{1,0:T(8,128)(2,1)S(1)} %get-tuple-element.75), channel_id=1, source_target_pairs={{0,4},{4,8},{8,12},{1,5},{5,9},{9,13},{2,6},{6,10},{10,14},{3,7},{... | collective-permute-start | bytes 86024 | tf_op jit(solution)/shard_map/ppermute | solution.py:850
  16.8 1.6 %collective-permute-start = (bf16[32,640]{1,0:T(8,128)(2,1)S(1)}, bf16[32,640]{1,0:T(8,128)(2,1)S(1)}, u32[]{:S(2)}, u32[]{:S(2)}) collective-permute-start(bf16[32,640]{1,0:T(8,128)(2,1)S(1)} %get-tuple-element.65), channel_id=1, source_target_pairs={{0,4},{4,8},{8,12},{12,0},{1,5},{5,9},{9,13},{13,1},{2,6},{6,10},{... | collective-permute-start | bytes 122888 | tf_op jit(solution)/shard_map/ppermute | solution.py:833
  18.5 1.6 %shard_map.133 = (f32[128,640]{1,0:T(8,128)S(1)}, f32[128,256]{1,0:T(8,128)S(1)}, f32[128,128]{1,0:T(8,128)S(1)}, f32[128,128]{1,0:T(8,128)S(1)}, bf16[136,640]{...) custom-call(s32[3]{0:T(128)S(1)} %pad_add_fusion.place_ref, ...), custom_call_target="tpu_custom_call" | custom-call | flops 300000000 | tf_op jit(solution)/shard_map/pallas_call | solution.py:731
  20.0 2.3 %collective-permute-start.10 = (bf16[136,640]{1,0:T(8,128)(2,1)S(1)}, bf16[136,640]{1,0:T(8,128)(2,1)S(1)}, u32[]{:S(2)}, u32[]{:S(2)}) collective-permute-start(bf16[136,640]{1,0:T(8,128)(2,1)S(1)} %get-tuple-element.78), channel_id=1, source_target_pairs={{0,4},{4,8},{8,12},{12,0},{1,5},{5,9},{9,13},{13,1},{2,6},{6,10},{... | collective-permute-start | bytes 522248 | tf_op jit(solution)/shard_map/ppermute | solution.py:871
  22.3 2.9 %collective-permute-start.11 = (bf16[136,640]{1,0:T(8,128)(2,1)S(1)}, bf16[136,640]{1,0:T(8,128)(2,1)S(1)}, u32[]{:S(2)}, u32[]{:S(2)}) collective-permute-start(bf16[136,640]{1,0:T(8,128)(2,1)S(1)} %get-tuple-element.79), channel_id=1, source_target_pairs={{0,8},{4,12},{8,0},{12,4},{1,9},{5,13},{9,1},{13,5},{2,10},{6,14},... | collective-permute-start | bytes 522248 | tf_op jit(solution)/shard_map/ppermute | solution.py:871
  25.2 1.0 collective-permute-start.12
  26.2 0.5 collective-permute-start.1
  26.7 2.8 %collective-permute-start.2 = (bf16[32,640]{1,0:T(8,128)(2,1)S(1)}, bf16[32,640]{1,0:T(8,128)(2,1)S(1)}, u32[]{:S(2)}, u32[]{:S(2)}) collective-permute-start(bf16[32,640]{1,0:T(8,128)(2,1)S(1)} %get-tuple-element.67), channel_id=1, source_target_pairs={{0,12},{4,0},{8,4},{12,8},{1,13},{5,1},{9,5},{13,9},{2,14},{6,2},{... | collective-permute-start | bytes 122888 | tf_op jit(solution)/shard_map/ppermute | solution.py:833
  29.6 11.7 %collective-permute-done.1.refs_2_ = bf16[32,640]{1,0:T(8,128)(2,1)S(1)} collective-permute-done((bf16[32,640]{1,0:T(8,128)(2,1)S(1)}, bf16[32,640]{1,0:T(8,128)(2,1)S(1)}, u32[]{:S(2)}, u32[]{:S(2)}) %collective-permute-start.1) | collective-permute-done | bytes 40992 | tf_op jit(solution)/shard_map/ppermute | solution.py:833
  41.4 1.5 %collective-permute-start.4 = (bf16[4,32,640]{2,1,0:T(8,128)(2,1)S(1)}, bf16[4,32,640]{2,1,0:T(8,128)(2,1)S(1)}, u32[]{:S(2)}, u32[]{:S(2)}) collective-permute-start(bf16[4,32,640]{2,1,0:T(8,128)(2,1)S(1)} %shard_map.130.refs_0_), channel_id=1, source_target_pairs={{0,2},{1,3},{2,0},{3,1},{4,6},{5,7},{6,4},{7,5},{8,10},{9,11},{10,... | collective-permute-start | bytes 491528 | tf_op jit(solution)/shard_map/ppermute | solution.py:746
  42.9 2.5 %shard_map.134 = (f32[128,640]{1,0:T(8,128)S(1)}, f32[128,256]{1,0:T(8,128)S(1)}, f32[128,128]{1,0:T(8,128)S(1)}, f32[128,128]{1,0:T(8,128)S(1)}, f32[128,640]{1...) custom-call(f32[128,640]{1,0:T(8,128)S(1)} %get-tuple-element.81.inner_pre_ref, ...), custom_call_target="tpu_custom_call" | custom-call | flops 300000000 | tf_op jit(solution)/shard_map/pallas_call | solution.py:731
  45.5 1.4 %collective-permute-start.5 = (bf16[4,32,640]{2,1,0:T(8,128)(2,1)S(1)}, bf16[4,32,640]{2,1,0:T(8,128)(2,1)S(1)}, u32[]{:S(2)}, u32[]{:S(2)}) collective-permute-start(bf16[4,32,640]{2,1,0:T(8,128)(2,1)S(1)} %shard_map.130.refs_0_), channel_id=1, source_target_pairs={{0,3},{1,0},{2,1},{3,2},{4,7},{5,4},{6,5},{7,6},{8,11},{9,8},{10,9... | collective-permute-start | bytes 491528 | tf_op jit(solution)/shard_map/ppermute | solution.py:746
  46.9 2.1 %shard_map.135 = (bf16[136,640]{1,0:T(8,128)(2,1)S(1)}, bf16[128,256]{1,0:T(8,128)(2,1)S(1)}, bf16[128,128]{1,0:T(8,128)(2,1)S(1)}, f32[8,896]{1,0:T(8,128)S(1)}...) custom-call(s32[3]{0:T(128)S(1)} %pad_add_fusion.place_ref, ...), custom_call_target="tpu_custom_call" | custom-call | flops 500000000 | tf_op jit(solution)/shard_map/pallas_call | solution.py:731
  49.1 1.4 %collective-permute-start.13 = (bf16[136,640]{1,0:T(8,128)(2,1)S(1)}, bf16[136,640]{1,0:T(8,128)(2,1)S(1)}, u32[]{:S(2)}, u32[]{:S(2)}) collective-permute-start(bf16[136,640]{1,0:T(8,128)(2,1)S(1)} %get-tuple-element.91.refs_1_.pair_ref), channel_id=1, source_target_pairs={{0,4},{4,8},{8,12},{12,0},{1,5},{5,9},{9,13},{13,1},{2,6},{6,10},{... | collective-permute-start | bytes 522248 | tf_op jit(solution)/shard_map/ppermute | solution.py:746
  50.5 1.6 %collective-permute-start.14 = (bf16[136,640]{1,0:T(8,128)(2,1)S(1)}, bf16[136,640]{1,0:T(8,128)(2,1)S(1)}, u32[]{:S(2)}, u32[]{:S(2)}) collective-permute-start(bf16[136,640]{1,0:T(8,128)(2,1)S(1)} %get-tuple-element.91.refs_1_.pair_ref), channel_id=1, source_target_pairs={{0,8},{4,12},{8,0},{12,4},{1,9},{5,13},{9,1},{13,5},{2,10},{6,14},... | collective-permute-start | bytes 522248 | tf_op jit(solution)/shard_map/ppermute | solution.py:746
  52.1 0.9 collective-permute-start.15
  53.0 0.9 shard_map.131
  53.8 4.4 %collective-permute-done.13.refs_2_ = bf16[136,640]{1,0:T(8,128)(2,1)S(1)} collective-permute-done((bf16[136,640]{1,0:T(8,128)(2,1)S(1)}, bf16[136,640]{1,0:T(8,128)(2,1)S(1)}, u32[]{:S(2)}, u32[]{:S(2)}) %collective-permute-start.13) | collective-permute-done | bytes 174112 | tf_op jit(solution)/shard_map/ppermute | solution.py:746
  58.3 5.6 %collective-permute-done.14.refs_3_ = bf16[136,640]{1,0:T(8,128)(2,1)S(1)} collective-permute-done((bf16[136,640]{1,0:T(8,128)(2,1)S(1)}, bf16[136,640]{1,0:T(8,128)(2,1)S(1)}, u32[]{:S(2)}, u32[]{:S(2)}) %collective-permute-start.14) | collective-permute-done | bytes 174112 | tf_op jit(solution)/shard_map/ppermute | solution.py:746
  63.9 1.0 shard_map.136
  64.9 1.6 %collective-permute-start.16 = (bf16[336,640]{1,0:T(8,128)(2,1)S(1)}, bf16[336,640]{1,0:T(8,128)(2,1)S(1)}, u32[]{:S(2)}, u32[]{:S(2)}) collective-permute-start(bf16[336,640]{1,0:T(8,128)(2,1)S(1)} %get-tuple-element.96), channel_id=1, source_target_pairs={{0,16},{16,0},{1,17},{17,1},{2,18},{18,2},{3,19},{19,3},{4,20},{20... | collective-permute-start | bytes 1290248 | tf_op jit(solution)/shard_map/ppermute | solution.py:979
  66.5 1.4 %collective-permute-start.22 = (bf16[40,256]{1,0:T(8,128)(2,1)S(1)}, bf16[40,256]{1,0:T(8,128)(2,1)S(1)}, u32[]{:S(2)}, u32[]{:S(2)}) collective-permute-start(bf16[40,256]{1,0:T(8,128)(2,1)S(1)} %get-tuple-element.112), channel_id=1, source_target_pairs={{0,2},{1,3},{2,0},{3,1},{4,6},{5,7},{6,4},{7,5},{8,10},{9,11},{10,... | collective-permute-start | bytes 61448 | tf_op jit(solution)/shard_map/ppermute | solution.py:943
  67.9 1.5 %collective-permute-start.23 = (bf16[40,256]{1,0:T(8,128)(2,1)S(1)}, bf16[40,256]{1,0:T(8,128)(2,1)S(1)}, u32[]{:S(2)}, u32[]{:S(2)}) collective-permute-start(bf16[40,256]{1,0:T(8,128)(2,1)S(1)} %get-tuple-element.113), channel_id=1, source_target_pairs={{0,3},{1,0},{2,1},{3,2},{4,7},{5,4},{6,5},{7,6},{8,11},{9,8},{10,9... | collective-permute-start | bytes 61448 | tf_op jit(solution)/shard_map/ppermute | solution.py:943
  69.4 0.4 collective-permute-done.21.refs_1_
  69.7 0.6 collective-permute-done.22.refs_2_
  70.3 0.5 collective-permute-done.23.refs_3_
  70.9 4.2 %collective-permute-start.24 = (bf16[40,256]{1,0:T(8,128)(2,1)S(1)}, bf16[40,256]{1,0:T(8,128)(2,1)S(1)}, u32[]{:S(2)}, u32[]{:S(2)}) collective-permute-start(bf16[40,256]{1,0:T(8,128)(2,1)S(1)} %shard_map.140.refs_1_), channel_id=1, source_target_pairs={{0,4},{4,8},{8,12},{12,0},{1,5},{5,9},{9,13},{13,1},{2,6},{6,10},{... | collective-permute-start | bytes 61448 | tf_op jit(solution)/shard_map/ppermute | solution.py:746
  75.2 2.3 %collective-permute-start.26 = (bf16[40,256]{1,0:T(8,128)(2,1)S(1)}, bf16[40,256]{1,0:T(8,128)(2,1)S(1)}, u32[]{:S(2)}, u32[]{:S(2)}) collective-permute-start(bf16[40,256]{1,0:T(8,128)(2,1)S(1)} %shard_map.140.refs_1_), channel_id=1, source_target_pairs={{0,12},{4,0},{8,4},{12,8},{1,13},{5,1},{9,5},{13,9},{2,14},{6,2},{... | collective-permute-start | bytes 61448 | tf_op jit(solution)/shard_map/ppermute | solution.py:746
  77.5 2.5 %collective-permute-done.25.refs_3_ = bf16[40,256]{1,0:T(8,128)(2,1)S(1)} collective-permute-done((bf16[40,256]{1,0:T(8,128)(2,1)S(1)}, bf16[40,256]{1,0:T(8,128)(2,1)S(1)}, u32[]{:S(2)}, u32[]{:S(2)}) %collective-permute-start.25) | collective-permute-done | bytes 20512 | tf_op jit(solution)/shard_map/ppermute | solution.py:746
  80.0 0.8 shard_map.141
  80.9 2.4 %shard_map.138 = (bf16[40,2560]{1,0:T(8,128)(2,1)S(1)}, bf16[40,2560]{1,0:T(8,128)(2,1)S(1)}, bf16[40,2560]{1,0:T(8,128)(2,1)S(1)}, bf16[40,2560]{1,0:T(8,128)(2,1)S(1)}) custom-call(s32[3]{0:T(128)S(1)} %pad_add_fusion.place_ref, bf16[136,640]{1,0:T(8,128)(2,1)S(1)} %get-tuple-element.91.refs_1_.pair_ref, f32[8,896]{1,0:T(8,128)S(1)} %get-tuple-element.97.early_ref, ...), custom_call_target="tpu_custom_call" | custom-call | flops 400000000 | tf_op jit(solution)/shard_map/pallas_call | solution.py:731
  83.3 1.0 collective-permute-start.17
  84.4 1.1 %collective-permute-start.18 = (bf16[40,2560]{1,0:T(8,128)(2,1)S(1)}, bf16[40,2560]{1,0:T(8,128)(2,1)S(1)}, u32[]{:S(2)}, u32[]{:S(2)}) collective-permute-start(bf16[40,2560]{1,0:T(8,128)(2,1)S(1)} %get-tuple-element.104), channel_id=1, source_target_pairs={{0,2},{1,3},{2,0},{3,1},{4,6},{5,7},{6,4},{7,5},{8,10},{9,11},{10,... | collective-permute-start | bytes 614408 | tf_op jit(solution)/shard_map/ppermute | solution.py:962
  85.5 0.4 collective-permute-start.19
  85.9 1.0 collective-permute-start.28
  86.9 10.0 %collective-permute-done.28.refs_2_ = bf16[160,256]{1,0:T(8,128)(2,1)S(1)} collective-permute-done((bf16[160,256]{1,0:T(8,128)(2,1)S(1)}, bf16[160,256]{1,0:T(8,128)(2,1)S(1)}, u32[]{:S(2)}, u32[]{:S(2)}) %collective-permute-start.28) | collective-permute-done | bytes 81952 | tf_op jit(solution)/shard_map/ppermute | solution.py:995
  96.9 2.1 %collective-permute-done.29.refs_3_ = bf16[160,256]{1,0:T(8,128)(2,1)S(1)} collective-permute-done((bf16[160,256]{1,0:T(8,128)(2,1)S(1)}, bf16[160,256]{1,0:T(8,128)(2,1)S(1)}, u32[]{:S(2)}, u32[]{:S(2)}) %collective-permute-start.29) | collective-permute-done | bytes 81952 | tf_op jit(solution)/shard_map/ppermute | solution.py:995
  99.0 0.6 collective-permute-start.30
  99.6 0.8 shard_map.139
  100.4 1.3 %collective-permute-start.20 = (bf16[8,2560]{1,0:T(8,128)(2,1)S(1)}, bf16[8,2560]{1,0:T(8,128)(2,1)S(1)}, u32[]{:S(2)}, u32[]{:S(2)}) collective-permute-start(bf16[8,2560]{1,0:T(8,128)(2,1)S(1)} %get-tuple-element.108), channel_id=1, source_target_pairs={{4,0},{8,4},{12,8},{5,1},{9,5},{13,9},{6,2},{10,6},{14,10},{7,3},{... | collective-permute-start | bytes 122888 | tf_op jit(solution)/shard_map/ppermute | solution.py:1018
  101.6 0.5 shard_map.137
  102.1 1.1 %collective-permute-done.30.mixer_arrived_ref = bf16[80,256]{1,0:T(8,128)(2,1)S(1)} collective-permute-done((bf16[80,256]{1,0:T(8,128)(2,1)S(1)}, bf16[80,256]{1,0:T(8,128)(2,1)S(1)}, u32[]{:S(2)}, u32[]{:S(2)}) %collective-permute-start.30) | collective-permute-done | bytes 40992 | tf_op jit(solution)/shard_map/ppermute | solution.py:1005
  103.2 3.4 %collective-permute-done.20.late_ref = bf16[8,2560]{1,0:T(8,128)(2,1)S(1)} collective-permute-done((bf16[8,2560]{1,0:T(8,128)(2,1)S(1)}, bf16[8,2560]{1,0:T(8,128)(2,1)S(1)}, u32[]{:S(2)}, u32[]{:S(2)}) %collective-permute-start.20) | collective-permute-done | bytes 40992 | tf_op jit(solution)/shard_map/ppermute | solution.py:1018
  106.7 2.1 %shard_map.143 = (f32[320,640]{1,0:T(8,128)}, f32[10,320]{1,0:T(8,128)}, bf16[32,2560]{1,0:T(8,128)(2,1)}, f32[80,256]{1,0:T(8,128)}) custom-call(s32[3]{0:T(128)S(1)} %pad_add_fusion.place_ref, f32[320,640]{1,0:T(8,128)S(1)} %get-tuple-element.94.kept_ref, f32[16,320]{1,0:T(8,128)S(1)} %get-tuple-element.95.step_ref, ...), custom_call_target="tpu_custom_call", output_to_operand_aliasing={{2}: (4, {})} | custom-call | flops 100000000 | tf_op jit(solution)/shard_map/pallas_call | solution.py:731
  (36 shorter events, 0.5 us)
Async XLA Ops:
  0.6 7.4 %collective-permute-start.7 = (bf16[32,2560]{1,0:T(8,128)(2,1)}, bf16[32,2560]{1,0:T(8,128)(2,1)S(1)}, u32[]{:S(2)}, u32[]{:S(2)}) collective-permute-start(bf16[32,2560]{1,0:T(8,128)(2,1)} %bitcast.14), channel_id=1, source_target_pairs={{0,2},{1,3},{2,0},{3,1},{4,6},{5,7},{6,4},{7,5},{8,10},{9,11},{10,... | collective-permute-start | bytes 491528 | tf_op jit(solution)/shard_map/ppermute | solution.py:757
  3.7 7.9 %collective-permute-start.6 = (bf16[32,2560]{1,0:T(8,128)(2,1)}, bf16[32,2560]{1,0:T(8,128)(2,1)S(1)}, u32[]{:S(2)}, u32[]{:S(2)}) collective-permute-start(bf16[32,2560]{1,0:T(8,128)(2,1)} %bitcast.15), channel_id=1, source_target_pairs={{0,1},{1,0},{2,3},{3,2},{4,5},{5,4},{6,7},{7,6},{8,9},{9,8},{10,11... | collective-permute-start | bytes 491528 | tf_op jit(solution)/shard_map/ppermute | solution.py:757
  8.1 3.5 %collective-permute-start.8 = (bf16[32,2560]{1,0:T(8,128)(2,1)S(1)}, bf16[32,2560]{1,0:T(8,128)(2,1)S(1)}, u32[]{:S(2)}, u32[]{:S(2)}) collective-permute-start(bf16[32,2560]{1,0:T(8,128)(2,1)S(1)} %collective-permute-done.7.refs_2_), channel_id=1, source_target_pairs={{0,1},{1,0},{2,3},{3,2},{4,5},{5,4},{6,7},{7,6},{8,9},{9,8},{10,11... | collective-permute-start | bytes 491528 | tf_op jit(solution)/shard_map/ppermute | solution.py:757
  11.5 6.9 %copy-start = (bf16[1,128,640]{2,1,0:T(8,128)(2,1)S(1)}, bf16[1,128,640]{2,1,0:T(8,128)(2,1)}, u32[]{:S(2)}) copy-start(bf16[1,128,640]{2,1,0:T(8,128)(2,1)} %param.19) | copy-start | bytes 491524
  11.5 6.9 %copy-start.1 = (f32[4,640]{1,0:T(4,128)S(1)}, f32[4,640]{1,0:T(4,128)}, u32[]{:S(2)}) copy-start(f32[4,640]{1,0:T(4,128)} %refs_10_.1) | copy-start | bytes 30724
  11.6 6.9 %copy-start.2 = (f32[4,256]{1,0:T(4,128)S(1)}, f32[4,256]{1,0:T(4,128)}, u32[]{:S(2)}) copy-start(f32[4,256]{1,0:T(4,128)} %refs_11_.1) | copy-start | bytes 12292
  13.1 5.4 %collective-permute-start.9 = (bf16[16,896]{1,0:T(8,128)(2,1)S(1)}, bf16[16,896]{1,0:T(8,128)(2,1)S(1)}, u32[]{:S(2)}, u32[]{:S(2)}) collective-permute-start(bf16[16,896]{1,0:T(8,128)(2,1)S(1)} %get-tuple-element.75), channel_id=1, source_target_pairs={{0,4},{4,8},{8,12},{1,5},{5,9},{9,13},{2,6},{6,10},{10,14},{3,7},{... | collective-permute-start | bytes 86024 | tf_op jit(solution)/shard_map/ppermute | solution.py:850
  16.8 9.9 %collective-permute-start = (bf16[32,640]{1,0:T(8,128)(2,1)S(1)}, bf16[32,640]{1,0:T(8,128)(2,1)S(1)}, u32[]{:S(2)}, u32[]{:S(2)}) collective-permute-start(bf16[32,640]{1,0:T(8,128)(2,1)S(1)} %get-tuple-element.65), channel_id=1, source_target_pairs={{0,4},{4,8},{8,12},{12,0},{1,5},{5,9},{9,13},{13,1},{2,6},{6,10},{... | collective-permute-start | bytes 122888 | tf_op jit(solution)/shard_map/ppermute | solution.py:833
  20.0 25.5 %collective-permute-start.10 = (bf16[136,640]{1,0:T(8,128)(2,1)S(1)}, bf16[136,640]{1,0:T(8,128)(2,1)S(1)}, u32[]{:S(2)}, u32[]{:S(2)}) collective-permute-start(bf16[136,640]{1,0:T(8,128)(2,1)S(1)} %get-tuple-element.78), channel_id=1, source_target_pairs={{0,4},{4,8},{8,12},{12,0},{1,5},{5,9},{9,13},{13,1},{2,6},{6,10},{... | collective-permute-start | bytes 522248 | tf_op jit(solution)/shard_map/ppermute | solution.py:871
  22.3 24.7 %collective-permute-start.11 = (bf16[136,640]{1,0:T(8,128)(2,1)S(1)}, bf16[136,640]{1,0:T(8,128)(2,1)S(1)}, u32[]{:S(2)}, u32[]{:S(2)}) collective-permute-start(bf16[136,640]{1,0:T(8,128)(2,1)S(1)} %get-tuple-element.79), channel_id=1, source_target_pairs={{0,8},{4,12},{8,0},{12,4},{1,9},{5,13},{9,1},{13,5},{2,10},{6,14},... | collective-permute-start | bytes 522248 | tf_op jit(solution)/shard_map/ppermute | solution.py:871
  25.2 21.8 %collective-permute-start.12 = (bf16[136,640]{1,0:T(8,128)(2,1)S(1)}, bf16[136,640]{1,0:T(8,128)(2,1)S(1)}, u32[]{:S(2)}, u32[]{:S(2)}) collective-permute-start(bf16[136,640]{1,0:T(8,128)(2,1)S(1)} %get-tuple-element.80), channel_id=1, source_target_pairs={{0,12},{4,0},{8,4},{12,8},{1,13},{5,1},{9,5},{13,9},{2,14},{6,2},{... | collective-permute-start | bytes 522248 | tf_op jit(solution)/shard_map/ppermute | solution.py:871
  26.2 15.1 %collective-permute-start.1 = (bf16[32,640]{1,0:T(8,128)(2,1)S(1)}, bf16[32,640]{1,0:T(8,128)(2,1)S(1)}, u32[]{:S(2)}, u32[]{:S(2)}) collective-permute-start(bf16[32,640]{1,0:T(8,128)(2,1)S(1)} %get-tuple-element.66), channel_id=1, source_target_pairs={{0,8},{4,12},{8,0},{12,4},{1,9},{5,13},{9,1},{13,5},{2,10},{6,14},... | collective-permute-start | bytes 122888 | tf_op jit(solution)/shard_map/ppermute | solution.py:833
  26.7 14.6 %collective-permute-start.2 = (bf16[32,640]{1,0:T(8,128)(2,1)S(1)}, bf16[32,640]{1,0:T(8,128)(2,1)S(1)}, u32[]{:S(2)}, u32[]{:S(2)}) collective-permute-start(bf16[32,640]{1,0:T(8,128)(2,1)S(1)} %get-tuple-element.67), channel_id=1, source_target_pairs={{0,12},{4,0},{8,4},{12,8},{1,13},{5,1},{9,5},{13,9},{2,14},{6,2},{... | collective-permute-start | bytes 122888 | tf_op jit(solution)/shard_map/ppermute | solution.py:833
  41.3 10.8 %collective-permute-start.3 = (bf16[4,32,640]{2,1,0:T(8,128)(2,1)S(1)}, bf16[4,32,640]{2,1,0:T(8,128)(2,1)S(1)}, u32[]{:S(2)}, u32[]{:S(2)}) collective-permute-start(bf16[4,32,640]{2,1,0:T(8,128)(2,1)S(1)} %shard_map.130.refs_0_), channel_id=1, source_target_pairs={{0,1},{1,2},{2,3},{3,0},{4,5},{5,6},{6,7},{7,4},{8,9},{9,10},{10,1... | collective-permute-start | bytes 491528 | tf_op jit(solution)/shard_map/ppermute | solution.py:746
  41.4 11.6 %collective-permute-start.4 = (bf16[4,32,640]{2,1,0:T(8,128)(2,1)S(1)}, bf16[4,32,640]{2,1,0:T(8,128)(2,1)S(1)}, u32[]{:S(2)}, u32[]{:S(2)}) collective-permute-start(bf16[4,32,640]{2,1,0:T(8,128)(2,1)S(1)} %shard_map.130.refs_0_), channel_id=1, source_target_pairs={{0,2},{1,3},{2,0},{3,1},{4,6},{5,7},{6,4},{7,5},{8,10},{9,11},{10,... | collective-permute-start | bytes 491528 | tf_op jit(solution)/shard_map/ppermute | solution.py:746
  45.5 7.5 %collective-permute-start.5 = (bf16[4,32,640]{2,1,0:T(8,128)(2,1)S(1)}, bf16[4,32,640]{2,1,0:T(8,128)(2,1)S(1)}, u32[]{:S(2)}, u32[]{:S(2)}) collective-permute-start(bf16[4,32,640]{2,1,0:T(8,128)(2,1)S(1)} %shard_map.130.refs_0_), channel_id=1, source_target_pairs={{0,3},{1,0},{2,1},{3,2},{4,7},{5,4},{6,5},{7,6},{8,11},{9,8},{10,9... | collective-permute-start | bytes 491528 | tf_op jit(solution)/shard_map/ppermute | solution.py:746
  49.1 9.2 %collective-permute-start.13 = (bf16[136,640]{1,0:T(8,128)(2,1)S(1)}, bf16[136,640]{1,0:T(8,128)(2,1)S(1)}, u32[]{:S(2)}, u32[]{:S(2)}) collective-permute-start(bf16[136,640]{1,0:T(8,128)(2,1)S(1)} %get-tuple-element.91.refs_1_.pair_ref), channel_id=1, source_target_pairs={{0,4},{4,8},{8,12},{12,0},{1,5},{5,9},{9,13},{13,1},{2,6},{6,10},{... | collective-permute-start | bytes 522248 | tf_op jit(solution)/shard_map/ppermute | solution.py:746
  50.5 13.5 %collective-permute-start.14 = (bf16[136,640]{1,0:T(8,128)(2,1)S(1)}, bf16[136,640]{1,0:T(8,128)(2,1)S(1)}, u32[]{:S(2)}, u32[]{:S(2)}) collective-permute-start(bf16[136,640]{1,0:T(8,128)(2,1)S(1)} %get-tuple-element.91.refs_1_.pair_ref), channel_id=1, source_target_pairs={{0,8},{4,12},{8,0},{12,4},{1,9},{5,13},{9,1},{13,5},{2,10},{6,14},... | collective-permute-start | bytes 522248 | tf_op jit(solution)/shard_map/ppermute | solution.py:746
  52.1 11.8 %collective-permute-start.15 = (bf16[136,640]{1,0:T(8,128)(2,1)S(1)}, bf16[136,640]{1,0:T(8,128)(2,1)S(1)}, u32[]{:S(2)}, u32[]{:S(2)}) collective-permute-start(bf16[136,640]{1,0:T(8,128)(2,1)S(1)} %get-tuple-element.91.refs_1_.pair_ref), channel_id=1, source_target_pairs={{0,12},{4,0},{8,4},{12,8},{1,13},{5,1},{9,5},{13,9},{2,14},{6,2},{... | collective-permute-start | bytes 522248 | tf_op jit(solution)/shard_map/ppermute | solution.py:746
  64.9 41.7 %collective-permute-start.16 = (bf16[336,640]{1,0:T(8,128)(2,1)S(1)}, bf16[336,640]{1,0:T(8,128)(2,1)S(1)}, u32[]{:S(2)}, u32[]{:S(2)}) collective-permute-start(bf16[336,640]{1,0:T(8,128)(2,1)S(1)} %get-tuple-element.96), channel_id=1, source_target_pairs={{0,16},{16,0},{1,17},{17,1},{2,18},{18,2},{3,19},{19,3},{4,20},{20... | collective-permute-start | bytes 1290248 | tf_op jit(solution)/shard_map/ppermute | solution.py:979
  66.5 3.2 %collective-permute-start.21 = (bf16[40,256]{1,0:T(8,128)(2,1)S(1)}, bf16[40,256]{1,0:T(8,128)(2,1)S(1)}, u32[]{:S(2)}, u32[]{:S(2)}) collective-permute-start(bf16[40,256]{1,0:T(8,128)(2,1)S(1)} %get-tuple-element.111), channel_id=1, source_target_pairs={{0,1},{1,2},{2,3},{3,0},{4,5},{5,6},{6,7},{7,4},{8,9},{9,10},{10,1... | collective-permute-start | bytes 61448 | tf_op jit(solution)/shard_map/ppermute | solution.py:943
  66.5 3.8 %collective-permute-start.22 = (bf16[40,256]{1,0:T(8,128)(2,1)S(1)}, bf16[40,256]{1,0:T(8,128)(2,1)S(1)}, u32[]{:S(2)}, u32[]{:S(2)}) collective-permute-start(bf16[40,256]{1,0:T(8,128)(2,1)S(1)} %get-tuple-element.112), channel_id=1, source_target_pairs={{0,2},{1,3},{2,0},{3,1},{4,6},{5,7},{6,4},{7,5},{8,10},{9,11},{10,... | collective-permute-start | bytes 61448 | tf_op jit(solution)/shard_map/ppermute | solution.py:943
  67.9 2.9 %collective-permute-start.23 = (bf16[40,256]{1,0:T(8,128)(2,1)S(1)}, bf16[40,256]{1,0:T(8,128)(2,1)S(1)}, u32[]{:S(2)}, u32[]{:S(2)}) collective-permute-start(bf16[40,256]{1,0:T(8,128)(2,1)S(1)} %get-tuple-element.113), channel_id=1, source_target_pairs={{0,3},{1,0},{2,1},{3,2},{4,7},{5,4},{6,5},{7,6},{8,11},{9,8},{10,9... | collective-permute-start | bytes 61448 | tf_op jit(solution)/shard_map/ppermute | solution.py:943
  70.9 6.7 %collective-permute-start.24 = (bf16[40,256]{1,0:T(8,128)(2,1)S(1)}, bf16[40,256]{1,0:T(8,128)(2,1)S(1)}, u32[]{:S(2)}, u32[]{:S(2)}) collective-permute-start(bf16[40,256]{1,0:T(8,128)(2,1)S(1)} %shard_map.140.refs_1_), channel_id=1, source_target_pairs={{0,4},{4,8},{8,12},{12,0},{1,5},{5,9},{9,13},{13,1},{2,6},{6,10},{... | collective-permute-start | bytes 61448 | tf_op jit(solution)/shard_map/ppermute | solution.py:746
  75.1 4.9 %collective-permute-start.25 = (bf16[40,256]{1,0:T(8,128)(2,1)S(1)}, bf16[40,256]{1,0:T(8,128)(2,1)S(1)}, u32[]{:S(2)}, u32[]{:S(2)}) collective-permute-start(bf16[40,256]{1,0:T(8,128)(2,1)S(1)} %shard_map.140.refs_1_), channel_id=1, source_target_pairs={{0,8},{4,12},{8,0},{12,4},{1,9},{5,13},{9,1},{13,5},{2,10},{6,14},... | collective-permute-start | bytes 61448 | tf_op jit(solution)/shard_map/ppermute | solution.py:746
  75.2 4.8 %collective-permute-start.26 = (bf16[40,256]{1,0:T(8,128)(2,1)S(1)}, bf16[40,256]{1,0:T(8,128)(2,1)S(1)}, u32[]{:S(2)}, u32[]{:S(2)}) collective-permute-start(bf16[40,256]{1,0:T(8,128)(2,1)S(1)} %shard_map.140.refs_1_), channel_id=1, source_target_pairs={{0,12},{4,0},{8,4},{12,8},{1,13},{5,1},{9,5},{13,9},{2,14},{6,2},{... | collective-permute-start | bytes 61448 | tf_op jit(solution)/shard_map/ppermute | solution.py:746
  80.9 5.1 %collective-permute-start.27 = (bf16[160,256]{1,0:T(8,128)(2,1)S(1)}, bf16[160,256]{1,0:T(8,128)(2,1)S(1)}, u32[]{:S(2)}, u32[]{:S(2)}) collective-permute-start(bf16[160,256]{1,0:T(8,128)(2,1)S(1)} %get-tuple-element.115), channel_id=1, source_target_pairs={{0,1},{1,2},{2,3},{3,0},{4,5},{5,6},{6,7},{7,4},{8,9},{9,10},{10,1... | collective-permute-start | bytes 245768 | tf_op jit(solution)/shard_map/ppermute | solution.py:995
  83.3 16.3 %collective-permute-start.17 = (bf16[40,2560]{1,0:T(8,128)(2,1)S(1)}, bf16[40,2560]{1,0:T(8,128)(2,1)S(1)}, u32[]{:S(2)}, u32[]{:S(2)}) collective-permute-start(bf16[40,2560]{1,0:T(8,128)(2,1)S(1)} %get-tuple-element.103), channel_id=1, source_target_pairs={{0,1},{1,2},{2,3},{3,0},{4,5},{5,6},{6,7},{7,4},{8,9},{9,10},{10,1... | collective-permute-start | bytes 614408 | tf_op jit(solution)/shard_map/ppermute | solution.py:962
  84.4 15.2 %collective-permute-start.18 = (bf16[40,2560]{1,0:T(8,128)(2,1)S(1)}, bf16[40,2560]{1,0:T(8,128)(2,1)S(1)}, u32[]{:S(2)}, u32[]{:S(2)}) collective-permute-start(bf16[40,2560]{1,0:T(8,128)(2,1)S(1)} %get-tuple-element.104), channel_id=1, source_target_pairs={{0,2},{1,3},{2,0},{3,1},{4,6},{5,7},{6,4},{7,5},{8,10},{9,11},{10,... | collective-permute-start | bytes 614408 | tf_op jit(solution)/shard_map/ppermute | solution.py:962
  85.5 14.1 %collective-permute-start.19 = (bf16[40,2560]{1,0:T(8,128)(2,1)S(1)}, bf16[40,2560]{1,0:T(8,128)(2,1)S(1)}, u32[]{:S(2)}, u32[]{:S(2)}) collective-permute-start(bf16[40,2560]{1,0:T(8,128)(2,1)S(1)} %get-tuple-element.105), channel_id=1, source_target_pairs={{0,3},{1,0},{2,1},{3,2},{4,7},{5,4},{6,5},{7,6},{8,11},{9,8},{10,9... | collective-permute-start | bytes 614408 | tf_op jit(solution)/shard_map/ppermute | solution.py:962
  85.9 11.0 %collective-permute-start.28 = (bf16[160,256]{1,0:T(8,128)(2,1)S(1)}, bf16[160,256]{1,0:T(8,128)(2,1)S(1)}, u32[]{:S(2)}, u32[]{:S(2)}) collective-permute-start(bf16[160,256]{1,0:T(8,128)(2,1)S(1)} %get-tuple-element.116), channel_id=1, source_target_pairs={{0,2},{1,3},{2,0},{3,1},{4,6},{5,7},{6,4},{7,5},{8,10},{9,11},{10,... | collective-permute-start | bytes 245768 | tf_op jit(solution)/shard_map/ppermute | solution.py:995
  96.9 2.1 %collective-permute-start.29 = (bf16[160,256]{1,0:T(8,128)(2,1)S(1)}, bf16[160,256]{1,0:T(8,128)(2,1)S(1)}, u32[]{:S(2)}, u32[]{:S(2)}) collective-permute-start(bf16[160,256]{1,0:T(8,128)(2,1)S(1)} %get-tuple-element.117), channel_id=1, source_target_pairs={{0,3},{1,0},{2,1},{3,2},{4,7},{5,4},{6,5},{7,6},{8,11},{9,8},{10,9... | collective-permute-start | bytes 245768 | tf_op jit(solution)/shard_map/ppermute | solution.py:995
  99.0 4.2 %collective-permute-start.30 = (bf16[80,256]{1,0:T(8,128)(2,1)S(1)}, bf16[80,256]{1,0:T(8,128)(2,1)S(1)}, u32[]{:S(2)}, u32[]{:S(2)}) collective-permute-start(bf16[80,256]{1,0:T(8,128)(2,1)S(1)} %get-tuple-element.119), channel_id=1, source_target_pairs={{0,16},{16,0},{1,17},{17,1},{2,18},{18,2},{3,19},{19,3},{4,20},{20... | collective-permute-start | bytes 122888 | tf_op jit(solution)/shard_map/ppermute | solution.py:1005
  100.4 6.3 %collective-permute-start.20 = (bf16[8,2560]{1,0:T(8,128)(2,1)S(1)}, bf16[8,2560]{1,0:T(8,128)(2,1)S(1)}, u32[]{:S(2)}, u32[]{:S(2)}) collective-permute-start(bf16[8,2560]{1,0:T(8,128)(2,1)S(1)} %get-tuple-element.108), channel_id=1, source_target_pairs={{4,0},{8,4},{12,8},{5,1},{9,5},{13,9},{6,2},{10,6},{14,10},{7,3},{... | collective-permute-start | bytes 122888 | tf_op jit(solution)/shard_map/ppermute | solution.py:1018
